TPU v7x, 32 devices: a whole 2x2x4 slice. The times are simulated.
32 devices in a mesh: hel: 8 (over z, x), rad: 4 (over y, core).
Axes of the slice: x: 2, y: 2, z: 4, core: 2. Of those that a mesh axis runs over, the one named last changes fastest.
Arguments:
- psi_start: float32 [8, 64, 16, 768], P('hel', 'rad'), may hold values from -6 to 6
- potential: float32 [64, 16, 1536], P('rad'), may hold values from -0.5 to 0.5
- basis: bfloat16 [768, 1536], replicated, may hold values from -0.21875 to 0.21875
- kinetic: bfloat16 [64, 64], replicated, may hold values from -0.75 to 0.75
- radial_factor: float32 [64], P('rad'), may hold values from 0.002 to 0.02
- damping: float32 [64], P('rad'), may hold values from 0.7 to 1
- coupling: bfloat16 [8, 768], P('hel'), may hold values from -2 to 2
- helicity: int32 [8], P('hel'), may hold values from 0 to 7
- chan_rad: int32 [1024], replicated, may hold values from 0 to 63
- chan_vib: int32 [1024], replicated, may hold values from 0 to 15
- projector: bfloat16 [1024, 768], replicated, may hold values from -0.21875 to 0.21875
Outputs:
- psi_final: float32 [8, 64, 16, 768], P('hel', 'rad')
- amplitude: float32 [8, 1024], P('hel', 'rad')
All inputs are finite; a program needn't handle non-finite values.
Results may differ from a plain program's by a relative error of at most 0.0046.
Values may be sent and summed in bfloat16 or wider, within the bound.
No kernel may reach another device: no remote copies, remote signals or barrier semaphores. Data moves between devices by JAX's collectives and lax.ppermute only.
A program may use at most 64 MiB of HBM per device.

v0:
```python
import jax
import jax.numpy as jnp
from jax import lax
from jax.sharding import PartitionSpec as P

ITERS = 3


def from_behind(block, axis, distance):
    devices = range(lax.axis_size(axis))
    route = [(i - distance, i) for i in devices if i - distance in devices]
    return lax.ppermute(block, axis, route)


def per_device(
    psi_start,
    potential,
    basis,
    kinetic,
    radial_factor,
    damping,
    coupling,
    helicity,
    chan_rad,
    chan_vib,
    projector,
):
    hdev, rdev, nvib, nang = psi_start.shape
    nquad = basis.shape[1]
    rad_index = lax.axis_index("rad")
    hel_index = lax.axis_index("hel")
    total_blocks = lax.axis_size("hel") * hdev
    block_ids = hel_index * hdev + jnp.arange(hdev, dtype=jnp.int32)
    coupling_eff = jnp.where(
        (block_ids < total_blocks - 1)[:, None], coupling, jnp.zeros_like(coupling)
    )
    kvalue = helicity.astype(jnp.float32)
    kin_rows = lax.dynamic_slice_in_dim(kinetic, rad_index * rdev, rdev, 0)
    pot_rows = potential.reshape(1, -1, nquad)
    damp = damping[None, :, None, None]

    def ham(psi):
        packed = psi.astype(jnp.bfloat16)
        lower_pb, lower_cp = from_behind((packed, coupling_eff), "hel", 1)
        upper_pb = from_behind(packed, "hel", -1)
        kin = jnp.einsum(
            "rs,ksvj->krvj",
            kin_rows,
            lax.all_gather(packed, "rad", axis=1, tiled=True),
            preferred_element_type=jnp.float32,
        )
        grid = jnp.dot(packed.reshape(-1, nang), basis, preferred_element_type=jnp.float32)
        scaled = (grid.reshape(hdev, -1, nquad) * pot_rows).astype(jnp.bfloat16)
        ang = lax.dot_general(
            scaled.reshape(-1, nquad),
            basis,
            (((1,), (1,)), ((), ())),
            preferred_element_type=jnp.float32,
        )
        ang = ang.reshape(psi.shape)
        upper = jnp.concatenate([packed[1:], upper_pb], axis=0).astype(jnp.float32)
        lower = jnp.concatenate([lower_pb, packed[:-1]], axis=0).astype(jnp.float32)
        coupling_prev = jnp.concatenate([lower_cp, coupling_eff[:-1]], axis=0).astype(jnp.float32)
        cor = (
            coupling_eff.astype(jnp.float32)[:, None, None, :] * upper
            + coupling_prev[:, None, None, :] * lower
        )
        cen = (
            -2.0 * (kvalue * kvalue)[:, None, None, None] * radial_factor[None, :, None, None] * psi
        )
        return kin + ang + cen + cor

    previous = psi_start
    current = damp * ham(psi_start)
    for step in range(ITERS - 1):
        following = damp * (2.0 * ham(current) - damp * previous)
        previous, current = (current, following)
    final_b = current.astype(jnp.bfloat16)
    local_rad = chan_rad - rad_index * rdev
    inside = (local_rad >= 0) & (local_rad < rdev)
    slot = jnp.where(inside, local_rad * nvib + chan_vib, -1)
    select = (slot[:, None] == jnp.arange(rdev * nvib, dtype=jnp.int32)[None, :]).astype(
        jnp.bfloat16
    )
    rows = jnp.einsum(
        "cq,kqj->kcj",
        select,
        final_b.reshape(hdev, rdev * nvib, nang),
        preferred_element_type=jnp.float32,
    )
    partial_amp = jnp.sum(rows * projector.astype(jnp.float32)[None], axis=-1)
    summed = lax.psum(partial_amp, "rad")
    share = summed.shape[1] // lax.axis_size("rad")
    amplitude = lax.dynamic_slice_in_dim(summed, rad_index * share, share, 1)
    return (current, amplitude)


def solution(mesh):
    placed = (
        P("hel", "rad", None, None),
        P("rad", None, None),
        P(),
        P(),
        P("rad"),
        P("rad"),
        P("hel", None),
        P("hel"),
        P(),
        P(),
        P(),
    )
    return jax.shard_map(
        per_device,
        mesh=mesh,
        in_specs=placed,
        out_specs=(P("hel", "rad", None, None), P("hel", "rad")),
        check_vma=False,
    )
```

profile of v0, /device:TPU:24, one launch (start us, length us, event | category | flops | bytes accessed | tf_op | source)
XLA Modules:
  0.0 106.6 jit_solution(11813456667591361320)
XLA Ops:
  7.2 2.4 %copy.48 = bf16[1,16,16,768]{3,1,2,0:T(8,128)(2,1)} copy(f32[1,16,16,768]{3,2,1,0:T(8,128)} %param.11) | data formatting | bytes 1179648 | tf_op args[0]
  9.8 3.4 %collective-permute-start.2 = (bf16[1,16,16,768]{3,1,2,0:T(8,128)(2,1)}, bf16[1,16,16,768]{3,1,2,0:T(8,128)(2,1)S(1)}, u32[]{:S(2)}, u32[]{:S(2)}) collective-permute-start(bf16[1,16,16,768]{3,1,2,0:T(8,128)(2,1)} %copy.48), channel_id=1, source_target_pairs={{0,4},{4,8},{8,12},{12,16},{16,20},{20,24},{24,28},{1,5},{5,9},{9,... | collective-permute-start | bytes 1179656 | tf_op jit(solution)/shard_map/ppermute | solution.py:12
  13.2 3.3 %collective-permute-start = (bf16[1,16,16,768]{3,1,2,0:T(8,128)(2,1)}, bf16[1,16,16,768]{3,1,2,0:T(8,128)(2,1)}, u32[]{:S(2)}, u32[]{:S(2)}) collective-permute-start(bf16[1,16,16,768]{3,1,2,0:T(8,128)(2,1)} %copy.48), channel_id=1, source_target_pairs={{4,0},{8,4},{12,8},{16,12},{20,16},{24,20},{28,24},{5,1},{9,5},{13... | collective-permute-start | bytes 1179656 | tf_op jit(solution)/shard_map/ppermute | solution.py:12
  16.5 0.6 convert_reduce_fusion.1
  17.1 3.2 %collective-permute-start.1 = (bf16[1,768]{1,0:T(2,128)(2,1)}, bf16[1,768]{1,0:T(2,128)(2,1)}, u32[]{:S(2)}, u32[]{:S(2)}) collective-permute-start(bf16[1,768]{1,0:T(2,128)(2,1)} %get-tuple-element.7), channel_id=1, source_target_pairs={{0,4},{4,8},{8,12},{12,16},{16,20},{20,24},{24,28},{1,5},{5,9},{9,... | collective-permute-start | bytes 4616 | tf_op jit(solution)/shard_map/ppermute | solution.py:12
  20.4 1.1 %copy.22 = bf16[1,16,16,768]{3,2,1,0:T(8,128)(2,1)S(1)} copy(bf16[1,16,16,768]{3,1,2,0:T(8,128)(2,1)} %copy.48) | data formatting | bytes 786432 | tf_op jit(solution)/shard_map/convert_element_type | solution.py:43
  21.5 2.2 %fusion.1 = bf16[256,1536]{1,0:T(8,128)(2,1)S(1)} fusion(f32[256,1536]{1,0:T(8,128)} %bitcast.127, bf16[256,768]{1,0:T(8,128)(2,1)S(1)} %bitcast.130, bf16[768,1536]{1,0:T(8,128)(2,1)S(1)} %copy-done), kind=kOutput, calls=%fused_computation.5 | convolution fusion | flops 604766208 | bytes 5111808 | tf_op jit(solution)/shard_map/dot_general | solution.py:52
  23.7 2.0 %fusion.25 = f32[1,16,16,768]{3,1,2,0:T(8,128)} fusion(bf16[768,1536]{1,0:T(8,128)(2,1)S(1)} %copy-done, bf16[16,16,1536]{2,1,0:T(8,128)(2,1)S(1)} %bitcast.133), kind=kOutput, calls=%fused_computation.23 | convolution fusion | flops 603979776 | bytes 3932160 | tf_op jit(solution)/shard_map/dot_general | solution.py:54
  26.4 0.7 convert_reduce_fusion
  27.1 5.1 %collective-permute-done = bf16[1,16,16,768]{3,1,2,0:T(8,128)(2,1)} collective-permute-done((bf16[1,16,16,768]{3,1,2,0:T(8,128)(2,1)}, bf16[1,16,16,768]{3,1,2,0:T(8,128)(2,1)}, u32[]{:S(2)}, u32[]{:S(2)}) %collective-permute-start) | collective-permute-done | bytes 393248 | tf_op jit(solution)/shard_map/ppermute | solution.py:12
  32.2 3.4 %fusion.71 = (bf16[1,16,16,768]{3,1,2,0:T(8,128)(2,1)}, f32[1,16,16,768]{3,1,2,0:T(8,128)}) fusion(bf16[1,16,16,768]{3,1,2,0:T(8,128)(2,1)S(1)} %collective-permute-done.2, f32[768]{0:T(1024)S(1)} %convert_reduce_fusion, bf16[1,16,16,768]{3,1,2,0:T(8,128)(2,1)} %collective-permute-done, f32[768]{0:T(1024)S(1)} %get-tuple-element.6, ...), kind=kOutput, calls=%fused_computation.56 | convolution fusion | flops 27328512 | bytes 5122180 | tf_op jit(solution)/shard_map/rs,ksvj->krvj/dot_general | solution.py:46
  35.7 1.9 %collective-permute-start.4 = (bf16[1,16,16,768]{3,1,2,0:T(8,128)(2,1)}, bf16[1,16,16,768]{3,1,2,0:T(8,128)(2,1)S(1)}, u32[]{:S(2)}, u32[]{:S(2)}) collective-permute-start(bf16[1,16,16,768]{3,1,2,0:T(8,128)(2,1)} %get-tuple-element.8), channel_id=1, source_target_pairs={{0,4},{4,8},{8,12},{12,16},{16,20},{20,24},{24,28},{1,5},{5,9},{9,... | collective-permute-start | bytes 1179656 | tf_op jit(solution)/shard_map/ppermute | solution.py:12
  37.7 4.8 %collective-permute-start.3 = (bf16[1,16,16,768]{3,1,2,0:T(8,128)(2,1)}, bf16[1,16,16,768]{3,1,2,0:T(8,128)(2,1)}, u32[]{:S(2)}, u32[]{:S(2)}) collective-permute-start(bf16[1,16,16,768]{3,1,2,0:T(8,128)(2,1)} %get-tuple-element.8), channel_id=1, source_target_pairs={{4,0},{8,4},{12,8},{16,12},{20,16},{24,20},{28,24},{5,1},{9,5},{13... | collective-permute-start | bytes 1179656 | tf_op jit(solution)/shard_map/ppermute | solution.py:12
  42.5 1.1 %copy.25 = bf16[1,16,16,768]{3,2,1,0:T(8,128)(2,1)S(1)} copy(bf16[1,16,16,768]{3,1,2,0:T(8,128)(2,1)} %get-tuple-element.8) | data formatting | bytes 786432 | tf_op jit(solution)/shard_map/convert_element_type | solution.py:43
  43.6 2.3 %fusion.2 = bf16[256,1536]{1,0:T(8,128)(2,1)S(1)} fusion(f32[256,1536]{1,0:T(8,128)} %bitcast.128, bf16[256,768]{1,0:T(8,128)(2,1)S(1)} %bitcast.131, bf16[768,1536]{1,0:T(8,128)(2,1)S(1)} %copy-done), kind=kOutput, calls=%fused_computation.6 | convolution fusion | flops 604766208 | bytes 5111808 | tf_op jit(solution)/shard_map/dot_general | solution.py:52
  45.9 2.0 %fusion.28 = f32[1,16,16,768]{3,1,2,0:T(8,128)} fusion(bf16[768,1536]{1,0:T(8,128)(2,1)S(1)} %copy-done, bf16[16,16,1536]{2,1,0:T(8,128)(2,1)S(1)} %bitcast.134), kind=kOutput, calls=%fused_computation.24 | convolution fusion | flops 603979776 | bytes 3932160 | tf_op jit(solution)/shard_map/dot_general | solution.py:54
  47.9 2.0 %collective-permute-done.4 = bf16[1,16,16,768]{3,1,2,0:T(8,128)(2,1)S(1)} collective-permute-done((bf16[1,16,16,768]{3,1,2,0:T(8,128)(2,1)}, bf16[1,16,16,768]{3,1,2,0:T(8,128)(2,1)S(1)}, u32[]{:S(2)}, u32[]{:S(2)}) %collective-permute-start.4) | collective-permute-done | bytes 393248 | tf_op jit(solution)/shard_map/ppermute | solution.py:12
  49.9 8.4 %collective-permute-done.3 = bf16[1,16,16,768]{3,1,2,0:T(8,128)(2,1)} collective-permute-done((bf16[1,16,16,768]{3,1,2,0:T(8,128)(2,1)}, bf16[1,16,16,768]{3,1,2,0:T(8,128)(2,1)}, u32[]{:S(2)}, u32[]{:S(2)}) %collective-permute-start.3) | collective-permute-done | bytes 393248 | tf_op jit(solution)/shard_map/ppermute | solution.py:12
  58.3 3.7 %fusion.72 = (bf16[1,16,16,768]{3,1,2,0:T(8,128)(2,1)}, f32[1,16,16,768]{3,1,2,0:T(8,128)}) fusion(f32[1,16,16,768]{3,2,1,0:T(8,128)S(1)} %copy-done.1, bf16[1,16,16,768]{3,1,2,0:T(8,128)(2,1)S(1)} %collective-permute-done.4, f32[768]{0:T(1024)S(1)} %convert_reduce_fusion, bf16[1,16,16,768]{3,1,2,0:T(8,128)(2,1)} %collective-permute-done.3, ...), kind=kOutput, calls=%fused_computation.57 | convolution fusion | flops 27918336 | bytes 5908612 | tf_op jit(solution)/shard_map/rs,ksvj->krvj/dot_general | solution.py:46
  62.1 2.7 %copy.31 = bf16[1024,768]{0,1:T(8,128)(2,1)} copy(bf16[1024,768]{1,0:T(8,128)(2,1)} %param.21) | data formatting | bytes 3145728 | tf_op args[10]
  64.8 0.6 add_select_fusion
  65.4 1.9 %collective-permute-start.6 = (bf16[1,16,16,768]{3,1,2,0:T(8,128)(2,1)S(1)}, bf16[1,16,16,768]{3,1,2,0:T(8,128)(2,1)S(1)}, u32[]{:S(2)}, u32[]{:S(2)}) collective-permute-start(bf16[1,16,16,768]{3,1,2,0:T(8,128)(2,1)S(1)} %copy-done.3), channel_id=1, source_target_pairs={{0,4},{4,8},{8,12},{12,16},{16,20},{20,24},{24,28},{1,5},{5,9},{9,... | collective-permute-start | bytes 1179656 | tf_op jit(solution)/shard_map/ppermute | solution.py:12
  67.3 4.8 %collective-permute-start.5 = (bf16[1,16,16,768]{3,1,2,0:T(8,128)(2,1)S(1)}, bf16[1,16,16,768]{3,1,2,0:T(8,128)(2,1)}, u32[]{:S(2)}, u32[]{:S(2)}) collective-permute-start(bf16[1,16,16,768]{3,1,2,0:T(8,128)(2,1)S(1)} %copy-done.3), channel_id=1, source_target_pairs={{4,0},{8,4},{12,8},{16,12},{20,16},{24,20},{28,24},{5,1},{9,5},{13... | collective-permute-start | bytes 1179656 | tf_op jit(solution)/shard_map/ppermute | solution.py:12
  72.2 2.2 %fusion.3 = bf16[256,1536]{1,0:T(8,128)(2,1)S(1)} fusion(f32[256,1536]{1,0:T(8,128)} %bitcast.129, bf16[256,768]{1,0:T(8,128)(2,1)S(1)} %bitcast.132, bf16[768,1536]{1,0:T(8,128)(2,1)S(1)} %copy-done), kind=kOutput, calls=%fused_computation.7 | convolution fusion | flops 604766208 | bytes 5111808 | tf_op jit(solution)/shard_map/dot_general | solution.py:52
  74.4 2.0 %fusion.31 = f32[1,16,16,768]{3,1,2,0:T(8,128)} fusion(bf16[768,1536]{1,0:T(8,128)(2,1)S(1)} %copy-done, bf16[16,16,1536]{2,1,0:T(8,128)(2,1)S(1)} %bitcast.135), kind=kOutput, calls=%fused_computation.25 | convolution fusion | flops 603979776 | bytes 3932160 | tf_op jit(solution)/shard_map/dot_general | solution.py:54
  76.4 2.8 %collective-permute-done.6 = bf16[1,16,16,768]{3,1,2,0:T(8,128)(2,1)S(1)} collective-permute-done((bf16[1,16,16,768]{3,1,2,0:T(8,128)(2,1)S(1)}, bf16[1,16,16,768]{3,1,2,0:T(8,128)(2,1)S(1)}, u32[]{:S(2)}, u32[]{:S(2)}) %collective-permute-start.6) | collective-permute-done | bytes 393248 | tf_op jit(solution)/shard_map/ppermute | solution.py:12
  79.3 0.8 copy-done.5
  80.1 7.7 %collective-permute-done.5 = bf16[1,16,16,768]{3,1,2,0:T(8,128)(2,1)} collective-permute-done((bf16[1,16,16,768]{3,1,2,0:T(8,128)(2,1)S(1)}, bf16[1,16,16,768]{3,1,2,0:T(8,128)(2,1)}, u32[]{:S(2)}, u32[]{:S(2)}) %collective-permute-start.5) | collective-permute-done | bytes 393248 | tf_op jit(solution)/shard_map/ppermute | solution.py:12
  87.7 2.6 %fusion.73 = (bf16[1,16,16,768]{3,1,2,0:T(8,128)(2,1)S(1)}, f32[1,16,16,768]{3,1,2,0:T(8,128)S(1)}) fusion(f32[1,16,16,768]{3,1,2,0:T(8,128)S(1)} %copy-done.2, bf16[1,16,16,768]{3,1,2,0:T(8,128)(2,1)} %copy-done.5, f32[768]{0:T(1024)S(1)} %convert_reduce_fusion, bf16[1,16,16,768]{3,1,2,0:T(8,128)(2,1)} %collective-permute-done.5, ...), kind=kOutput, calls=%fused_computation.58 | convolution fusion | flops 27918336 | bytes 5908612 | tf_op jit(solution)/shard_map/rs,ksvj->krvj/dot_general | solution.py:46
  90.3 1.3 %copy.32 = f32[1,16,16,768]{3,2,1,0:T(8,128)} copy(f32[1,16,16,768]{3,1,2,0:T(8,128)S(1)} %get-tuple-element.13) | data formatting | bytes 1572864
  91.8 0.8 fusion
  92.6 6.9 %psum.7 = f32[1,1024]{1,0:T(1,128)S(1)} all-reduce(f32[1,1024]{1,0:T(1,128)S(1)} %bitcast.137), channel_id=1, replica_groups=mesh['hel'=8,'rad'=4] {'rad'}, use_global_device_ids=true, to_apply=%region_1.2 | all-reduce | flops 1024 | bytes 8192 | tf_op jit(solution)/shard_map/psum | solution.py:92
  (38 shorter events, 1.1 us)
Async XLA Ops:
  7.2 14.3 %copy-start = (bf16[768,1536]{1,0:T(8,128)(2,1)S(1)}, bf16[768,1536]{1,0:T(8,128)(2,1)}, u32[]{:S(2)}) copy-start(bf16[768,1536]{1,0:T(8,128)(2,1)} %param.13) | copy-start | bytes 7077892
  7.2 9.3 %copy-start.10 = (bf16[1,768]{1,0:T(2,128)(2,1)S(1)}, bf16[1,768]{1,0:T(2,128)(2,1)}, u32[]{:S(2)}) copy-start(bf16[1,768]{1,0:T(2,128)(2,1)} %param.17) | copy-start | bytes 4612
  7.2 25.0 %all-gather.4.cloned.1.call-start = ((), (), s32[]{:S(2)}) async-start(), calls=%async_computation | async-start | bytes 1966080 | tf_op jit(solution)/shard_map/all_gather | solution.py:49
  9.7 48.6 %all-gather.6.cloned.1.call-start = ((), (), s32[]{:S(2)}) async-start(), calls=%async_computation.1 | async-start | bytes 1966080 | tf_op jit(solution)/shard_map/all_gather | solution.py:49
  9.8 17.4 %collective-permute-start.2 = (bf16[1,16,16,768]{3,1,2,0:T(8,128)(2,1)}, bf16[1,16,16,768]{3,1,2,0:T(8,128)(2,1)S(1)}, u32[]{:S(2)}, u32[]{:S(2)}) collective-permute-start(bf16[1,16,16,768]{3,1,2,0:T(8,128)(2,1)} %copy.48), channel_id=1, source_target_pairs={{0,4},{4,8},{8,12},{12,16},{16,20},{20,24},{24,28},{1,5},{5,9},{9,... | collective-permute-start | bytes 1179656 | tf_op jit(solution)/shard_map/ppermute | solution.py:12
  13.2 19.0 %collective-permute-start = (bf16[1,16,16,768]{3,1,2,0:T(8,128)(2,1)}, bf16[1,16,16,768]{3,1,2,0:T(8,128)(2,1)}, u32[]{:S(2)}, u32[]{:S(2)}) collective-permute-start(bf16[1,16,16,768]{3,1,2,0:T(8,128)(2,1)} %copy.48), channel_id=1, source_target_pairs={{4,0},{8,4},{12,8},{16,12},{20,16},{24,20},{28,24},{5,1},{9,5},{13... | collective-permute-start | bytes 1179656 | tf_op jit(solution)/shard_map/ppermute | solution.py:12
  17.1 9.3 %collective-permute-start.1 = (bf16[1,768]{1,0:T(2,128)(2,1)}, bf16[1,768]{1,0:T(2,128)(2,1)}, u32[]{:S(2)}, u32[]{:S(2)}) collective-permute-start(bf16[1,768]{1,0:T(2,128)(2,1)} %get-tuple-element.7), channel_id=1, source_target_pairs={{0,4},{4,8},{8,12},{12,16},{16,20},{20,24},{24,28},{1,5},{5,9},{9,... | collective-permute-start | bytes 4616 | tf_op jit(solution)/shard_map/ppermute | solution.py:12
  23.7 2.7 %copy-start.11 = (f32[16]{0:T(128)S(1)}, f32[16]{0:T(128)}, u32[]{:S(2)}) copy-start(f32[16]{0:T(128)} %param.15) | copy-start | bytes 196
  23.7 8.5 %copy-start.1 = (f32[1,16,16,768]{3,2,1,0:T(8,128)S(1)}, f32[1,16,16,768]{3,2,1,0:T(8,128)}, u32[]{:S(2)}) copy-start(f32[1,16,16,768]{3,2,1,0:T(8,128)} %param.11) | copy-start | bytes 2359300
  23.7 8.5 %copy-start.6 = (f32[16]{0:T(128)S(1)}, f32[16]{0:T(128)}, u32[]{:S(2)}) copy-start(f32[16]{0:T(128)} %param.16) | copy-start | bytes 196
  35.7 52.0 %all-gather.8.cloned.1.call-start = ((), (), s32[]{:S(2)}) async-start(), calls=%async_computation.2 | async-start | bytes 1966080 | tf_op jit(solution)/shard_map/all_gather | solution.py:49
  35.7 14.1 %collective-permute-start.4 = (bf16[1,16,16,768]{3,1,2,0:T(8,128)(2,1)}, bf16[1,16,16,768]{3,1,2,0:T(8,128)(2,1)S(1)}, u32[]{:S(2)}, u32[]{:S(2)}) collective-permute-start(bf16[1,16,16,768]{3,1,2,0:T(8,128)(2,1)} %get-tuple-element.8), channel_id=1, source_target_pairs={{0,4},{4,8},{8,12},{12,16},{16,20},{20,24},{24,28},{1,5},{5,9},{9,... | collective-permute-start | bytes 1179656 | tf_op jit(solution)/shard_map/ppermute | solution.py:12
  37.7 20.6 %collective-permute-start.3 = (bf16[1,16,16,768]{3,1,2,0:T(8,128)(2,1)}, bf16[1,16,16,768]{3,1,2,0:T(8,128)(2,1)}, u32[]{:S(2)}, u32[]{:S(2)}) collective-permute-start(bf16[1,16,16,768]{3,1,2,0:T(8,128)(2,1)} %get-tuple-element.8), channel_id=1, source_target_pairs={{4,0},{8,4},{12,8},{16,12},{20,16},{24,20},{28,24},{5,1},{9,5},{13... | collective-permute-start | bytes 1179656 | tf_op jit(solution)/shard_map/ppermute | solution.py:12
  62.0 2.7 %copy-start.7 = (s32[1024]{0:T(1024)S(1)}, s32[1024]{0:T(1024)}, u32[]{:S(2)}) copy-start(s32[1024]{0:T(1024)} %param.20) | copy-start | bytes 12292
  62.1 2.7 %copy-start.8 = (s32[1024]{0:T(1024)S(1)}, s32[1024]{0:T(1024)}, u32[]{:S(2)}) copy-start(s32[1024]{0:T(1024)} %param.19) | copy-start | bytes 12292
  62.1 3.3 %copy-start.3 = (bf16[1,16,16,768]{3,1,2,0:T(8,128)(2,1)S(1)}, bf16[1,16,16,768]{3,1,2,0:T(8,128)(2,1)}, u32[]{:S(2)}) copy-start(bf16[1,16,16,768]{3,1,2,0:T(8,128)(2,1)} %get-tuple-element.10) | copy-start | bytes 1179652
  65.4 13.9 %collective-permute-start.6 = (bf16[1,16,16,768]{3,1,2,0:T(8,128)(2,1)S(1)}, bf16[1,16,16,768]{3,1,2,0:T(8,128)(2,1)S(1)}, u32[]{:S(2)}, u32[]{:S(2)}) collective-permute-start(bf16[1,16,16,768]{3,1,2,0:T(8,128)(2,1)S(1)} %copy-done.3), channel_id=1, source_target_pairs={{0,4},{4,8},{8,12},{12,16},{16,20},{20,24},{24,28},{1,5},{5,9},{9,... | collective-permute-start | bytes 1179656 | tf_op jit(solution)/shard_map/ppermute | solution.py:12
  67.3 20.4 %collective-permute-start.5 = (bf16[1,16,16,768]{3,1,2,0:T(8,128)(2,1)S(1)}, bf16[1,16,16,768]{3,1,2,0:T(8,128)(2,1)}, u32[]{:S(2)}, u32[]{:S(2)}) collective-permute-start(bf16[1,16,16,768]{3,1,2,0:T(8,128)(2,1)S(1)} %copy-done.3), channel_id=1, source_target_pairs={{4,0},{8,4},{12,8},{16,12},{20,16},{24,20},{28,24},{5,1},{9,5},{13... | collective-permute-start | bytes 1179656 | tf_op jit(solution)/shard_map/ppermute | solution.py:12
  74.4 13.3 %copy-start.2 = (f32[1,16,16,768]{3,1,2,0:T(8,128)S(1)}, f32[1,16,16,768]{3,1,2,0:T(8,128)}, u32[]{:S(2)}) copy-start(f32[1,16,16,768]{3,1,2,0:T(8,128)} %get-tuple-element.9) | copy-start | bytes 2359300
  79.3 0.8 copy-start.5
  90.3 1.5 %copy-start.4 = (bf16[1024,768]{0,1:T(8,128)(2,1)S(1)}, bf16[1024,768]{0,1:T(8,128)(2,1)}, u32[]{:S(2)}) copy-start(bf16[1024,768]{0,1:T(8,128)(2,1)} %copy.31) | copy-start | bytes 4718596
  90.3 1.5 %copy-start.9 = (s32[1024]{0:T(1024)S(1)}, s32[1024]{0:T(1024)}, u32[]{:S(2)}) copy-start(s32[1024]{0:T(1024)} %add_select_fusion) | copy-start | bytes 12292
Sparse Core Ops, SparseCore 0:
  9.8 20.6 all-gather.3
  35.8 19.6 all-gather.5
  62.2 19.6 all-gather.7
where the time goes:
time: 107 us
  waiting for transfers between devices  26.1 us (24%)
  starting transfers between devices  23.6 us (22%)
  matrix products  23.1 us (22%)
  between operations  14.7 us (14%)
  local copies, waits for them, and re-layouts  10.3 us (10%)
  blocking collectives  6.9 us (6%)
  other arithmetic  1.91 us (2%)
    ppermute x7, waiting for transfers between devices, from_behind(): return lax.ppermute(block, axis, route)  26 us
    ppermute x7, starting transfers between devices, from_behind(): return lax.ppermute(block, axis, route)  23.5 us
    dot_general x3, matrix products, ham(): jnp.einsum('rs,ksvj->krvj', kin_rows, lax.all_gather(packed, 'rad', axis=...  9.73 us
    unnamed x27, local copies, waits for them, and re-layouts  7.29 us
    psum x1, blocking collectives, per_device(): summed = lax.psum(partial_amp, 'rad')  6.9 us
    dot_general x3, matrix products, ham(): jnp.dot(packed.reshape(-1, nang), basis, preferred_element_type=jnp.float32)  6.64 us
    dot_general x3, matrix products, ham(): lax.dot_general(scaled.reshape(-1, nquad), basis, (((1,), (1,)), ((), ())...  5.97 us
    convert_element_type x3, local copies, waits for them, and re-layouts, ham(): packed = psi.astype(jnp.bfloat16)  2.37 us
  transfers between devices with their start and end apart: 10, of which 5 were waited for; matrix products, arithmetic and copies ran while one was open for 18% of the time, Pallas kernels for 0%

commit v1 on v0

v1 whole, which is shorter than its diff:
```python
import functools

import jax
import jax.numpy as jnp
from jax import lax
from jax.experimental import pallas as pl
from jax.experimental.pallas import tpu as pltpu
from jax.sharding import Mesh
from jax.sharding import PartitionSpec as P

ITERS = 3
LANES = 128
NT = (((1,), (1,)), ((), ()))
F32 = jnp.float32
BF16 = jnp.bfloat16


def windows(blocks, groups):
    own = blocks // groups
    spans = []
    for n in range(1, ITERS + 1):
        reach = ITERS - n
        size = max(
            min(blocks, (g + 1) * own + reach) - max(0, g * own - reach) for g in range(groups)
        )
        spans.append((size, reach))
    return own, spans


def propagate(shape, rotated, n_parts, *refs):
    blocks, ygroups, groups, slab, nang, nquad, nchan, qstep, jstep = shape
    where_ref = refs[0]
    psi_parts = refs[1 : 1 + n_parts]
    pot_parts = refs[1 + n_parts : 1 + 2 * n_parts]
    basis_ref, kin_ref, rad_ref, vib_ref, proj_ref, out_ref = refs[
        1 + 2 * n_parts : 7 + 2 * n_parts
    ]
    pb0, pb1, pb2, p1, p2, scaled, pot, damp, radial, centri, coup = refs[7 + 2 * n_parts :]
    core = where_ref[0]
    vib = where_ref[1]
    nrad = ygroups * groups * slab
    own, spans = windows(blocks, groups)
    chan_rows = nang // LANES

    zero_block = jnp.zeros((1, nrad, nang), BF16)
    for buf in (pb0, pb1, pb2):
        buf[pl.ds(0, 1)] = zero_block
        buf[pl.ds(blocks + 1, 1)] = zero_block
    coup[0] = jnp.zeros((1, nang), F32)

    part_index = 0
    for psi_ref, pot_ref in zip(psi_parts, pot_parts):
        for i in range(psi_ref.shape[0]):
            slot = lax.rem(core + part_index, groups) if rotated else part_index
            for y in range(ygroups):
                row = pl.multiple_of((y * groups + slot) * slab, slab)
                for k in range(blocks):
                    pb0[k + 1, pl.ds(row, slab), :] = psi_ref[i, k, y, :, :nang]
                pot[pl.ds(row, slab), :] = pot_ref[i, y, :, :nquad].astype(F32)
                extra = pot_ref[i, y, :, nquad:].astype(F32)
                radial[pl.ds(row, slab), :] = jnp.broadcast_to(
                    extra[:, 0:1] + extra[:, 1:2], (slab, jstep)
                )
                damp[pl.ds(row, slab), :] = jnp.broadcast_to(
                    extra[:, 2:3] + extra[:, 3:4], (slab, jstep)
                )
            part_index += 1
    for k in range(blocks):
        page = psi_parts[0][0, k, 0, :, nang:].astype(F32)
        coup[k + 1] = jnp.concatenate([page[i : i + 1, :] for i in range(chan_rows)], axis=1)
        kvalue = page[chan_rows : chan_rows + 1, 0:1]
        centri[k] = jnp.broadcast_to(-2.0 * kvalue * kvalue, (1, jstep))

    def begin(n):
        size, reach = spans[max(n, 1) - 1]
        return jnp.clip(core * own - reach, 0, blocks - size)

    def step(n, source, prev, cur, target_b, target_f):
        size, reach = spans[n - 1]
        start = begin(n)
        rows = size * nrad
        shifts = [start - begin(m) for m in (n - 1, n - 2)]

        @pl.loop(0, nquad // qstep)
        def _(qi):
            q0 = pl.multiple_of(qi * qstep, qstep)
            grid = jnp.dot(
                source[pl.ds(start + 1, size)].reshape(rows, nang),
                basis_ref[:, pl.ds(q0, qstep)],
                preferred_element_type=F32,
            )
            prod = grid.reshape(size, nrad, qstep) * pot[:, pl.ds(q0, qstep)][None]
            scaled[pl.ds(0, rows), pl.ds(q0, qstep)] = prod.astype(BF16).reshape(rows, qstep)

        @pl.loop(0, nang // jstep)
        def _(ji):
            j0 = pl.multiple_of(ji * jstep, jstep)
            cols = pl.ds(j0, jstep)
            ang = lax.dot_general(
                scaled[pl.ds(0, rows), :], basis_ref[cols, :], NT, preferred_element_type=F32
            ).reshape(size, nrad, jstep)
            for i in range(size):
                k = start + i
                kin = jnp.dot(kin_ref[...], source[k + 1, :, cols], preferred_element_type=F32)
                upper = source[k + 2, :, cols].astype(F32)
                lower = source[k, :, cols].astype(F32)
                cor = coup[k + 1, :, cols] * upper + coup[k, :, cols] * lower
                if cur is None:
                    here = source[k + 1, :, cols].astype(F32)
                else:
                    here = cur[shifts[0] + i, :, cols]
                total = kin + ang[i] + centri[k] * radial[...] * here + cor
                if n == 1:
                    new = damp[...] * total
                else:
                    if n == 2:
                        before = prev[k + 1, :, cols].astype(F32)
                    else:
                        before = prev[shifts[1] + i, :, cols]
                    new = damp[...] * (2.0 * total - damp[...] * before)
                target_b[k + 1, :, cols] = new.astype(BF16)
                if target_f is not None:
                    target_f[i, :, cols] = new

    step(1, pb0, None, None, pb1, p1)
    step(2, pb1, pb0, p1, pb2, p2)
    step(3, pb2, p1, p2, pb0, None)

    first = core * own
    chan_block = nchan // (ygroups * groups)
    pieces = -(-chan_block // LANES)
    final = pb0[pl.ds(first + 1, own)].reshape(own * nrad, nang)
    rows_at = lax.broadcasted_iota(jnp.int32, (nrad, chan_block), 0)
    for y in range(ygroups):
        for slot in range(groups):
            dest = lax.rem(slot - core + groups, groups) if rotated else slot
            c0 = (y * groups + slot) * chan_block
            table = lax.dot_general(
                final, proj_ref[pl.ds(c0, chan_block), :], NT, preferred_element_type=F32
            ).reshape(own, nrad, chan_block)
            hit = (rows_at == rad_ref[:, c0 : c0 + chan_block]) & (
                vib_ref[:, c0 : c0 + chan_block] == vib
            )
            row = (y * groups + slot) * slab
            for i in range(own):
                amp = jnp.sum(jnp.where(hit, table[i], 0.0), axis=0, keepdims=True)
                if pieces * LANES > chan_block:
                    amp = jnp.concatenate(
                        [amp, jnp.zeros((1, pieces * LANES - chan_block), F32)], axis=1
                    )
                high = amp.astype(BF16).astype(F32)
                low = amp - high
                lines = [high[:, s * LANES : (s + 1) * LANES] for s in range(pieces)]
                lines += [low[:, s * LANES : (s + 1) * LANES] for s in range(pieces)]
                lines.append(jnp.zeros((slab - 2 * pieces, LANES), F32))
                out_ref[dest, i, y, :, nang:] = jnp.concatenate(lines, axis=0).astype(BF16)
                out_ref[dest, i, y, :, :nang] = pb0[first + i + 1, row : row + slab, :]


def run_blocks(where, psi_parts, pot_parts, basis, kinetic, chan_rad, chan_vib, projector, dims):
    blocks, ygroups, groups, slab = dims
    nang, nquad = basis.shape
    nchan = projector.shape[0]
    nrad = ygroups * groups * slab
    own, spans = windows(blocks, groups)
    qstep, jstep = 256, 256
    shape = (blocks, ygroups, groups, slab, nang, nquad, nchan, qstep, jstep)
    rotated = len(psi_parts) > 1
    vmem = pl.BlockSpec(memory_space=pltpu.VMEM)
    smem = pl.BlockSpec(memory_space=pltpu.SMEM)
    body = functools.partial(propagate, shape, rotated, len(psi_parts))
    n_in = 2 * len(psi_parts) + 5
    most = spans[0][0]
    return pl.pallas_call(
        body,
        out_shape=jax.ShapeDtypeStruct((groups, own, ygroups, slab, nang + LANES), BF16),
        in_specs=[smem] + [vmem] * n_in,
        out_specs=vmem,
        scratch_shapes=[
            pltpu.VMEM((blocks + 2, nrad, nang), BF16),
            pltpu.VMEM((blocks + 2, nrad, nang), BF16),
            pltpu.VMEM((blocks + 2, nrad, nang), BF16),
            pltpu.VMEM((spans[0][0], nrad, nang), F32),
            pltpu.VMEM((spans[1][0], nrad, nang), F32),
            pltpu.VMEM((most * nrad, nquad), BF16),
            pltpu.VMEM((nrad, nquad), F32),
            pltpu.VMEM((nrad, jstep), F32),
            pltpu.VMEM((nrad, jstep), F32),
            pltpu.VMEM((blocks, 1, jstep), F32),
            pltpu.VMEM((blocks + 1, 1, nang), F32),
        ],
        compiler_params=pltpu.CompilerParams(vmem_limit_bytes=60 * 1024 * 1024),
        name="propagate",
    )(where, *psi_parts, *pot_parts, basis, kinetic, chan_rad, chan_vib, projector)


def two_halves(value):
    high = lax.reduce_precision(value, 8, 7)
    return high.astype(BF16), (value - high).astype(BF16)


def per_device(
    psi_start,
    potential,
    basis,
    kinetic,
    radial_factor,
    damping,
    coupling,
    helicity,
    chan_rad,
    chan_vib,
    projector,
):
    _, slab, nvib, nang = psi_start.shape
    nquad = basis.shape[1]
    nchan = projector.shape[0]
    blocks = lax.axis_size("hel")
    ygroups = lax.axis_size("y")
    groups = lax.axis_size("c")
    hel_index = lax.axis_index("hel")
    y_index = lax.axis_index("y")
    core = lax.axis_index("c")
    swap = [(0, 1), (1, 0)]

    rf_high, rf_low = two_halves(radial_factor)
    dp_high, dp_low = two_halves(damping)
    extra = jnp.stack([rf_high, rf_low, dp_high, dp_low], axis=1)
    extra = jnp.pad(extra, ((0, 0), (0, LANES - extra.shape[1])))
    mine = lax.dynamic_slice_in_dim(potential, hel_index * ygroups, ygroups, 1).astype(BF16)
    pages = jnp.concatenate(
        [
            jnp.swapaxes(mine, 0, 1),
            jnp.broadcast_to(extra[None], (ygroups,) + extra.shape),
        ],
        axis=2,
    )
    if ygroups == 2:
        kept = lax.dynamic_index_in_dim(pages, y_index, 0, False)
        got = lax.ppermute(lax.dynamic_index_in_dim(pages, 1 - y_index, 0, False), "y", swap)
        pages = jnp.stack(
            [jnp.where(y_index == 0, kept, got), jnp.where(y_index == 0, got, kept)]
        )
    elif ygroups > 2:
        pages = lax.all_to_all(pages, "y", 0, 0, tiled=True)

    ce = jnp.where(hel_index < blocks - 1, coupling, jnp.zeros_like(coupling))
    chan_rows = nang // LANES
    aux = jnp.concatenate(
        [
            ce.reshape(chan_rows, LANES),
            jnp.broadcast_to(helicity.astype(BF16)[:, None], (1, LANES)),
            jnp.zeros((slab - chan_rows - 1, LANES), BF16),
        ],
        axis=0,
    )
    send = jnp.concatenate(
        [
            jnp.swapaxes(psi_start[0].astype(BF16), 0, 1),
            jnp.broadcast_to(aux[None], (nvib, slab, LANES)),
        ],
        axis=2,
    )
    received = lax.all_to_all(send, ("hel", "y"), 0, 0, tiled=True)
    received = received.reshape(1, blocks, ygroups, slab, nang + LANES)
    pages = pages[None]
    if groups == 2:
        psi_parts = [received, lax.ppermute(received, "c", swap)]
        pot_parts = [pages, lax.ppermute(pages, "c", swap)]
    else:
        psi_parts = [lax.all_gather(received, "c", axis=0, tiled=True)]
        pot_parts = [lax.all_gather(pages, "c", axis=0, tiled=True)]

    where = jnp.stack([core, hel_index * ygroups + y_index]).astype(jnp.int32)
    result = run_blocks(
        where,
        psi_parts,
        pot_parts,
        basis,
        kinetic,
        chan_rad[None],
        chan_vib[None],
        projector,
        (blocks, ygroups, groups, slab),
    )
    if groups == 2:
        kept = result[0]
        got = lax.ppermute(result[1], "c", swap)
        back = jnp.concatenate(
            [jnp.where(core == 0, kept, got), jnp.where(core == 0, got, kept)], axis=0
        )
    else:
        back = lax.all_to_all(result, "c", 0, 0, tiled=True)
    back = back.reshape(blocks * ygroups, slab, nang + LANES)
    home = lax.all_to_all(back, ("hel", "y"), 0, 0, tiled=True)
    psi_final = jnp.swapaxes(home[:, :, :nang], 0, 1).astype(F32)[None]
    chan_block = nchan // (ygroups * groups)
    pieces = -(-chan_block // LANES)
    lines = jnp.sum(home[:, : 2 * pieces, nang:].astype(F32), axis=0)
    amplitude = (lines[:pieces] + lines[pieces:]).reshape(1, -1)[:, :chan_block]
    return (psi_final, amplitude)


def solution(mesh):
    nhel, nrad = mesh.shape["hel"], mesh.shape["rad"]

    def run(*args):
        nvib = args[0].shape[2]
        groups = nhel * nrad // nvib
        fine = Mesh(
            mesh.devices.reshape(nhel, nrad // groups, groups), ("hel", "y", "c")
        )
        rad = ("y", "c")
        placed = (
            P("hel", rad, None, None),
            P(rad, None, None),
            P(),
            P(),
            P(rad),
            P(rad),
            P("hel", None),
            P("hel"),
            P(),
            P(),
            P(),
        )
        return jax.shard_map(
            per_device,
            mesh=fine,
            in_specs=placed,
            out_specs=(P("hel", rad, None, None), P("hel", rad)),
            check_vma=False,
        )(*args)

    return run
```

time: 107 us -> 67.2 us (0.63)
  the two profiles are of different devices: /device:TPU:24 before, /device:TPU:0 now
where the time goes in v1:
time: 67.2 us; the launch traced here: 66.8 us
  blocking collectives  17.7 us (26%)
  Pallas kernels  14.4 us (21%)
  waiting for transfers between devices  13.6 us (20%)
  starting transfers between devices  10.4 us (15%)
  local copies, waits for them, and re-layouts  5.06 us (8%)
  other arithmetic  4.02 us (6%)
  between operations  1.58 us (2%)
    all_to_all x1, blocking collectives, per_device(): home = lax.all_to_all(back, ('hel', 'y'), 0, 0, tiled=True)  17.7 us
    pallas_call x1, Pallas kernels, run_blocks(): pl.pallas_call(body, out_shape=jax.ShapeDtypeStruct((groups, own, ygroups...  14.4 us
    all_to_all x1, waiting for transfers between devices, per_device(): received = lax.all_to_all(send, ('hel', 'y'), 0, 0, tiled=True)  11.6 us
    all_to_all x1, starting transfers between devices, per_device(): received = lax.all_to_all(send, ('hel', 'y'), 0, 0, tiled=True)  7.66 us
    unnamed x18, local copies, waits for them, and re-layouts  3.83 us
    ppermute x1, starting transfers between devices, per_device(): lax.ppermute(lax.dynamic_index_in_dim(pages, 1 - y_index, 0, False), 'y',...  1.98 us
    ppermute x1, waiting for transfers between devices, per_device(): got = lax.ppermute(result[1], 'c', swap)  1.35 us
  transfers between devices with their start and end apart: 5, of which 3 were waited for; matrix products, arithmetic and copies ran while one was open for 1% of the time, Pallas kernels for 0%

profile of v1, /device:TPU:0, one launch (start us, length us, event | category | flops | bytes accessed | tf_op | source)
XLA Modules:
  0.0 66.8 jit_solution(4135603425526157431)
XLA Ops:
  0.6 0.0 copy-start
  0.6 0.0 copy-start.6
  0.7 0.0 copy-start.5
  1.4 0.1 pad.18.clone
  1.5 0.1 pad.19.clone
  1.6 1.6 %copy.32 = bf16[1,16,16,768]{3,1,2,0:T(8,128)(2,1)S(1)} copy(f32[1,16,16,768]{3,2,1,0:T(8,128)} %param.11) | data formatting | bytes 1179648 | tf_op args[0]
  3.2 0.7 %fusion.6 = bf16[768]{0:T(1024)(128)(2,1)S(1)} fusion(bf16[1,768]{1,0:T(2,128)(2,1)} %param.17, pred[]{:T(512)S(6)} %lt.13), kind=kLoop, calls=%fused_computation.25 | loop fusion | flops 768 | bytes 3073 | tf_op jit(solution)/shard_map/jit(_where)/select_n | solution.py:247
  3.9 0.1 maximum_maximum_fusion
  4.0 0.8 %pad_maximum_fusion = bf16[16,16,896]{2,1,0:T(8,128)(2,1)} fusion(bf16[16,16,128]{2,1,0:T(8,128)(2,1)S(1)} %broadcast_in_dim.45, bf16[16,16,768]{2,1,0:T(8,128)(2,1)S(1)} %bitcast.54), kind=kLoop, calls=%fused_computation.2 | loop fusion | flops 917504 | bytes 917504 | tf_op jit(solution)/shard_map/concatenate | solution.py:257
  4.8 7.7 %all-to-all-start = ((bf16[16,16,896]{2,1,0:T(8,128)(2,1)}), bf16[16,16,896]{2,1,0:T(8,128)(2,1)S(1)}, u32[]{:S(2)}, u32[]{:S(2)}) async-start(bf16[16,16,896]{2,1,0:T(8,128)(2,1)} %pad_maximum_fusion), calls=%async_computation | async-start | bytes 917504 | tf_op jit(solution)/shard_map/all_to_all | solution.py:264
  12.5 0.1 copy.25
  12.6 0.1 constant_dynamic-slice_fusion
  12.7 2.0 %collective-permute-start.1 = (bf16[16,1664]{1,0:T(8,128)(2,1)S(1)}, bf16[16,1664]{1,0:T(8,128)(2,1)S(1)}, u32[]{:S(2)}, u32[]{:S(2)}) collective-permute-start(bf16[16,1664]{1,0:T(8,128)(2,1)S(1)} %fusion.3), channel_id=1, source_target_pairs={{0,2},{2,0},{1,3},{3,1},{4,6},{6,4},{5,7},{7,5},{8,10},{10,8},{9,1... | collective-permute-start | bytes 159752 | tf_op jit(solution)/shard_map/ppermute | solution.py:240
  14.7 11.6 %all-to-all-done = bf16[16,16,896]{2,1,0:T(8,128)(2,1)S(1)} async-done(((bf16[16,16,896]{2,1,0:T(8,128)(2,1)}), bf16[16,16,896]{2,1,0:T(8,128)(2,1)S(1)}, u32[]{:S(2)}, u32[]{:S(2)}) %all-to-all-start) | async-done | bytes 458784 | tf_op jit(solution)/shard_map/all_to_all | solution.py:264
  26.3 0.0 collective-permute-start
  26.3 0.0 collective-permute-done.1
  26.4 0.6 collective-permute-start.2
  26.9 0.7 pad_add_fusion.refs_0_
  27.6 0.7 %collective-permute-done.2.refs_4_ = bf16[1,2,16,1664]{3,2,1,0:T(8,128)(2,1)S(1)} collective-permute-done((bf16[1,2,16,1664]{3,2,1,0:T(8,128)(2,1)S(1)}, bf16[1,2,16,1664]{3,2,1,0:T(8,128)(2,1)S(1)}, u32[]{:S(2)}, u32[]{:S(2)}) %collective-permute-start.2) | collective-permute-done | bytes 106528 | tf_op jit(solution)/shard_map/ppermute | solution.py:269
  28.3 0.0 collective-permute-done.refs_2_
  28.3 0.6 copy-done.4
  28.9 0.2 copy-done.2
  29.1 14.4 %propagate.1 = bf16[2,4,2,16,896]{4,3,2,1,0:T(8,128)(2,1)} custom-call(s32[2]{0:T(128)} %pad_add_fusion.refs_0_, bf16[1,8,2,16,896]{4,3,2,1,0:T(8,128)(2,1)} %bitcast.52, bf16[1,8,2,16,896]{4,3,2,1,0:T(8,128)(2,1)} %copy-done.2, bf16[1,2,16,1664]{3,2,1,0:T(8,128)(2,1)} %copy-done.3, bf16[1,2,16,1664]{3,2,1,0:T(8,128)(2,1)} %copy-done.4, ...), custom_call_target="tpu_custom_call" | custom-call | tf_op jit(solution)/shard_map/propagate/pallas_call | solution.py:174
  43.5 1.0 %slice_bitcast_fusion = bf16[4,2,16,896]{3,2,1,0:T(8,128)(2,1)S(1)} fusion(bf16[2,4,2,16,896]{4,3,2,1,0:T(8,128)(2,1)} %propagate.1), kind=kLoop, calls=%fused_computation.5 | loop fusion | bytes 458752 | tf_op jit(solution)/shard_map/squeeze | solution.py:288
  44.4 0.2 collective-permute-start.3
  44.6 1.4 %collective-permute-done.3 = bf16[4,2,16,896]{3,2,1,0:T(8,128)(2,1)S(1)} collective-permute-done((bf16[4,2,16,896]{3,2,1,0:T(8,128)(2,1)S(1)}, bf16[4,2,16,896]{3,2,1,0:T(8,128)(2,1)S(1)}, u32[]{:S(2)}, u32[]{:S(2)}) %collective-permute-start.3) | collective-permute-done | bytes 229408 | tf_op jit(solution)/shard_map/ppermute | solution.py:288
  46.0 1.0 %broadcast_select_fusion.1 = (bf16[4,2,16,896]{3,2,1,0:T(8,128)(2,1)S(1)}, bf16[4,2,16,896]{3,2,1,0:T(8,128)(2,1)S(1)}) fusion(bf16[4,2,16,896]{3,2,1,0:T(8,128)(2,1)S(1)} %collective-permute-done.3, pred[]{:T(512)S(6)} %eq.8, bf16[2,4,2,16,896]{4,3,2,1,0:T(8,128)(2,1)} %propagate.1), kind=kLoop, calls=%fused_computation.8 | loop fusion | flops 229376 | bytes 917505 | tf_op jit(solution)/shard_map/jit(_where)/select_n | solution.py:290
  47.0 0.1 pad_maximum_fusion.1
  47.0 17.7 %all_to_all.10 = bf16[16,16,896]{2,1,0:T(8,128)(2,1)S(1)} all-to-all(bf16[16,16,896]{2,1,0:T(8,128)(2,1)S(1)} %bitcast.53), channel_id=1, replica_groups=mesh['hel'=8,'y'=2,'c'=2] {'hel','y'}, dimensions={0} | all-to-all | bytes 917504 | tf_op jit(solution)/shard_map/all_to_all | solution.py:295
  64.8 0.6 slice_add_fusion
  65.4 0.1 convert_bitcast_fusion
  65.4 1.3 %copy.23 = f32[1,16,16,768]{3,2,1,0:T(8,128)} copy(f32[1,16,16,768]{3,1,2,0:T(8,128)S(1)} %convert_bitcast_fusion) | data formatting | bytes 1572864
  (20 shorter events, 0.2 us)
Async XLA Ops:
  0.6 12.0 %copy-start = (f32[16,16,1536]{2,1,0:T(8,128)S(1)}, f32[16,16,1536]{2,1,0:T(8,128)}, u32[]{:S(2)}) copy-start(f32[16,16,1536]{2,1,0:T(8,128)} %param.12) | copy-start | bytes 4718596
  0.6 11.8 %copy-start.6 = (f32[16]{0:T(128)S(1)}, f32[16]{0:T(128)}, u32[]{:S(2)}) copy-start(f32[16]{0:T(128)} %param.16) | copy-start | bytes 196
  0.7 11.8 %copy-start.5 = (f32[16]{0:T(128)S(1)}, f32[16]{0:T(128)}, u32[]{:S(2)}) copy-start(f32[16]{0:T(128)} %param.15) | copy-start | bytes 196
  4.8 21.5 %all-to-all-start = ((bf16[16,16,896]{2,1,0:T(8,128)(2,1)}), bf16[16,16,896]{2,1,0:T(8,128)(2,1)S(1)}, u32[]{:S(2)}, u32[]{:S(2)}) async-start(bf16[16,16,896]{2,1,0:T(8,128)(2,1)} %pad_maximum_fusion), calls=%async_computation | async-start | bytes 917504 | tf_op jit(solution)/shard_map/all_to_all | solution.py:264
  12.7 13.6 %collective-permute-start.1 = (bf16[16,1664]{1,0:T(8,128)(2,1)S(1)}, bf16[16,1664]{1,0:T(8,128)(2,1)S(1)}, u32[]{:S(2)}, u32[]{:S(2)}) collective-permute-start(bf16[16,1664]{1,0:T(8,128)(2,1)S(1)} %fusion.3), channel_id=1, source_target_pairs={{0,2},{2,0},{1,3},{3,1},{4,6},{6,4},{5,7},{7,5},{8,10},{10,8},{9,1... | collective-permute-start | bytes 159752 | tf_op jit(solution)/shard_map/ppermute | solution.py:240
  26.3 2.0 %copy-start.1 = (bf16[16,16,896]{2,1,0:T(8,128)(2,1)}, bf16[16,16,896]{2,1,0:T(8,128)(2,1)S(1)}, u32[]{:S(2)}) copy-start(bf16[16,16,896]{2,1,0:T(8,128)(2,1)S(1)} %all-to-all-done) | copy-start | bytes 1376260
  26.3 2.0 %collective-permute-start = (bf16[1,8,2,16,896]{4,3,2,1,0:T(8,128)(2,1)S(1)}, bf16[1,8,2,16,896]{4,3,2,1,0:T(8,128)(2,1)S(1)}, u32[]{:S(2)}, u32[]{:S(2)}) collective-permute-start(bf16[1,8,2,16,896]{4,3,2,1,0:T(8,128)(2,1)S(1)} %bitcast.51), channel_id=1, source_target_pairs={{0,1},{1,0},{2,3},{3,2},{4,5},{5,4},{6,7},{7,6},{8,9},{9,8},{10,11... | collective-permute-start | bytes 1376264 | tf_op jit(solution)/shard_map/ppermute | solution.py:268
  26.4 1.9 %copy-start.3 = (bf16[1,2,16,1664]{3,2,1,0:T(8,128)(2,1)}, bf16[1,2,16,1664]{3,2,1,0:T(8,128)(2,1)S(1)}, u32[]{:S(2)}) copy-start(bf16[1,2,16,1664]{3,2,1,0:T(8,128)(2,1)S(1)} %maximum_bitcast_fusion.refs_3_) | copy-start | bytes 319492
  26.4 1.9 %collective-permute-start.2 = (bf16[1,2,16,1664]{3,2,1,0:T(8,128)(2,1)S(1)}, bf16[1,2,16,1664]{3,2,1,0:T(8,128)(2,1)S(1)}, u32[]{:S(2)}, u32[]{:S(2)}) collective-permute-start(bf16[1,2,16,1664]{3,2,1,0:T(8,128)(2,1)S(1)} %maximum_bitcast_fusion.refs_3_), channel_id=1, source_target_pairs={{0,1},{1,0},{2,3},{3,2},{4,5},{5,4},{6,7},{7,6},{8,9},{9,8},{10,11... | collective-permute-start | bytes 319496 | tf_op jit(solution)/shard_map/ppermute | solution.py:269
  28.3 0.7 copy-start.4
  28.3 0.8 %copy-start.2 = (bf16[1,8,2,16,896]{4,3,2,1,0:T(8,128)(2,1)}, bf16[1,8,2,16,896]{4,3,2,1,0:T(8,128)(2,1)S(1)}, u32[]{:S(2)}) copy-start(bf16[1,8,2,16,896]{4,3,2,1,0:T(8,128)(2,1)S(1)} %collective-permute-done.refs_2_) | copy-start | bytes 1376260
  44.4 1.6 %collective-permute-start.3 = (bf16[4,2,16,896]{3,2,1,0:T(8,128)(2,1)S(1)}, bf16[4,2,16,896]{3,2,1,0:T(8,128)(2,1)S(1)}, u32[]{:S(2)}, u32[]{:S(2)}) collective-permute-start(bf16[4,2,16,896]{3,2,1,0:T(8,128)(2,1)S(1)} %slice_bitcast_fusion), channel_id=1, source_target_pairs={{0,1},{1,0},{2,3},{3,2},{4,5},{5,4},{6,7},{7,6},{8,9},{9,8},{10,11... | collective-permute-start | bytes 688136 | tf_op jit(solution)/shard_map/ppermute | solution.py:288

commit v2 on v0

v2 whole, which is shorter than its diff:
```python
import functools

import jax
import jax.numpy as jnp
from jax import lax
from jax.experimental import pallas as pl
from jax.experimental.pallas import tpu as pltpu
from jax.sharding import Mesh
from jax.sharding import PartitionSpec as P

ITERS = 3
LANES = 128
STEP = 256
NT = (((1,), (1,)), ((), ()))
F32 = jnp.float32
BF16 = jnp.bfloat16
VMEM = pl.BlockSpec(memory_space=pltpu.VMEM)
SMEM = pl.BlockSpec(memory_space=pltpu.SMEM)
PARAMS = pltpu.CompilerParams(vmem_limit_bytes=24 * 1024 * 1024)


def rows_of(ref, k, nang):
    block = ref[k, :, :, :nang]
    return block.reshape(block.shape[0] * block.shape[1], nang)


def angular(dims, first_step, *refs):
    blocks, ygroups, slab, nang, nquad = dims
    if first_step:
        msg_ref, page_ref, basis_ref, out_ref = refs[:4]
        own_ref, here_ref = msg_ref, None
        scaled, pot, radial, coup = refs[4:]
    else:
        msg_ref, page_ref, basis_ref, own_ref, here_ref, out_ref = refs[:6]
        scaled, pot, radial, coup = refs[6:]
    nrad = ygroups * slab
    chan_rows = nang // LANES
    pot[...] = page_ref[:, :, :nquad].reshape(nrad, nquad).astype(F32)
    extra = page_ref[:, :, nquad:].reshape(nrad, LANES).astype(F32)
    factor = jnp.broadcast_to(extra[:, 0:1] + extra[:, 1:2], (nrad, STEP))
    for k in range(blocks):
        page = msg_ref[k, 0, :, nang:].astype(F32)
        coup[k] = jnp.concatenate([page[i : i + 1, :] for i in range(chan_rows)], axis=1)
        kvalue = page[chan_rows : chan_rows + 1, 0:1]
        radial[k] = (-2.0 * kvalue * kvalue) * factor

    @pl.loop(0, nquad // STEP)
    def _(qi):
        cols = pl.ds(pl.multiple_of(qi * STEP, STEP), STEP)
        grid = jnp.dot(
            own_ref[:, :, :, :nang].reshape(blocks * nrad, nang),
            basis_ref[:, cols],
            preferred_element_type=F32,
        )
        prod = grid.reshape(blocks, nrad, STEP) * pot[:, cols][None]
        scaled[:, cols] = prod.astype(BF16).reshape(blocks * nrad, STEP)

    @pl.loop(0, nang // STEP)
    def _(ji):
        cols = pl.ds(pl.multiple_of(ji * STEP, STEP), STEP)
        ang = lax.dot_general(
            scaled[...], basis_ref[cols, :], NT, preferred_element_type=F32
        ).reshape(blocks, nrad, STEP)

        def block(k):
            return own_ref[k, :, :, cols].reshape(nrad, STEP).astype(F32)

        for k in range(blocks):
            here = block(k) if here_ref is None else here_ref[k, :, cols]
            total = ang[k] + radial[k] * here
            if k + 1 < blocks:
                total += coup[k, :, cols] * block(k + 1)
            if k > 0:
                total += coup[k - 1, :, cols] * block(k - 1)
            out_ref[k, :, cols] = total


def finish(dims, rotated, n, *refs):
    blocks, ygroups, groups, slab, nang, nquad, nchan = dims
    last = n == ITERS
    where_ref, page_ref, kin_ref, part_ref, own_ref, got_ref = refs[:6]
    rest = list(refs[6:])
    prev_ref = rest.pop(0) if n > 1 else None
    if last:
        rad_ref, vib_ref, proj_ref, out_ref, final = rest
    else:
        next_ref, full_ref = rest
    core = where_ref[0]
    nrad = ygroups * slab
    every = nrad * groups

    spot = lax.broadcasted_iota(jnp.int32, (every, every), 1)
    slot = spot // nrad
    if rotated:
        slot = lax.rem(slot + core, groups)
    true_at = (lax.rem(spot // slab, ygroups) * groups + slot) * slab + lax.rem(spot, slab)
    pick = (lax.broadcasted_iota(jnp.int32, (every, every), 0) == true_at).astype(BF16)
    lines = [
        kin_ref[pl.ds(pl.multiple_of((y * groups + core) * slab, slab), slab), :]
        for y in range(ygroups)
    ]
    kin_rows = jnp.dot(
        jnp.concatenate(lines, axis=0), pick, preferred_element_type=F32
    ).astype(BF16)

    extra = page_ref[:, :, nquad:].reshape(nrad, LANES).astype(F32)
    damp = jnp.broadcast_to(extra[:, 2:3] + extra[:, 3:4], (nrad, nang))
    for k in range(blocks):
        if rotated:
            pieces = [rows_of(own_ref, k, nang), rows_of(got_ref, k, nang)]
        else:
            pieces = [rows_of(got_ref.at[g], k, nang) for g in range(groups)]
        near = jnp.concatenate(pieces, axis=0)
        total = part_ref[k] + jnp.dot(kin_rows, near, preferred_element_type=F32)
        if n == 1:
            new = damp * total
        else:
            if n == 2:
                before = rows_of(prev_ref, k, nang).astype(F32)
            else:
                before = prev_ref[k]
            new = damp * (2.0 * total - damp * before)
        if last:
            final[k] = new.astype(BF16)
        else:
            full_ref[k] = new
            next_ref[k] = new.astype(BF16).reshape(ygroups, slab, nang)
    if not last:
        return

    span = nchan // ygroups
    rows_at = lax.broadcasted_iota(jnp.int32, (nrad, span), 0)
    rows_at = (rows_at // slab * groups + core) * slab + lax.rem(rows_at, slab)
    for y in range(ygroups):
        chan = pl.ds(y * span, span)
        table = lax.dot_general(
            final[...].reshape(blocks * nrad, nang),
            proj_ref[chan, :],
            NT,
            preferred_element_type=F32,
        ).reshape(blocks, nrad, span)
        hit = (rows_at == rad_ref[:, chan]) & (vib_ref[:, chan] == where_ref[1])
        for k in range(blocks):
            amp = jnp.sum(jnp.where(hit, table[k], 0.0), axis=0, keepdims=True)
            high = amp.astype(BF16).astype(F32)
            low = amp - high
            tile = [part[:, s : s + LANES] for part in (high, low) for s in range(0, span, LANES)]
            if len(tile) < slab:
                tile.append(jnp.zeros((slab - len(tile), LANES), F32))
            out_ref[k, y, :, nang:] = jnp.concatenate(tile, axis=0).astype(BF16)
            out_ref[k, y, :, :nang] = final[k, y * slab : (y + 1) * slab, :]


def two_halves(value):
    high = lax.reduce_precision(value, 8, 7)
    return high.astype(BF16), (value - high).astype(BF16)


def per_device(
    psi_start,
    potential,
    basis,
    kinetic,
    radial_factor,
    damping,
    coupling,
    helicity,
    chan_rad,
    chan_vib,
    projector,
):
    _, slab, nvib, nang = psi_start.shape
    nquad = basis.shape[1]
    nchan = projector.shape[0]
    blocks = lax.axis_size("hel")
    ygroups = lax.axis_size("y")
    groups = lax.axis_size("c")
    hel_index = lax.axis_index("hel")
    y_index = lax.axis_index("y")
    core = lax.axis_index("c")
    swap = [(0, 1), (1, 0)]
    nrad = ygroups * slab
    rotated = groups == 2

    rf_high, rf_low = two_halves(radial_factor)
    dp_high, dp_low = two_halves(damping)
    extra = jnp.stack([rf_high, rf_low, dp_high, dp_low], axis=1)
    extra = jnp.pad(extra, ((0, 0), (0, LANES - extra.shape[1])))
    mine = lax.dynamic_slice_in_dim(potential, hel_index * ygroups, ygroups, 1).astype(BF16)
    pages = jnp.concatenate(
        [jnp.swapaxes(mine, 0, 1), jnp.broadcast_to(extra[None], (ygroups,) + extra.shape)],
        axis=2,
    )
    if ygroups == 2:
        kept = lax.dynamic_index_in_dim(pages, y_index, 0, False)
        got = lax.ppermute(lax.dynamic_index_in_dim(pages, 1 - y_index, 0, False), "y", swap)
        pages = jnp.stack(
            [jnp.where(y_index == 0, kept, got), jnp.where(y_index == 0, got, kept)]
        )
    elif ygroups > 2:
        pages = lax.all_to_all(pages, "y", 0, 0, tiled=True)

    ce = jnp.where(hel_index < blocks - 1, coupling, jnp.zeros_like(coupling))
    chan_rows = nang // LANES
    aux = jnp.concatenate(
        [
            ce.reshape(chan_rows, LANES),
            jnp.broadcast_to(helicity.astype(BF16)[:, None], (1, LANES)),
            jnp.zeros((slab - chan_rows - 1, LANES), BF16),
        ],
        axis=0,
    )
    send = jnp.concatenate(
        [
            jnp.swapaxes(psi_start[0].astype(BF16), 0, 1),
            jnp.broadcast_to(aux[None], (nvib, slab, LANES)),
        ],
        axis=2,
    )
    message = lax.all_to_all(send, ("hel", "y"), 0, 0, tiled=True)
    message = message.reshape(blocks, ygroups, slab, nang + LANES)

    where = jnp.stack([core, hel_index * ygroups + y_index]).astype(jnp.int32)
    flops = 4 * blocks * nrad * nang * nquad
    cost = pl.CostEstimate(flops=flops, bytes_accessed=8 * 1024 * 1024, transcendentals=0)
    own, full = message, None
    before = []
    for n in range(1, ITERS + 1):
        if rotated:
            got = lax.ppermute(own, "c", swap)
        else:
            got = lax.all_gather(own, "c", axis=0, tiled=False)
        extra_in = [] if n == 1 else [own, full]
        part = pl.pallas_call(
            functools.partial(angular, (blocks, ygroups, slab, nang, nquad), n == 1),
            out_shape=jax.ShapeDtypeStruct((blocks, nrad, nang), F32),
            in_specs=[VMEM] * (3 + len(extra_in)),
            out_specs=VMEM,
            scratch_shapes=[
                pltpu.VMEM((blocks * nrad, nquad), BF16),
                pltpu.VMEM((nrad, nquad), F32),
                pltpu.VMEM((blocks, nrad, STEP), F32),
                pltpu.VMEM((blocks, 1, nang), F32),
            ],
            compiler_params=PARAMS,
            cost_estimate=cost,
            name=f"angular{n}",
        )(message, pages, basis, *extra_in)
        operands = [where, pages, kinetic, part, own, got] + before[-1:]
        scratch = []
        if n == ITERS:
            operands += [chan_rad[None], chan_vib[None], projector]
            outs = jax.ShapeDtypeStruct((blocks, ygroups, slab, nang + LANES), BF16)
            scratch = [pltpu.VMEM((blocks, nrad, nang), BF16)]
        else:
            outs = [
                jax.ShapeDtypeStruct((blocks, ygroups, slab, nang), BF16),
                jax.ShapeDtypeStruct((blocks, nrad, nang), F32),
            ]
        before.append(own if n == 1 else full)
        done = pl.pallas_call(
            functools.partial(
                finish, (blocks, ygroups, groups, slab, nang, nquad, nchan), rotated, n
            ),
            out_shape=outs,
            in_specs=[SMEM] + [VMEM] * (len(operands) - 1),
            out_specs=VMEM if n == ITERS else [VMEM, VMEM],
            scratch_shapes=scratch,
            compiler_params=PARAMS,
            name=f"finish{n}",
        )(*operands)
        if n < ITERS:
            own, full = done

    back = done.reshape(blocks * ygroups, slab, nang + LANES)
    home = lax.all_to_all(back, ("hel", "y"), 0, 0, tiled=True)
    psi_final = jnp.swapaxes(home[:, :, :nang], 0, 1).astype(F32)[None]
    span = nchan // ygroups
    pieces = span // LANES
    lines = jnp.sum(home[:, : 2 * pieces, nang:].astype(F32), axis=0)
    shared = (lines[:pieces] + lines[pieces:]).reshape(groups, 1, span // groups)
    amplitude = lax.dynamic_index_in_dim(shared, core, 0, False)
    if rotated:
        amplitude += lax.ppermute(lax.dynamic_index_in_dim(shared, 1 - core, 0, False), "c", swap)
    else:
        amplitude = lax.dynamic_index_in_dim(lax.psum(shared, "c"), core, 0, False)
    return (psi_final, amplitude)


def solution(mesh):
    nhel, nrad = mesh.shape["hel"], mesh.shape["rad"]

    def run(*args):
        nvib = args[0].shape[2]
        groups = nhel * nrad // nvib
        fine = Mesh(mesh.devices.reshape(nhel, nrad // groups, groups), ("hel", "y", "c"))
        rad = ("y", "c")
        placed = (
            P("hel", rad, None, None),
            P(rad, None, None),
            P(),
            P(),
            P(rad),
            P(rad),
            P("hel", None),
            P("hel"),
            P(),
            P(),
            P(),
        )
        return jax.shard_map(
            per_device,
            mesh=fine,
            in_specs=placed,
            out_specs=(P("hel", rad, None, None), P("hel", rad)),
            check_vma=False,
        )(*args)

    return run
```

time: 107 us -> 62.8 us (0.59)
  the two profiles are of different devices: /device:TPU:24 before, /device:TPU:0 now
where the time goes in v2:
time: 62.8 us; the launch traced here: 62.3 us
  waiting for transfers between devices  25.9 us (41%)
  starting transfers between devices  14.1 us (22%)
  Pallas kernels  13.2 us (21%)
  local copies, waits for them, and re-layouts  5.04 us (8%)
  other arithmetic  2.4 us (4%)
  between operations  1.68 us (3%)
    all_to_all x1, waiting for transfers between devices, per_device(): home = lax.all_to_all(back, ('hel', 'y'), 0, 0, tiled=True)  14.4 us
    all_to_all x1, waiting for transfers between devices, per_device(): message = lax.all_to_all(send, ('hel', 'y'), 0, 0, tiled=True)  11.5 us
    pallas_call x3, Pallas kernels, per_device(): pl.pallas_call(functools.partial(angular, (blocks, ygroups, slab, nang, n...  9.07 us
    all_to_all x1, starting transfers between devices, per_device(): message = lax.all_to_all(send, ('hel', 'y'), 0, 0, tiled=True)  7.66 us
    unnamed x22, local copies, waits for them, and re-layouts  4.74 us
    pallas_call x3, Pallas kernels, per_device(): pl.pallas_call(functools.partial(finish, (blocks, ygroups, groups, slab,...  4.18 us
    all_to_all x1, starting transfers between devices, per_device(): home = lax.all_to_all(back, ('hel', 'y'), 0, 0, tiled=True)  3.76 us
    ppermute x1, starting transfers between devices, per_device(): lax.ppermute(lax.dynamic_index_in_dim(pages, 1 - y_index, 0, False), 'y',...  1.98 us
  transfers between devices with their start and end apart: 7, of which 2 were waited for; matrix products, arithmetic and copies ran while one was open for 3% of the time, Pallas kernels for 15%

profile of v2, /device:TPU:0, one launch (start us, length us, event | category | flops | bytes accessed | tf_op | source)
XLA Modules:
  0.0 62.3 jit_solution(15847538147322450578)
XLA Ops:
  0.6 0.0 copy-start
  1.4 0.1 pad.8.clone
  1.5 0.1 pad.9.clone
  1.6 1.6 %copy.32 = bf16[1,16,16,768]{3,1,2,0:T(8,128)(2,1)S(1)} copy(f32[1,16,16,768]{3,2,1,0:T(8,128)} %param.11) | data formatting | bytes 1179648 | tf_op args[0]
  3.2 0.7 %fusion.6 = bf16[768]{0:T(1024)(128)(2,1)S(1)} fusion(bf16[1,768]{1,0:T(2,128)(2,1)} %param.17, pred[]{:T(512)S(6)} %lt.23), kind=kLoop, calls=%fused_computation.20 | loop fusion | flops 768 | bytes 3073 | tf_op jit(solution)/shard_map/jit(_where)/select_n | solution.py:203
  3.9 0.1 maximum_maximum_fusion
  4.0 0.8 %pad_maximum_fusion = bf16[16,16,896]{2,1,0:T(8,128)(2,1)} fusion(bf16[16,16,128]{2,1,0:T(8,128)(2,1)S(1)} %broadcast_in_dim.43, bf16[16,16,768]{2,1,0:T(8,128)(2,1)S(1)} %bitcast.54), kind=kLoop, calls=%fused_computation.2 | loop fusion | flops 917504 | bytes 917504 | tf_op jit(solution)/shard_map/concatenate | solution.py:213
  4.8 7.7 %all-to-all-start = ((bf16[16,16,896]{2,1,0:T(8,128)(2,1)}), bf16[16,16,896]{2,1,0:T(8,128)(2,1)S(1)}, u32[]{:S(2)}, u32[]{:S(2)}) async-start(bf16[16,16,896]{2,1,0:T(8,128)(2,1)} %pad_maximum_fusion), calls=%async_computation | async-start | bytes 917504 | tf_op jit(solution)/shard_map/all_to_all | solution.py:220
  12.5 0.1 constant_dynamic-slice_fusion.2
  12.6 0.1 copy.25
  12.8 2.0 %collective-permute-start = (bf16[16,1664]{1,0:T(8,128)(2,1)S(1)}, bf16[16,1664]{1,0:T(8,128)(2,1)S(1)}, u32[]{:S(2)}, u32[]{:S(2)}) collective-permute-start(bf16[16,1664]{1,0:T(8,128)(2,1)S(1)} %fusion.3), channel_id=1, source_target_pairs={{0,2},{2,0},{1,3},{3,1},{4,6},{6,4},{5,7},{7,5},{8,10},{10,8},{9,1... | collective-permute-start | bytes 159752 | tf_op jit(solution)/shard_map/ppermute | solution.py:196
  14.7 0.1 pad_add_fusion.refs_0_
  14.8 11.5 %all-to-all-done = bf16[16,16,896]{2,1,0:T(8,128)(2,1)S(1)} async-done(((bf16[16,16,896]{2,1,0:T(8,128)(2,1)}), bf16[16,16,896]{2,1,0:T(8,128)(2,1)S(1)}, u32[]{:S(2)}, u32[]{:S(2)}) %all-to-all-start) | async-done | bytes 458784 | tf_op jit(solution)/shard_map/all_to_all | solution.py:220
  26.4 0.0 copy-start.1
  26.4 1.7 %copy-done.1 = bf16[768,1536]{1,0:T(8,128)(2,1)S(1)} copy-done((bf16[768,1536]{1,0:T(8,128)(2,1)S(1)}, bf16[768,1536]{1,0:T(8,128)(2,1)}, u32[]{:S(2)}) %copy-start.1) | copy-done | bytes 2359320
  28.0 3.0 %angular1.1.refs_3_ = f32[8,32,768]{2,1,0:T(8,128)S(1)} custom-call(bf16[8,2,16,896]{3,2,1,0:T(8,128)(2,1)S(1)} %bitcast.47, bf16[2,16,1664]{2,1,0:T(8,128)(2,1)S(1)} %pad_maximum_fusion.1.refs_1_, bf16[768,1536]{1,0:T(8,128)(2,1)S(1)} %copy-done.1), custom_call_target="tpu_custom_call" | custom-call | flops 1207959552 | bytes 8388608 | tf_op jit(solution)/shard_map/angular1/pallas_call | solution.py:234
  31.1 0.9 %finish1.1 = (bf16[8,2,16,768]{3,2,1,0:T(8,128)(2,1)S(1)}, f32[8,32,768]{2,1,0:T(8,128)S(1)}) custom-call(s32[2]{0:T(128)S(1)} %pad_add_fusion.refs_0_, bf16[2,16,1664]{2,1,0:T(8,128)(2,1)S(1)} %pad_maximum_fusion.1.refs_1_, bf16[64,64]{1,0:T(8,128)(2,1)S(1)} %copy-done.4, f32[8,32,768]{2,1,0:T(8,128)S(1)} %angular1.1.refs_3_, ...), custom_call_target="tpu_custom_call" | custom-call | tf_op jit(solution)/shard_map/finish1/pallas_call | solution.py:261
  32.0 0.6 collective-permute-start.2
  32.6 3.0 %angular2.1.refs_3_ = f32[8,32,768]{2,1,0:T(8,128)S(1)} custom-call(bf16[8,2,16,896]{3,2,1,0:T(8,128)(2,1)S(1)} %bitcast.49, bf16[2,16,1664]{2,1,0:T(8,128)(2,1)S(1)} %pad_maximum_fusion.1.refs_1_, bf16[768,1536]{1,0:T(8,128)(2,1)S(1)} %copy-done.2, bf16[8,2,16,768]{3,2,1,0:T(8,128)(2,1)S(1)} %get-tuple-element.6.refs_3_.refs_4_, ...), custom_call_target="tpu_custom_call" | custom-call | flops 1207959552 | bytes 8388608 | tf_op jit(solution)/shard_map/angular2/pallas_call | solution.py:234
  35.6 1.0 %finish2.1 = (bf16[8,2,16,768]{3,2,1,0:T(8,128)(2,1)S(1)}, f32[8,32,768]{2,1,0:T(8,128)S(1)}) custom-call(s32[2]{0:T(128)S(1)} %pad_add_fusion.refs_0_, bf16[2,16,1664]{2,1,0:T(8,128)(2,1)S(1)} %pad_maximum_fusion.1.refs_1_, bf16[64,64]{1,0:T(8,128)(2,1)S(1)} %copy-done.4, f32[8,32,768]{2,1,0:T(8,128)S(1)} %angular2.1.refs_3_, ...), custom_call_target="tpu_custom_call" | custom-call | tf_op jit(solution)/shard_map/finish2/pallas_call | solution.py:261
  36.6 0.1 collective-permute-start.3
  36.7 0.0 copy-start.3
  36.7 0.0 copy-start.5
  36.7 0.0 copy-start.6
  36.7 3.0 %angular3.1.refs_3_ = f32[8,32,768]{2,1,0:T(8,128)S(1)} custom-call(bf16[8,2,16,896]{3,2,1,0:T(8,128)(2,1)S(1)} %bitcast.51, bf16[2,16,1664]{2,1,0:T(8,128)(2,1)S(1)} %pad_maximum_fusion.1.refs_1_, bf16[768,1536]{1,0:T(8,128)(2,1)S(1)} %copy-done.2, bf16[8,2,16,768]{3,2,1,0:T(8,128)(2,1)S(1)} %get-tuple-element.8.refs_3_.refs_4_, ...), custom_call_target="tpu_custom_call" | custom-call | flops 1207959552 | bytes 8388608 | tf_op jit(solution)/shard_map/angular3/pallas_call | solution.py:234
  39.8 2.3 %finish3.1 = bf16[8,2,16,896]{3,2,1,0:T(8,128)(2,1)} custom-call(s32[2]{0:T(128)S(1)} %pad_add_fusion.refs_0_, bf16[2,16,1664]{2,1,0:T(8,128)(2,1)S(1)} %pad_maximum_fusion.1.refs_1_, bf16[64,64]{1,0:T(8,128)(2,1)S(1)} %copy-done.4, f32[8,32,768]{2,1,0:T(8,128)S(1)} %angular3.1.refs_3_, bf16[8,2,16,768]{3,2,1,0:T(8,128)(2,1)S(1)} %get-tuple-element.8.refs_3_.refs_4_, ...), custom_call_target="tpu_custom_call" | custom-call | tf_op jit(solution)/shard_map/finish3/pallas_call | solution.py:261
  42.1 3.8 %all-to-all-start.1 = ((bf16[16,16,896]{2,1,0:T(8,128)(2,1)}), bf16[16,16,896]{2,1,0:T(8,128)(2,1)S(1)}, u32[]{:S(2)}, u32[]{:S(2)}) async-start(bf16[16,16,896]{2,1,0:T(8,128)(2,1)} %bitcast.17), calls=%async_computation.1 | async-start | bytes 917504 | tf_op jit(solution)/shard_map/all_to_all | solution.py:276
  45.9 14.4 %all-to-all-done.1 = bf16[16,16,896]{2,1,0:T(8,128)(2,1)S(1)} async-done(((bf16[16,16,896]{2,1,0:T(8,128)(2,1)}), bf16[16,16,896]{2,1,0:T(8,128)(2,1)S(1)}, u32[]{:S(2)}, u32[]{:S(2)}) %all-to-all-start.1) | async-done | bytes 458784 | tf_op jit(solution)/shard_map/all_to_all | solution.py:276
  60.3 0.1 collective-permute-start.4
  60.4 0.1 convert_bitcast_fusion
  60.4 1.3 %copy.23 = f32[1,16,16,768]{3,2,1,0:T(8,128)} copy(f32[1,16,16,768]{3,1,2,0:T(8,128)S(1)} %convert_bitcast_fusion) | data formatting | bytes 1572864
  61.8 0.6 fusion.8
  (32 shorter events, 0.2 us)
Async XLA Ops:
  0.6 11.8 %copy-start = (f32[16,16,1536]{2,1,0:T(8,128)S(1)}, f32[16,16,1536]{2,1,0:T(8,128)}, u32[]{:S(2)}) copy-start(f32[16,16,1536]{2,1,0:T(8,128)} %param.12) | copy-start | bytes 4718596
  1.6 11.0 %copy-start.7 = (f32[16]{0:T(128)S(1)}, f32[16]{0:T(128)}, u32[]{:S(2)}) copy-start(f32[16]{0:T(128)} %param.15) | copy-start | bytes 196
  1.6 11.0 %copy-start.8 = (f32[16]{0:T(128)S(1)}, f32[16]{0:T(128)}, u32[]{:S(2)}) copy-start(f32[16]{0:T(128)} %param.16) | copy-start | bytes 196
  4.8 21.5 %all-to-all-start = ((bf16[16,16,896]{2,1,0:T(8,128)(2,1)}), bf16[16,16,896]{2,1,0:T(8,128)(2,1)S(1)}, u32[]{:S(2)}, u32[]{:S(2)}) async-start(bf16[16,16,896]{2,1,0:T(8,128)(2,1)} %pad_maximum_fusion), calls=%async_computation | async-start | bytes 917504 | tf_op jit(solution)/shard_map/all_to_all | solution.py:220
  12.8 13.6 %collective-permute-start = (bf16[16,1664]{1,0:T(8,128)(2,1)S(1)}, bf16[16,1664]{1,0:T(8,128)(2,1)S(1)}, u32[]{:S(2)}, u32[]{:S(2)}) collective-permute-start(bf16[16,1664]{1,0:T(8,128)(2,1)S(1)} %fusion.3), channel_id=1, source_target_pairs={{0,2},{2,0},{1,3},{3,1},{4,6},{6,4},{5,7},{7,5},{8,10},{10,8},{9,1... | collective-permute-start | bytes 159752 | tf_op jit(solution)/shard_map/ppermute | solution.py:196
  26.3 4.8 %collective-permute-start.1 = (bf16[8,2,16,896]{3,2,1,0:T(8,128)(2,1)S(1)}, bf16[8,2,16,896]{3,2,1,0:T(8,128)(2,1)S(1)}, u32[]{:S(2)}, u32[]{:S(2)}) collective-permute-start(bf16[8,2,16,896]{3,2,1,0:T(8,128)(2,1)S(1)} %bitcast.46), channel_id=1, source_target_pairs={{0,1},{1,0},{2,3},{3,2},{4,5},{5,4},{6,7},{7,6},{8,9},{9,8},{10,11... | collective-permute-start | bytes 1376264 | tf_op jit(solution)/shard_map/ppermute | solution.py:230
  26.4 1.7 %copy-start.1 = (bf16[768,1536]{1,0:T(8,128)(2,1)S(1)}, bf16[768,1536]{1,0:T(8,128)(2,1)}, u32[]{:S(2)}) copy-start(bf16[768,1536]{1,0:T(8,128)(2,1)} %refs_2_.10) | copy-start | bytes 7077892
  28.0 3.0 %copy-start.4 = (bf16[64,64]{1,0:T(8,128)(2,1)S(1)}, bf16[64,64]{1,0:T(8,128)(2,1)}, u32[]{:S(2)}) copy-start(bf16[64,64]{1,0:T(8,128)(2,1)} %refs_2_.11) | copy-start | bytes 24580
  28.0 4.6 %copy-start.2 = (bf16[768,1536]{1,0:T(8,128)(2,1)S(1)}, bf16[768,1536]{1,0:T(8,128)(2,1)}, u32[]{:S(2)}) copy-start(bf16[768,1536]{1,0:T(8,128)(2,1)} %refs_2_.10) | copy-start | bytes 7077892
  32.0 3.6 %collective-permute-start.2 = (bf16[8,2,16,768]{3,2,1,0:T(8,128)(2,1)S(1)}, bf16[8,2,16,768]{3,2,1,0:T(8,128)(2,1)S(1)}, u32[]{:S(2)}, u32[]{:S(2)}) collective-permute-start(bf16[8,2,16,768]{3,2,1,0:T(8,128)(2,1)S(1)} %get-tuple-element.6.refs_3_.refs_4_), channel_id=1, source_target_pairs={{0,1},{1,0},{2,3},{3,2},{4,5},{5,4},{6,7},{7,6},{8,9},{9,8},{10,11... | collective-permute-start | bytes 1179656 | tf_op jit(solution)/shard_map/ppermute | solution.py:230
  36.6 3.2 %collective-permute-start.3 = (bf16[8,2,16,768]{3,2,1,0:T(8,128)(2,1)S(1)}, bf16[8,2,16,768]{3,2,1,0:T(8,128)(2,1)S(1)}, u32[]{:S(2)}, u32[]{:S(2)}) collective-permute-start(bf16[8,2,16,768]{3,2,1,0:T(8,128)(2,1)S(1)} %get-tuple-element.8.refs_3_.refs_4_), channel_id=1, source_target_pairs={{0,1},{1,0},{2,3},{3,2},{4,5},{5,4},{6,7},{7,6},{8,9},{9,8},{10,11... | collective-permute-start | bytes 1179656 | tf_op jit(solution)/shard_map/ppermute | solution.py:230
  36.7 3.1 %copy-start.3 = (bf16[1024,768]{1,0:T(8,128)(2,1)S(1)}, bf16[1024,768]{1,0:T(8,128)(2,1)}, u32[]{:S(2)}) copy-start(bf16[1024,768]{1,0:T(8,128)(2,1)} %refs_9_.1) | copy-start | bytes 4718596
  36.7 3.1 %copy-start.5 = (s32[1024]{0:T(1024)S(1)}, s32[1024]{0:T(1024)}, u32[]{:S(2)}) copy-start(s32[1024]{0:T(1024)} %param.19) | copy-start | bytes 12292
  36.7 3.1 %copy-start.6 = (s32[1024]{0:T(1024)S(1)}, s32[1024]{0:T(1024)}, u32[]{:S(2)}) copy-start(s32[1024]{0:T(1024)} %param.20) | copy-start | bytes 12292
  42.1 18.1 %all-to-all-start.1 = ((bf16[16,16,896]{2,1,0:T(8,128)(2,1)}), bf16[16,16,896]{2,1,0:T(8,128)(2,1)S(1)}, u32[]{:S(2)}, u32[]{:S(2)}) async-start(bf16[16,16,896]{2,1,0:T(8,128)(2,1)} %bitcast.17), calls=%async_computation.1 | async-start | bytes 917504 | tf_op jit(solution)/shard_map/all_to_all | solution.py:276
  60.3 1.5 %collective-permute-start.4 = (f32[1,256]{1,0:T(1,128)S(1)}, f32[1,256]{1,0:T(1,128)S(1)}, u32[]{:S(2)}, u32[]{:S(2)}) collective-permute-start(f32[1,256]{1,0:T(1,128)S(1)} %fusion.9), channel_id=1, source_target_pairs={{0,1},{1,0},{2,3},{3,2},{4,5},{5,4},{6,7},{7,6},{8,9},{9,8},{10,11... | collective-permute-start | bytes 3080 | tf_op jit(solution)/shard_map/ppermute | solution.py:284

commit v3 on v2

--- a/solution.py
+++ b/solution.py
@@ -15,40 +15,138 @@
 F32 = jnp.float32
 BF16 = jnp.bfloat16
 VMEM = pl.BlockSpec(memory_space=pltpu.VMEM)
+HBM = pl.BlockSpec(memory_space=pltpu.HBM)
 SMEM = pl.BlockSpec(memory_space=pltpu.SMEM)
 PARAMS = pltpu.CompilerParams(vmem_limit_bytes=24 * 1024 * 1024)
 
 
-def rows_of(ref, k, nang):
-    block = ref[k, :, :, :nang]
-    return block.reshape(block.shape[0] * block.shape[1], nang)
+def pack(dims, where_ref, psi_ref, coup_ref, out_ref, wide, ready, in_sems, out_sems):
+    slab, nvib, chan_rows, steps = dims
+    rows = slab * nvib
+    tall = STEP // LANES * slab
+
+    def load(step):
+        cols = pl.ds(step * STEP, STEP)
+        return pltpu.make_async_copy(psi_ref.at[:, cols], wide.at[:, cols], in_sems.at[step])
+
+    def save(step):
+        size = tall if step < steps - 1 else ready.shape[1] - tall * step
+        lines = pl.ds(step * tall, size)
+        return pltpu.make_async_copy(
+            ready.at[:, lines, :], out_ref.at[:, lines, :], out_sems.at[step]
+        )
+
+    for step in range(steps):
+        load(step).start()
+    at = lax.broadcasted_iota(jnp.int32, (rows, rows), 0)
+    source = lax.rem(at, slab) * nvib + at // slab
+    pick = (lax.broadcasted_iota(jnp.int32, (rows, rows), 1) == source).astype(BF16)
+
+    keep = (where_ref[2] > 0).astype(F32)
+    ce = coup_ref[...].astype(F32) * keep
+    lines = [ce[:, i * LANES : (i + 1) * LANES] for i in range(chan_rows)]
+    lines.append(jnp.zeros((1, LANES), F32) + where_ref[3].astype(F32))
+    fill = -(chan_rows + 1) % 8
+    if fill:
+        lines.append(jnp.zeros((fill, LANES), F32))
+    tile = jnp.concatenate(lines, axis=0).astype(BF16)
+    for v in range(nvib):
+        ready[v, chan_rows * slab :, :] = tile
+
+    for step in range(steps):
+        load(step).wait()
+        here = wide[:, step * STEP : (step + 1) * STEP].astype(BF16)
+        moved = jnp.dot(pick, here, preferred_element_type=F32)
+        moved = moved.astype(BF16).reshape(nvib, slab, STEP)
+        for i in range(STEP // LANES):
+            row = step * tall + i * slab
+            ready[:, row : row + slab, :] = moved[:, :, i * LANES : (i + 1) * LANES]
+        save(step).start()
+    for step in range(steps):
+        save(step).wait()
+
+
+def unpack(dims, msg_ref, out_ref, wide, sems):
+    slab, nvib, steps = dims
+    rows = slab * nvib
+    tall = STEP // LANES * slab
+
+    def save(step):
+        cols = pl.ds(step * STEP, STEP)
+        return pltpu.make_async_copy(wide.at[:, cols], out_ref.at[:, cols], sems.at[step])
+
+    at = lax.broadcasted_iota(jnp.int32, (rows, rows), 0)
+    source = lax.rem(at, nvib) * slab + at // nvib
+    pick = (lax.broadcasted_iota(jnp.int32, (rows, rows), 1) == source).astype(BF16)
+    for step in range(steps):
+        parts = [
+            msg_ref[:, row : row + slab, :].reshape(rows, LANES)
+            for row in range(step * tall, (step + 1) * tall, slab)
+        ]
+        wide[:, step * STEP : (step + 1) * STEP] = jnp.dot(
+            pick, jnp.concatenate(parts, axis=1), preferred_element_type=F32
+        )
+        save(step).start()
+    for step in range(steps):
+        save(step).wait()
+
+
+def rows_of(ref, k):
+    block = ref[k]
+    return block.reshape(block.shape[0] * block.shape[1], block.shape[2])
+
+
+def rows_in(ref, k, slab, nang):
+    return jnp.concatenate(
+        [
+            jnp.concatenate(
+                [ref[k, y, i * slab : (i + 1) * slab, :] for i in range(nang // LANES)], axis=1
+            )
+            for y in range(ref.shape[1])
+        ],
+        axis=0,
+    )
 
 
 def angular(dims, first_step, *refs):
     blocks, ygroups, slab, nang, nquad = dims
+    msg_ref, page_ref, basis_ref = refs[:3]
     if first_step:
-        msg_ref, page_ref, basis_ref, out_ref = refs[:4]
-        own_ref, here_ref = msg_ref, None
-        scaled, pot, radial, coup = refs[4:]
+        out_ref, own_ref, held = refs[3:6]
+        here_ref = None
+        scaled, pot, radial, coup, sems = refs[6:]
+        basis_hbm, basis_ref = basis_ref, held
+
+        def load(qi):
+            cols = pl.ds(qi * STEP, STEP)
+            return pltpu.make_async_copy(basis_hbm.at[:, cols], held.at[:, cols], sems.at[qi])
+
+        for qi in range(nquad // STEP):
+            load(qi).start()
     else:
-        msg_ref, page_ref, basis_ref, own_ref, here_ref, out_ref = refs[:6]
+        own_ref, here_ref, out_ref = refs[3:6]
         scaled, pot, radial, coup = refs[6:]
     nrad = ygroups * slab
     chan_rows = nang // LANES
+    base = chan_rows * slab
     pot[...] = page_ref[:, :, :nquad].reshape(nrad, nquad).astype(F32)
     extra = page_ref[:, :, nquad:].reshape(nrad, LANES).astype(F32)
     factor = jnp.broadcast_to(extra[:, 0:1] + extra[:, 1:2], (nrad, STEP))
     for k in range(blocks):
-        page = msg_ref[k, 0, :, nang:].astype(F32)
+        page = msg_ref[k, 0, base : base + -(-(chan_rows + 1) // 8) * 8, :].astype(F32)
         coup[k] = jnp.concatenate([page[i : i + 1, :] for i in range(chan_rows)], axis=1)
         kvalue = page[chan_rows : chan_rows + 1, 0:1]
         radial[k] = (-2.0 * kvalue * kvalue) * factor
+        if first_step:
+            own_ref[k] = rows_in(msg_ref, k, slab, nang).reshape(ygroups, slab, nang)
 
     @pl.loop(0, nquad // STEP)
     def _(qi):
         cols = pl.ds(pl.multiple_of(qi * STEP, STEP), STEP)
+        if first_step:
+            pltpu.make_async_copy(basis_hbm.at[:, cols], held.at[:, cols], sems.at[qi]).wait()
         grid = jnp.dot(
-            own_ref[:, :, :, :nang].reshape(blocks * nrad, nang),
+            own_ref[...].reshape(blocks * nrad, nang),
             basis_ref[:, cols],
             preferred_element_type=F32,
         )
@@ -103,20 +201,23 @@
         jnp.concatenate(lines, axis=0), pick, preferred_element_type=F32
     ).astype(BF16)
 
+    def other(ref, k):
+        return rows_in(ref, k, slab, nang) if n == 1 else rows_of(ref, k)
+
     extra = page_ref[:, :, nquad:].reshape(nrad, LANES).astype(F32)
     damp = jnp.broadcast_to(extra[:, 2:3] + extra[:, 3:4], (nrad, nang))
     for k in range(blocks):
         if rotated:
-            pieces = [rows_of(own_ref, k, nang), rows_of(got_ref, k, nang)]
+            pieces = [rows_of(own_ref, k), other(got_ref, k)]
         else:
-            pieces = [rows_of(got_ref.at[g], k, nang) for g in range(groups)]
+            pieces = [other(got_ref.at[g], k) for g in range(groups)]
         near = jnp.concatenate(pieces, axis=0)
         total = part_ref[k] + jnp.dot(kin_rows, near, preferred_element_type=F32)
         if n == 1:
             new = damp * total
         else:
             if n == 2:
-                before = rows_of(prev_ref, k, nang).astype(F32)
+                before = rows_of(prev_ref, k).astype(F32)
             else:
                 before = prev_ref[k]
             new = damp * (2.0 * total - damp * before)
@@ -129,6 +230,8 @@
         return
 
     span = nchan // ygroups
+    height = 2 * (span // LANES)
+    base = nang // LANES * slab
     rows_at = lax.broadcasted_iota(jnp.int32, (nrad, span), 0)
     rows_at = (rows_at // slab * groups + core) * slab + lax.rem(rows_at, slab)
     for y in range(ygroups):
@@ -145,10 +248,15 @@
             high = amp.astype(BF16).astype(F32)
             low = amp - high
             tile = [part[:, s : s + LANES] for part in (high, low) for s in range(0, span, LANES)]
-            if len(tile) < slab:
-                tile.append(jnp.zeros((slab - len(tile), LANES), F32))
-            out_ref[k, y, :, nang:] = jnp.concatenate(tile, axis=0).astype(BF16)
-            out_ref[k, y, :, :nang] = final[k, y * slab : (y + 1) * slab, :]
+            out_ref[k, y, base : base + height, :] = jnp.concatenate(tile, axis=0).astype(BF16)
+            for i in range(nang // LANES):
+                out_ref[k, y, i * slab : (i + 1) * slab, :] = final[
+                    k, y * slab : (y + 1) * slab, i * LANES : (i + 1) * LANES
+                ]
+
+
+def in_hbm(array):
+    return pltpu.with_memory_space_constraint(array, pltpu.HBM)
 
 
 def two_halves(value):
@@ -200,63 +308,76 @@
     elif ygroups > 2:
         pages = lax.all_to_all(pages, "y", 0, 0, tiled=True)
 
-    ce = jnp.where(hel_index < blocks - 1, coupling, jnp.zeros_like(coupling))
     chan_rows = nang // LANES
-    aux = jnp.concatenate(
+    base = chan_rows * slab
+    where = jnp.stack(
         [
-            ce.reshape(chan_rows, LANES),
-            jnp.broadcast_to(helicity.astype(BF16)[:, None], (1, LANES)),
-            jnp.zeros((slab - chan_rows - 1, LANES), BF16),
+            core,
+            hel_index * ygroups + y_index,
+            (hel_index < blocks - 1).astype(jnp.int32),
+            helicity[0],
+        ]
+    ).astype(jnp.int32)
+    steps = nang // STEP
+    height = base + -(-(chan_rows + 1) // 8) * 8
+    send = pl.pallas_call(
+        functools.partial(pack, (slab, nvib, chan_rows, steps)),
+        out_shape=jax.ShapeDtypeStruct((nvib, height, LANES), BF16),
+        in_specs=[SMEM, HBM, VMEM],
+        out_specs=HBM,
+        scratch_shapes=[
+            pltpu.VMEM((slab * nvib, nang), F32),
+            pltpu.VMEM((nvib, height, LANES), BF16),
+            pltpu.SemaphoreType.DMA((steps,)),
+            pltpu.SemaphoreType.DMA((steps,)),
         ],
-        axis=0,
-    )
-    send = jnp.concatenate(
-        [
-            jnp.swapaxes(psi_start[0].astype(BF16), 0, 1),
-            jnp.broadcast_to(aux[None], (nvib, slab, LANES)),
-        ],
-        axis=2,
-    )
+        compiler_params=PARAMS,
+        name="pack",
+    )(where, in_hbm(psi_start.reshape(slab * nvib, nang)), coupling)
     message = lax.all_to_all(send, ("hel", "y"), 0, 0, tiled=True)
-    message = message.reshape(blocks, ygroups, slab, nang + LANES)
-
-    where = jnp.stack([core, hel_index * ygroups + y_index]).astype(jnp.int32)
+    message = message.reshape(blocks, ygroups, height, LANES)
+    basis = in_hbm(basis)
     flops = 4 * blocks * nrad * nang * nquad
     cost = pl.CostEstimate(flops=flops, bytes_accessed=8 * 1024 * 1024, transcendentals=0)
-    own, full = message, None
+    sent, own, full = message, None, None
+    out_height = base + 2 * (nchan // ygroups // LANES)
+    block_type = jax.ShapeDtypeStruct((blocks, ygroups, slab, nang), BF16)
+    full_type = jax.ShapeDtypeStruct((blocks, nrad, nang), F32)
+    held = [pltpu.SemaphoreType.DMA((nquad // STEP,))]
+    basis_type = jax.ShapeDtypeStruct(basis.shape, basis.dtype)
     before = []
     for n in range(1, ITERS + 1):
         if rotated:
-            got = lax.ppermute(own, "c", swap)
+            got = lax.ppermute(sent, "c", swap)
         else:
-            got = lax.all_gather(own, "c", axis=0, tiled=False)
+            got = lax.all_gather(sent, "c", axis=0, tiled=False)
         extra_in = [] if n == 1 else [own, full]
         part = pl.pallas_call(
             functools.partial(angular, (blocks, ygroups, slab, nang, nquad), n == 1),
-            out_shape=jax.ShapeDtypeStruct((blocks, nrad, nang), F32),
-            in_specs=[VMEM] * (3 + len(extra_in)),
-            out_specs=VMEM,
+            out_shape=[full_type, block_type, basis_type] if n == 1 else full_type,
+            in_specs=[VMEM, VMEM, HBM if n == 1 else VMEM] + [VMEM] * len(extra_in),
+            out_specs=[VMEM] * 3 if n == 1 else VMEM,
             scratch_shapes=[
                 pltpu.VMEM((blocks * nrad, nquad), BF16),
                 pltpu.VMEM((nrad, nquad), F32),
                 pltpu.VMEM((blocks, nrad, STEP), F32),
                 pltpu.VMEM((blocks, 1, nang), F32),
-            ],
+            ]
+            + held * (n == 1),
             compiler_params=PARAMS,
             cost_estimate=cost,
             name=f"angular{n}",
         )(message, pages, basis, *extra_in)
+        if n == 1:
+            part, own, basis = part
         operands = [where, pages, kinetic, part, own, got] + before[-1:]
         scratch = []
         if n == ITERS:
             operands += [chan_rad[None], chan_vib[None], projector]
-            outs = jax.ShapeDtypeStruct((blocks, ygroups, slab, nang + LANES), BF16)
+            outs = jax.ShapeDtypeStruct((blocks, ygroups, out_height, LANES), BF16)
             scratch = [pltpu.VMEM((blocks, nrad, nang), BF16)]
         else:
-            outs = [
-                jax.ShapeDtypeStruct((blocks, ygroups, slab, nang), BF16),
-                jax.ShapeDtypeStruct((blocks, nrad, nang), F32),
-            ]
+            outs = [block_type, full_type]
         before.append(own if n == 1 else full)
         done = pl.pallas_call(
             functools.partial(
@@ -271,20 +392,32 @@
         )(*operands)
         if n < ITERS:
             own, full = done
-
-    back = done.reshape(blocks * ygroups, slab, nang + LANES)
+            sent = own
+
+    back = done.reshape(blocks * ygroups, out_height, LANES)
     home = lax.all_to_all(back, ("hel", "y"), 0, 0, tiled=True)
-    psi_final = jnp.swapaxes(home[:, :, :nang], 0, 1).astype(F32)[None]
     span = nchan // ygroups
     pieces = span // LANES
-    lines = jnp.sum(home[:, : 2 * pieces, nang:].astype(F32), axis=0)
+    lines = jnp.sum(home[:, base:, :].astype(F32), axis=0)
     shared = (lines[:pieces] + lines[pieces:]).reshape(groups, 1, span // groups)
     amplitude = lax.dynamic_index_in_dim(shared, core, 0, False)
     if rotated:
         amplitude += lax.ppermute(lax.dynamic_index_in_dim(shared, 1 - core, 0, False), "c", swap)
     else:
         amplitude = lax.dynamic_index_in_dim(lax.psum(shared, "c"), core, 0, False)
-    return (psi_final, amplitude)
+    psi_final = pl.pallas_call(
+        functools.partial(unpack, (slab, nvib, steps)),
+        out_shape=jax.ShapeDtypeStruct((slab * nvib, nang), F32),
+        in_specs=[VMEM],
+        out_specs=HBM,
+        scratch_shapes=[
+            pltpu.VMEM((slab * nvib, nang), F32),
+            pltpu.SemaphoreType.DMA((steps,)),
+        ],
+        compiler_params=PARAMS,
+        name="unpack",
+    )(home)
+    return (psi_final.reshape(1, slab, nvib, nang), amplitude)
 
 
 def solution(mesh):

time: 62.8 us -> 61.5 us (0.979)
  Pallas kernels: 13.2 us -> 18.2 us
  local copies, waits for them, and re-layouts: 5.04 us -> 0.96 us
  other arithmetic: 2.4 us -> 0.74 us
  waiting for transfers between devices: 25.9 us -> 24.8 us
  starting transfers between devices: 14.1 us -> 14.8 us
    pallas_call x0 -> x2, Pallas kernels: none -> 3.93 us  [the longest x1 2.83 us: per_device(): pl.pallas_call(functools.partial(pack, (slab, nvib, chan_rows, steps)), o...]
    unnamed x22 -> x18, local copies, waits for them, and re-layouts: 4.74 us -> 0.83 us
    pallas_call x3, Pallas kernels: 9.07 us -> 10 us  [per_device(): pl.pallas_call(functools.partial(angular, (blocks, ygroups, slab, nang, n...]
    concatenate x2 -> x0, other arithmetic: 0.88 us -> none  [the longest x1 0.8 us: per_device(): jnp.concatenate([jnp.swapaxes(psi_start[0].astype(BF16), 0, 1), jnp.broad...]
    select_n x1 -> x0, other arithmetic: 0.71 us -> none  [per_device(): ce = jnp.where(hel_index < blocks - 1, coupling, jnp.zeros_like(coupling))]
    all_to_all x1, starting transfers between devices: 7.66 us -> 8.36 us  [per_device(): message = lax.all_to_all(send, ('hel', 'y'), 0, 0, tiled=True)]
  transfers between devices with their start and end apart: 7 -> 7, of which waited for: 2 -> 2; matrix products, arithmetic and copies ran while one was open for 3% -> 0% of each run, Pallas kernels for 15% -> 18%
where the time goes in v3:
time: 61.5 us; the launch traced here: 61.1 us
  waiting for transfers between devices  24.8 us (40%)
  Pallas kernels  18.2 us (30%)
  starting transfers between devices  14.8 us (24%)
  between operations  1.66 us (3%)
  local copies, waits for them, and re-layouts  0.96 us (2%)
  other arithmetic  0.74 us (1%)
    all_to_all x1, waiting for transfers between devices, per_device(): home = lax.all_to_all(back, ('hel', 'y'), 0, 0, tiled=True)  13.8 us
    all_to_all x1, waiting for transfers between devices, per_device(): message = lax.all_to_all(send, ('hel', 'y'), 0, 0, tiled=True)  10.9 us
    pallas_call x3, Pallas kernels, per_device(): pl.pallas_call(functools.partial(angular, (blocks, ygroups, slab, nang, n...  10 us
    all_to_all x1, starting transfers between devices, per_device(): message = lax.all_to_all(send, ('hel', 'y'), 0, 0, tiled=True)  8.36 us
    pallas_call x3, Pallas kernels, per_device(): pl.pallas_call(functools.partial(finish, (blocks, ygroups, groups, slab,...  4.23 us
    all_to_all x1, starting transfers between devices, per_device(): home = lax.all_to_all(back, ('hel', 'y'), 0, 0, tiled=True)  3.7 us
    pallas_call x1, Pallas kernels, per_device(): pl.pallas_call(functools.partial(pack, (slab, nvib, chan_rows, steps)), o...  2.83 us
    ppermute x1, starting transfers between devices, per_device(): lax.ppermute(lax.dynamic_index_in_dim(pages, 1 - y_index, 0, False), 'y',...  1.99 us
  transfers between devices with their start and end apart: 7, of which 2 were waited for; matrix products, arithmetic and copies ran while one was open for 0% of the time, Pallas kernels for 18%

profile of v3, /device:TPU:0, one launch (start us, length us, event | category | flops | bytes accessed | tf_op | source)
XLA Modules:
  0.0 61.1 jit_solution(17341721192731928330)
XLA Ops:
  0.6 0.0 copy-start
  1.4 0.1 pad_add_fusion.where_ref.refs_0_
  1.5 0.7 %copy-done.5 = bf16[1,768]{1,0:T(2,128)(2,1)S(1)} copy-done((bf16[1,768]{1,0:T(2,128)(2,1)S(1)}, bf16[1,768]{1,0:T(2,128)(2,1)}, u32[]{:S(2)}) %copy-start.5) | copy-done | bytes 1560
  2.2 2.8 %pack.1 = bf16[16,104,128]{2,1,0:T(8,128)(2,1)} custom-call(s32[4]{0:T(128)S(1)} %pad_add_fusion.where_ref.refs_0_, f32[256,768]{1,0:T(8,128)} %bitcast.46, bf16[1,768]{1,0:T(2,128)(2,1)S(1)} %copy-done.5), custom_call_target="tpu_custom_call" | custom-call | tf_op jit(solution)/shard_map/pack/pallas_call | solution.py:323
  5.0 8.4 %all-to-all-start = ((bf16[16,104,128]{2,1,0:T(8,128)(2,1)}), bf16[16,104,128]{2,1,0:T(8,128)(2,1)S(1)}, u32[]{:S(2)}, u32[]{:S(2)}) async-start(bf16[16,104,128]{2,1,0:T(8,128)(2,1)} %pack.1), calls=%async_computation | async-start | bytes 851968 | tf_op jit(solution)/shard_map/all_to_all | solution.py:337
  13.4 0.1 constant_dynamic-slice_fusion.2
  13.5 0.0 copy-done.6
  13.5 0.0 copy-done.7
  13.6 0.1 copy.17
  13.7 2.0 %collective-permute-start = (bf16[16,1664]{1,0:T(8,128)(2,1)S(1)}, bf16[16,1664]{1,0:T(8,128)(2,1)S(1)}, u32[]{:S(2)}, u32[]{:S(2)}) collective-permute-start(bf16[16,1664]{1,0:T(8,128)(2,1)S(1)} %fusion.2), channel_id=1, source_target_pairs={{0,2},{2,0},{1,3},{3,1},{4,6},{6,4},{5,7},{7,5},{8,10},{10,8},{9,1... | collective-permute-start | bytes 159752 | tf_op jit(solution)/shard_map/ppermute | solution.py:304
  15.7 10.9 %all-to-all-done = bf16[16,104,128]{2,1,0:T(8,128)(2,1)S(1)} async-done(((bf16[16,104,128]{2,1,0:T(8,128)(2,1)}), bf16[16,104,128]{2,1,0:T(8,128)(2,1)S(1)}, u32[]{:S(2)}, u32[]{:S(2)}) %all-to-all-start) | async-done | bytes 426016 | tf_op jit(solution)/shard_map/all_to_all | solution.py:337
  26.6 0.0 collective-permute-start.1
  26.6 0.0 collective-permute-done
  26.7 0.0 copy-start.2
  26.7 3.9 %angular1.1 = (f32[8,32,768]{2,1,0:T(8,128)S(1)}, bf16[8,2,16,768]{3,2,1,0:T(8,128)(2,1)S(1)}, bf16[768,1536]{1,0:T(8,128)(2,1)S(1)}) custom-call(bf16[8,2,104,128]{3,2,1,0:T(8,128)(2,1)S(1)} %bitcast.39, bf16[2,16,1664]{2,1,0:T(8,128)(2,1)S(1)} %pad_maximum_fusion.refs_1_, bf16[768,1536]{1,0:T(8,128)(2,1)} %refs_2_.4), custom_call_target="tpu_custom_call" | custom-call | flops 1207959552 | bytes 8388608 | tf_op jit(solution)/shard_map/angular1/pallas_call | solution.py:355
  30.7 0.0 collective-permute-done.1.refs_5_
  30.7 0.0 copy-done.2
  30.7 0.9 %finish1.1 = (bf16[8,2,16,768]{3,2,1,0:T(8,128)(2,1)S(1)}, f32[8,32,768]{2,1,0:T(8,128)S(1)}) custom-call(s32[4]{0:T(128)S(1)} %pad_add_fusion.where_ref.refs_0_, bf16[2,16,1664]{2,1,0:T(8,128)(2,1)S(1)} %pad_maximum_fusion.refs_1_, bf16[64,64]{1,0:T(8,128)(2,1)S(1)} %copy-done.2, f32[8,32,768]{2,1,0:T(8,128)S(1)} %get-tuple-element.10.refs_3_, ...), custom_call_target="tpu_custom_call" | custom-call | tf_op jit(solution)/shard_map/finish1/pallas_call | solution.py:382
  31.6 0.6 collective-permute-start.2
  32.2 3.0 %angular2.1.refs_3_ = f32[8,32,768]{2,1,0:T(8,128)S(1)} custom-call(bf16[8,2,104,128]{3,2,1,0:T(8,128)(2,1)S(1)} %bitcast.40, bf16[2,16,1664]{2,1,0:T(8,128)(2,1)S(1)} %pad_maximum_fusion.refs_1_, bf16[768,1536]{1,0:T(8,128)(2,1)S(1)} %get-tuple-element.9.refs_2_, bf16[8,2,16,768]{3,2,1,0:T(8,128)(2,1)S(1)} %get-tuple-element.12.refs_3_.refs_4_, ...), custom_call_target="tpu_custom_call" | custom-call | flops 1207959552 | bytes 8388608 | tf_op jit(solution)/shard_map/angular2/pallas_call | solution.py:355
  35.2 0.0 collective-permute-done.2.refs_5_
  35.2 1.0 %finish2.1 = (bf16[8,2,16,768]{3,2,1,0:T(8,128)(2,1)S(1)}, f32[8,32,768]{2,1,0:T(8,128)S(1)}) custom-call(s32[4]{0:T(128)S(1)} %pad_add_fusion.where_ref.refs_0_, bf16[2,16,1664]{2,1,0:T(8,128)(2,1)S(1)} %pad_maximum_fusion.refs_1_, bf16[64,64]{1,0:T(8,128)(2,1)S(1)} %copy-done.2, f32[8,32,768]{2,1,0:T(8,128)S(1)} %angular2.1.refs_3_, ...), custom_call_target="tpu_custom_call" | custom-call | tf_op jit(solution)/shard_map/finish2/pallas_call | solution.py:382
  36.2 0.1 collective-permute-start.3
  36.3 3.0 %angular3.1.refs_3_ = f32[8,32,768]{2,1,0:T(8,128)S(1)} custom-call(bf16[8,2,104,128]{3,2,1,0:T(8,128)(2,1)S(1)} %bitcast.41, bf16[2,16,1664]{2,1,0:T(8,128)(2,1)S(1)} %pad_maximum_fusion.refs_1_, bf16[768,1536]{1,0:T(8,128)(2,1)S(1)} %get-tuple-element.9.refs_2_, bf16[8,2,16,768]{3,2,1,0:T(8,128)(2,1)S(1)} %get-tuple-element.14.refs_3_.refs_4_, ...), custom_call_target="tpu_custom_call" | custom-call | flops 1207959552 | bytes 8388608 | tf_op jit(solution)/shard_map/angular3/pallas_call | solution.py:355
  39.4 0.0 collective-permute-done.3.refs_5_
  39.4 2.3 %finish3.1 = bf16[8,2,104,128]{3,2,1,0:T(8,128)(2,1)} custom-call(s32[4]{0:T(128)S(1)} %pad_add_fusion.where_ref.refs_0_, bf16[2,16,1664]{2,1,0:T(8,128)(2,1)S(1)} %pad_maximum_fusion.refs_1_, bf16[64,64]{1,0:T(8,128)(2,1)S(1)} %copy-done.2, f32[8,32,768]{2,1,0:T(8,128)S(1)} %angular3.1.refs_3_, ...), custom_call_target="tpu_custom_call" | custom-call | tf_op jit(solution)/shard_map/finish3/pallas_call | solution.py:382
  41.7 3.7 %all-to-all-start.1 = ((bf16[16,104,128]{2,1,0:T(8,128)(2,1)}), bf16[16,104,128]{2,1,0:T(8,128)(2,1)S(1)}, u32[]{:S(2)}, u32[]{:S(2)}) async-start(bf16[16,104,128]{2,1,0:T(8,128)(2,1)} %bitcast.16), calls=%async_computation.1 | async-start | bytes 851968 | tf_op jit(solution)/shard_map/all_to_all | solution.py:398
  45.4 13.8 %all-to-all-done.1.msg_ref = bf16[16,104,128]{2,1,0:T(8,128)(2,1)S(1)} async-done(((bf16[16,104,128]{2,1,0:T(8,128)(2,1)}), bf16[16,104,128]{2,1,0:T(8,128)(2,1)S(1)}, u32[]{:S(2)}, u32[]{:S(2)}) %all-to-all-start.1) | async-done | bytes 426016 | tf_op jit(solution)/shard_map/all_to_all | solution.py:398
  59.3 0.1 collective-permute-start.4
  59.4 1.1 %unpack.1 = f32[256,768]{1,0:T(8,128)} custom-call(bf16[16,104,128]{2,1,0:T(8,128)(2,1)S(1)} %all-to-all-done.1.msg_ref), custom_call_target="tpu_custom_call" | custom-call | tf_op jit(solution)/shard_map/unpack/pallas_call | solution.py:408
  60.5 0.0 collective-permute-done.4
  60.5 0.6 fusion.6
  (22 shorter events, 0.2 us)
Async XLA Ops:
  0.6 12.8 %copy-start = (f32[16,16,1536]{2,1,0:T(8,128)S(1)}, f32[16,16,1536]{2,1,0:T(8,128)}, u32[]{:S(2)}) copy-start(f32[16,16,1536]{2,1,0:T(8,128)} %param.12) | copy-start | bytes 4718596
  0.6 12.9 %copy-start.6 = (f32[16]{0:T(128)S(1)}, f32[16]{0:T(128)}, u32[]{:S(2)}) copy-start(f32[16]{0:T(128)} %param.15) | copy-start | bytes 196
  0.7 12.9 %copy-start.7 = (f32[16]{0:T(128)S(1)}, f32[16]{0:T(128)}, u32[]{:S(2)}) copy-start(f32[16]{0:T(128)} %param.16) | copy-start | bytes 196
  1.5 0.7 %copy-start.5 = (bf16[1,768]{1,0:T(2,128)(2,1)S(1)}, bf16[1,768]{1,0:T(2,128)(2,1)}, u32[]{:S(2)}) copy-start(bf16[1,768]{1,0:T(2,128)(2,1)} %coup_ref.1) | copy-start | bytes 4612
  5.0 21.6 %all-to-all-start = ((bf16[16,104,128]{2,1,0:T(8,128)(2,1)}), bf16[16,104,128]{2,1,0:T(8,128)(2,1)S(1)}, u32[]{:S(2)}, u32[]{:S(2)}) async-start(bf16[16,104,128]{2,1,0:T(8,128)(2,1)} %pack.1), calls=%async_computation | async-start | bytes 851968 | tf_op jit(solution)/shard_map/all_to_all | solution.py:337
  13.7 12.9 %collective-permute-start = (bf16[16,1664]{1,0:T(8,128)(2,1)S(1)}, bf16[16,1664]{1,0:T(8,128)(2,1)S(1)}, u32[]{:S(2)}, u32[]{:S(2)}) collective-permute-start(bf16[16,1664]{1,0:T(8,128)(2,1)S(1)} %fusion.2), channel_id=1, source_target_pairs={{0,2},{2,0},{1,3},{3,1},{4,6},{6,4},{5,7},{7,5},{8,10},{10,8},{9,1... | collective-permute-start | bytes 159752 | tf_op jit(solution)/shard_map/ppermute | solution.py:304
  26.6 4.0 %collective-permute-start.1 = (bf16[8,2,104,128]{3,2,1,0:T(8,128)(2,1)S(1)}, bf16[8,2,104,128]{3,2,1,0:T(8,128)(2,1)S(1)}, u32[]{:S(2)}, u32[]{:S(2)}) collective-permute-start(bf16[8,2,104,128]{3,2,1,0:T(8,128)(2,1)S(1)} %bitcast.38), channel_id=1, source_target_pairs={{0,1},{1,0},{2,3},{3,2},{4,5},{5,4},{6,7},{7,6},{8,9},{9,8},{10,11... | collective-permute-start | bytes 1277960 | tf_op jit(solution)/shard_map/ppermute | solution.py:351
  26.7 4.0 %copy-start.2 = (bf16[64,64]{1,0:T(8,128)(2,1)S(1)}, bf16[64,64]{1,0:T(8,128)(2,1)}, u32[]{:S(2)}) copy-start(bf16[64,64]{1,0:T(8,128)(2,1)} %refs_2_.7) | copy-start | bytes 24580
  31.6 3.6 %collective-permute-start.2 = (bf16[8,2,16,768]{3,2,1,0:T(8,128)(2,1)S(1)}, bf16[8,2,16,768]{3,2,1,0:T(8,128)(2,1)S(1)}, u32[]{:S(2)}, u32[]{:S(2)}) collective-permute-start(bf16[8,2,16,768]{3,2,1,0:T(8,128)(2,1)S(1)} %get-tuple-element.12.refs_3_.refs_4_), channel_id=1, source_target_pairs={{0,1},{1,0},{2,3},{3,2},{4,5},{5,4},{6,7},{7,6},{8,9},{9,8},{10,11... | collective-permute-start | bytes 1179656 | tf_op jit(solution)/shard_map/ppermute | solution.py:351
  36.2 3.2 %collective-permute-start.3 = (bf16[8,2,16,768]{3,2,1,0:T(8,128)(2,1)S(1)}, bf16[8,2,16,768]{3,2,1,0:T(8,128)(2,1)S(1)}, u32[]{:S(2)}, u32[]{:S(2)}) collective-permute-start(bf16[8,2,16,768]{3,2,1,0:T(8,128)(2,1)S(1)} %get-tuple-element.14.refs_3_.refs_4_), channel_id=1, source_target_pairs={{0,1},{1,0},{2,3},{3,2},{4,5},{5,4},{6,7},{7,6},{8,9},{9,8},{10,11... | collective-permute-start | bytes 1179656 | tf_op jit(solution)/shard_map/ppermute | solution.py:351
  36.3 3.1 %copy-start.1 = (bf16[1024,768]{1,0:T(8,128)(2,1)S(1)}, bf16[1024,768]{1,0:T(8,128)(2,1)}, u32[]{:S(2)}) copy-start(bf16[1024,768]{1,0:T(8,128)(2,1)} %refs_9_.1) | copy-start | bytes 4718596
  36.3 3.1 %copy-start.3 = (s32[1024]{0:T(1024)S(1)}, s32[1024]{0:T(1024)}, u32[]{:S(2)}) copy-start(s32[1024]{0:T(1024)} %param.19) | copy-start | bytes 12292
  36.3 3.1 %copy-start.4 = (s32[1024]{0:T(1024)S(1)}, s32[1024]{0:T(1024)}, u32[]{:S(2)}) copy-start(s32[1024]{0:T(1024)} %param.20) | copy-start | bytes 12292
  41.7 17.5 %all-to-all-start.1 = ((bf16[16,104,128]{2,1,0:T(8,128)(2,1)}), bf16[16,104,128]{2,1,0:T(8,128)(2,1)S(1)}, u32[]{:S(2)}, u32[]{:S(2)}) async-start(bf16[16,104,128]{2,1,0:T(8,128)(2,1)} %bitcast.16), calls=%async_computation.1 | async-start | bytes 851968 | tf_op jit(solution)/shard_map/all_to_all | solution.py:398
  59.3 1.2 %collective-permute-start.4 = (f32[1,256]{1,0:T(1,128)S(1)}, f32[1,256]{1,0:T(1,128)S(1)}, u32[]{:S(2)}, u32[]{:S(2)}) collective-permute-start(f32[1,256]{1,0:T(1,128)S(1)} %fusion.7), channel_id=1, source_target_pairs={{0,1},{1,0},{2,3},{3,2},{4,5},{5,4},{6,7},{7,6},{8,9},{9,8},{10,11... | collective-permute-start | bytes 3080 | tf_op jit(solution)/shard_map/ppermute | solution.py:405

commit v4 on v0

v4 whole, which is shorter than its diff:
```python
import functools

import jax
import jax.numpy as jnp
from jax import lax
from jax.experimental import pallas as pl
from jax.experimental.pallas import tpu as pltpu
from jax.sharding import Mesh
from jax.sharding import PartitionSpec as P

ITERS = 3
LANES = 128
STEP = 256
WIDE = 384
SMALL = 8
NT = (((1,), (1,)), ((), ()))
F32 = jnp.float32
BF16 = jnp.bfloat16
VMEM = pl.BlockSpec(memory_space=pltpu.VMEM)
HBM = pl.BlockSpec(memory_space=pltpu.HBM)
PARAMS = pltpu.CompilerParams(vmem_limit_bytes=24 * 1024 * 1024)


def in_hbm(array):
    return pltpu.with_memory_space_constraint(array, pltpu.HBM)


def moved_rows(rows, major):
    minor = rows // major
    at = lax.broadcasted_iota(jnp.int32, (1, rows), 1)
    dest = lax.rem(at, minor) * major + at // minor
    return (lax.broadcasted_iota(jnp.int32, (rows, rows), 0) == dest).astype(BF16)


def pack(
    dims, psi_ref, pot_ref, coup_ref, hel_ref, rf_ref, dp_ref, out_ref,
    wide, ready, coup, rf, dp, in_sems, out_sems, sems,
):
    slab, nvib, nang, share, blocks = dims
    near = lax.axis_size("hl")
    here = lax.axis_index("hl")
    is_last = lax.axis_index("g") * near + here == blocks - 1
    tall = WIDE // LANES * slab
    chunks = (nang + share) // WIDE
    height = (nang + share) // LANES * slab

    def load(i):
        if i * WIDE < share:
            first = pl.multiple_of(here * share + i * WIDE, LANES)
            source = pot_ref.at[:, pl.ds(first, WIDE)]
        else:
            source = psi_ref.at[:, pl.ds(i * WIDE - share, WIDE)]
        return pltpu.make_async_copy(source, wide.at[i], in_sems.at[i])

    def save(i):
        size = tall + (SMALL if i == chunks - 1 else 0)
        lines = pl.ds(i * tall, size)
        return pltpu.make_async_copy(
            ready.at[:, lines, :], out_ref.at[:, lines, :], out_sems.at[i]
        )

    small = [
        pltpu.make_async_copy(source, target, sems.at[i])
        for i, (source, target) in enumerate(
            [(coup_ref, coup), (rf_ref, rf), (dp_ref, dp)]
        )
    ]
    for i in range(chunks):
        load(i).start()
    for copy in small:
        copy.start()
    pick = moved_rows(slab * nvib, nvib)

    for copy in small:
        copy.wait()
    ce = jnp.where(is_last, 0.0, coup[...].astype(F32))
    lines = [ce[:, i * LANES : (i + 1) * LANES] for i in range(nang // LANES)]
    parts = []
    for value in (rf[...], dp[...]):
        high = value.astype(BF16).astype(F32)
        parts += [high, value - high]
    spread = (
        lax.rem(lax.broadcasted_iota(jnp.int32, (slab, LANES), 1), slab)
        == lax.broadcasted_iota(jnp.int32, (slab, LANES), 0)
    ).astype(BF16)
    filler = [jnp.zeros((SMALL - len(parts), slab), F32)]
    repeated = jnp.dot(
        jnp.concatenate(parts + filler, axis=0).astype(BF16), spread, preferred_element_type=F32
    )
    owner = lax.broadcasted_iota(jnp.int32, (SMALL, LANES), 1) // slab
    mine = owner == lax.broadcasted_iota(jnp.int32, (SMALL, LANES), 0)
    line = jnp.sum(jnp.where(mine, repeated, 0.0), axis=0, keepdims=True)
    lane = lax.broadcasted_iota(jnp.int32, (1, LANES), 1)
    lines.append(jnp.where(lane == LANES - 1, hel_ref[...].astype(F32), line))
    if len(lines) < SMALL:
        lines.append(jnp.zeros((SMALL - len(lines), LANES), F32))
    tile = jnp.concatenate(lines, axis=0).astype(BF16)
    for v in range(nvib):
        ready[v, height:, :] = tile

    for i in range(chunks):
        load(i).wait()
        moved = jnp.dot(pick, wide[i].astype(BF16), preferred_element_type=F32)
        moved = moved.astype(BF16).reshape(nvib, slab, WIDE)
        for t in range(WIDE // LANES):
            row = i * tall + t * slab
            ready[:, row : row + slab, :] = moved[:, :, t * LANES : (t + 1) * LANES]
        save(i).start()
    for i in range(chunks):
        save(i).wait()


def unpack(dims, msg_ref, out_ref, amp_ref, wide, sems):
    slab, nvib, nang, pieces = dims
    rows = slab * nvib
    tall = STEP // LANES * slab
    steps = nang // STEP

    def save(step):
        cols = pl.ds(step * STEP, STEP)
        return pltpu.make_async_copy(wide.at[:, cols], out_ref.at[:, cols], sems.at[step])

    pick = moved_rows(rows, slab)
    for step in range(steps):
        parts = [
            msg_ref[:, row : row + slab, :].reshape(rows, LANES)
            for row in range(step * tall, (step + 1) * tall, slab)
        ]
        wide[:, step * STEP : (step + 1) * STEP] = jnp.dot(
            pick, jnp.concatenate(parts, axis=1), preferred_element_type=F32
        )
        save(step).start()
    base = nang // LANES * slab
    lines = jnp.sum(msg_ref[:, base : base + SMALL, :].astype(F32), axis=0)
    lines = [lines[i : i + 1] + lines[pieces + i : pieces + i + 1] for i in range(pieces)]
    amp_ref[...] = jnp.concatenate(lines, axis=1)[:, : amp_ref.shape[1]]
    for step in range(steps):
        save(step).wait()


def rows_in(ref, first, count, slab, nang, base):
    return jnp.concatenate(
        [
            jnp.concatenate(
                [ref[m, base + i * slab : base + (i + 1) * slab, :] for i in range(nang // LANES)],
                axis=1,
            )
            for m in range(first, first + count)
        ],
        axis=0,
    )


def coupling_in(ref, m, base, nang):
    page = ref[m, base : base + SMALL, :].astype(F32)
    lines = [page[i : i + 1, :] for i in range(nang // LANES)]
    return jnp.concatenate(lines, axis=1), page[len(lines) : len(lines) + 1, :]


def unfold(dims, msg_ref, src, pot, radii, khat, coup):
    own, nslab, slab, nang, nquad = dims
    share = nquad // own
    top = share // LANES * slab
    base = top + nang // LANES * slab
    lane = lax.broadcasted_iota(jnp.int32, (slab, LANES), 1)
    row = lax.broadcasted_iota(jnp.int32, (slab, LANES), 0)
    for k in range(own):
        src[k] = rows_in(msg_ref, k * nslab, nslab, slab, nang, top)
        for m in range(nslab):
            for t in range(share // LANES):
                cols = pl.ds(k * share + t * LANES, LANES)
                tile = msg_ref[k * nslab + m, t * slab : (t + 1) * slab, :]
                pot[m * slab : (m + 1) * slab, cols] = tile.astype(F32)
        coup[k], line = coupling_in(msg_ref, k * nslab, base, nang)
        value = line[:, LANES - 1 :]
        khat[k] = jnp.broadcast_to(-2.0 * value * value, (1, LANES))
    for m in range(nslab):
        _, line = coupling_in(msg_ref, m, base, nang)
        for i in range(2):
            hit = (lane == row + 2 * i * slab) | (lane == row + (2 * i + 1) * slab)
            value = jnp.sum(jnp.where(hit, line, 0.0), axis=1, keepdims=True)
            radii[i, m * slab : (m + 1) * slab, :] = jnp.broadcast_to(value, (slab, LANES))


def advance(dims, n, *refs):
    own, nslab, slab, nang, nquad = dims
    nrad = nslab * slab
    full, before = None, None
    if n == 1:
        msg_ref, basis_hbm, kin_ref = refs[:3]
        new_ref, newb_ref, src, basis, pot, radii, khat, coup, scaled, sems = refs[3:]

        def load(qi):
            cols = pl.ds(qi * STEP, STEP)
            return pltpu.make_async_copy(basis_hbm.at[:, cols], basis.at[:, cols], sems.at[qi])

        for qi in range(nquad // STEP):
            load(qi).start()
        unfold(dims, msg_ref, src, pot, radii, khat, coup)
    else:
        src, full, before, basis, kin_ref, pot, radii, khat, coup = refs[:9]
        new_ref, newb_ref, scaled = refs[9:]

    @pl.loop(0, nquad // STEP)
    def _(qi):
        cols = pl.ds(pl.multiple_of(qi * STEP, STEP), STEP)
        if n == 1:
            pltpu.make_async_copy(basis_hbm.at[:, cols], basis.at[:, cols], sems.at[qi]).wait()
        grid = jnp.dot(
            src[...].reshape(own * nrad, nang), basis[:, cols], preferred_element_type=F32
        )
        prod = grid.reshape(own, nrad, STEP) * pot[:, cols][None]
        scaled[:, cols] = prod.astype(BF16).reshape(own * nrad, STEP)

    factor = jnp.concatenate([radii[0]] * (STEP // LANES), axis=1)
    damp = jnp.concatenate([radii[1]] * (STEP // LANES), axis=1)

    @pl.loop(0, nang // STEP)
    def _(ji):
        cols = pl.ds(pl.multiple_of(ji * STEP, STEP), STEP)
        ang = lax.dot_general(
            scaled[...], basis[cols, :], NT, preferred_element_type=F32
        ).reshape(own, nrad, STEP)
        for k in range(own):
            here = src[k, :, cols]
            total = ang[k] + jnp.dot(kin_ref[...], here, preferred_element_type=F32)
            value = here.astype(F32) if full is None else full[k, :, cols]
            total += jnp.concatenate([khat[k]] * (STEP // LANES), axis=1) * factor * value
            if k + 1 < own:
                total += coup[k, :, cols] * src[k + 1, :, cols].astype(F32)
            if k > 0:
                total += coup[k - 1, :, cols] * src[k - 1, :, cols].astype(F32)
            if n == 1:
                new = damp * total
            else:
                new = damp * (2.0 * total - damp * before[k, :, cols].astype(F32))
            new_ref[k, :, cols] = new
            newb_ref[k, :, cols] = new.astype(BF16)


def edges(dims, n, *refs):
    own, nslab, slab, nang, nquad, nchan, count = dims
    last = n == ITERS
    nrad = nslab * slab
    got_refs, rest = refs[:count], list(refs[count:])
    new_ref, newb_ref, radii, coup = rest[:4]
    rest = rest[4:]
    group = lax.axis_index("g")
    base = nang // LANES * slab
    if n == 1:
        newf_out, newb_out, *edge_outs, ce_out = rest
    elif last:
        ce_ref, rad_ref, vib_ref, proj_ref, out_ref, newb_out = rest
        newf_out = None
    else:
        ce_ref, newf_out, newb_out, *edge_outs = rest

    if count == 1:
        targets = [jnp.where(group == 0, own - 1, 0)]
    else:
        targets = [own - 1, 0]
    newb_out[...] = newb_ref[...]
    if not last:
        newf_out[...] = new_ref[...]
    scale = radii[1] if n == 1 else 2.0 * radii[1]
    scale = jnp.concatenate([scale] * (nang // LANES), axis=1)
    for i, (got, target) in enumerate(zip(got_refs, targets)):
        if n == 1:
            block = rows_in(got, 0, nslab, slab, nang, 0).astype(F32)
            theirs, _ = coupling_in(got, 0, base, nang)
            if count == 1:
                ce = jnp.where(group == 0, coup[own - 1], theirs)
            else:
                ce = coup[own - 1] if i == 0 else theirs
            ce_out[i] = ce
        else:
            block = got[...].astype(F32)
            ce = ce_ref[i]
        fixed = (new_ref[target] if i == 0 or own > 1 else fixed) + scale * (ce * block)
        if not last:
            newf_out[target] = fixed
        newb_out[target] = fixed.astype(BF16)
    if not last:
        for edge, target in zip(edge_outs, targets):
            edge[...] = newb_out[target]
        return

    chan = nchan // nslab
    pieces = -(-chan // LANES)
    high_at = nang // LANES * slab
    vib = lax.axis_index("hl") * nslab + lax.axis_index("rad")
    rows_at = lax.broadcasted_iota(jnp.int32, (nrad, chan), 0)
    final = newb_out[...].reshape(own * nrad, nang)
    for m in range(nslab):
        cols = slice(m * chan, (m + 1) * chan)
        table = lax.dot_general(
            final, proj_ref[cols, :], NT, preferred_element_type=F32
        ).reshape(own, nrad, chan)
        hit = (rows_at == rad_ref[:, cols]) & (vib_ref[:, cols] == vib)
        for k in range(own):
            amp = jnp.sum(jnp.where(hit, table[k], 0.0), axis=0, keepdims=True)
            if pieces * LANES > chan:
                amp = jnp.concatenate([amp, jnp.zeros((1, pieces * LANES - chan), F32)], axis=1)
            high = amp.astype(BF16).astype(F32)
            tile = [
                part[:, s * LANES : (s + 1) * LANES]
                for part in (high, amp - high)
                for s in range(pieces)
            ]
            if len(tile) < SMALL:
                tile.append(jnp.zeros((SMALL - len(tile), LANES), F32))
            to = k * nslab + m
            out_ref[to, high_at : high_at + SMALL, :] = jnp.concatenate(tile, axis=0).astype(BF16)
            for t in range(nang // LANES):
                out_ref[to, t * slab : (t + 1) * slab, :] = newb_out[
                    k, m * slab : (m + 1) * slab, t * LANES : (t + 1) * LANES
                ]


def per_device(
    psi_start,
    potential,
    basis,
    kinetic,
    radial_factor,
    damping,
    coupling,
    helicity,
    chan_rad,
    chan_vib,
    projector,
):
    _, slab, nvib, nang = psi_start.shape
    nquad = basis.shape[1]
    nchan = projector.shape[0]
    groups = lax.axis_size("g")
    own = lax.axis_size("hl")
    nslab = lax.axis_size("rad")
    blocks = groups * own
    group = lax.axis_index("g")
    nrad = nslab * slab
    share = nquad // own
    chunks = (nang + share) // WIDE
    height = (nang + share) // LANES * slab + SMALL
    shape = jax.ShapeDtypeStruct

    send = pl.pallas_call(
        functools.partial(pack, (slab, nvib, nang, share, blocks)),
        out_shape=shape((nvib, height, LANES), BF16),
        in_specs=[HBM] * 3 + [VMEM] + [HBM] * 2,
        out_specs=HBM,
        scratch_shapes=[
            pltpu.VMEM((chunks, slab * nvib, WIDE), F32),
            pltpu.VMEM((nvib, height, LANES), BF16),
            pltpu.VMEM((1, nang), BF16),
            pltpu.VMEM((1, slab), F32),
            pltpu.VMEM((1, slab), F32),
            pltpu.SemaphoreType.DMA((chunks,)),
            pltpu.SemaphoreType.DMA((chunks,)),
            pltpu.SemaphoreType.DMA((3,)),
        ],
        compiler_params=PARAMS,
        name="pack",
    )(
        in_hbm(psi_start.reshape(slab * nvib, nang)),
        in_hbm(potential.reshape(slab * nvib, nquad)),
        in_hbm(coupling),
        helicity[None],
        in_hbm(radial_factor[None]),
        in_hbm(damping[None]),
    )
    message = lax.all_to_all(send, ("hl", "rad"), 0, 0, tiled=True)

    count = 1 if groups == 2 else 2
    up = [(i, i + 1) for i in range(groups - 1)]
    down = [(i + 1, i) for i in range(groups - 1)]

    def swap(parts):
        if count == 1:
            return [lax.ppermute(parts[0], "g", [(0, 1), (1, 0)])]
        return [lax.ppermute(parts[1], "g", down), lax.ppermute(parts[0], "g", up)]

    rows = message[:, share // LANES * slab :]
    if count == 1:
        first = jnp.where(group == 0, own - 1, 0) * nslab
        edge = [lax.dynamic_slice_in_dim(rows, first, nslab, 0)]
    else:
        edge = [rows[(own - 1) * nslab :], rows[:nslab]]

    cost = pl.CostEstimate(
        flops=4 * own * nrad * nang * nquad, bytes_accessed=8 * 1024 * 1024, transcendentals=0
    )
    full_type = shape((own, nrad, nang), F32)
    block_type = shape((own, nrad, nang), BF16)
    edge_types = [shape((nrad, nang), BF16)] * count
    scaled = pltpu.VMEM((own * nrad, nquad), BF16)
    dims = (own, nslab, slab, nang, nquad)
    full = block = before = None
    for n in range(1, ITERS + 1):
        got = swap(edge)
        if n == 1:
            outs = [
                full_type,
                block_type,
                block_type,
                shape(basis.shape, BF16),
                shape((nrad, nquad), F32),
                shape((2, nrad, LANES), F32),
                shape((own, 1, LANES), F32),
                shape((own, 1, nang), F32),
            ]
            operands = [message, in_hbm(basis), kinetic]
            specs = [VMEM, HBM, VMEM]
            scratch = [scaled, pltpu.SemaphoreType.DMA((nquad // STEP,))]
        else:
            outs = [full_type, block_type]
            operands = [block, full, before, basis, kinetic, pot, radii, khat, coup]
            specs = [VMEM] * len(operands)
            scratch = [scaled]
        done = pl.pallas_call(
            functools.partial(advance, dims, n),
            out_shape=outs,
            in_specs=specs,
            out_specs=[VMEM] * len(outs),
            scratch_shapes=scratch,
            compiler_params=PARAMS,
            cost_estimate=cost,
            name=f"advance{n}",
        )(*operands)
        if n == 1:
            new, newb, before, basis, pot, radii, khat, coup = done
        else:
            before = full
            new, newb = done

        operands = got + [new, newb, radii, coup]
        outs = [full_type, block_type]
        scratch = []
        if n == 1:
            outs += edge_types + [shape((count, 1, nang), F32)]
        elif n == ITERS:
            operands += [ce, chan_rad[None], chan_vib[None], projector]
            outs = [shape((own * nslab, nang // LANES * slab + SMALL, LANES), BF16)]
            scratch = [pltpu.VMEM((own, nrad, nang), BF16)]
        else:
            operands += [ce]
            outs += edge_types
        done = pl.pallas_call(
            functools.partial(edges, dims + (nchan, count), n),
            out_shape=outs,
            in_specs=[VMEM] * len(operands),
            out_specs=[VMEM] * len(outs),
            scratch_shapes=scratch,
            compiler_params=PARAMS,
            name=f"edges{n}",
        )(*operands)
        if n == ITERS:
            break
        full, block = done[:2]
        edge = list(done[2 : 2 + count])
        if n == 1:
            ce = done[-1]

    home = lax.all_to_all(done[-1], ("hl", "rad"), 0, 0, tiled=True)
    chan = nchan // nslab
    psi_final, amplitude = pl.pallas_call(
        functools.partial(unpack, (slab, nvib, nang, -(-chan // LANES))),
        out_shape=[shape((slab * nvib, nang), F32), shape((1, chan), F32)],
        in_specs=[VMEM],
        out_specs=[HBM, VMEM],
        scratch_shapes=[
            pltpu.VMEM((slab * nvib, nang), F32),
            pltpu.SemaphoreType.DMA((nang // STEP,)),
        ],
        compiler_params=PARAMS,
        name="unpack",
    )(home)
    return (psi_final.reshape(1, slab, nvib, nang), amplitude)


def solution(mesh):
    nhel, nrad = mesh.shape["hel"], mesh.shape["rad"]

    def run(*args):
        nvib = args[0].shape[2]
        groups = nhel * nrad // nvib
        fine = Mesh(mesh.devices.reshape(groups, nhel // groups, nrad), ("g", "hl", "rad"))
        hel = ("g", "hl")
        placed = (
            P(hel, "rad", None, None),
            P("rad", None, None),
            P(),
            P(),
            P("rad"),
            P("rad"),
            P(hel, None),
            P(hel),
            P(),
            P(),
            P(),
        )
        return jax.shard_map(
            per_device,
            mesh=fine,
            in_specs=placed,
            out_specs=(P(hel, "rad", None, None), P(hel, "rad")),
            check_vma=False,
        )(*args)

    return run
```

time: 107 us -> 58.2 us (0.54)
  the two profiles are of different devices: /device:TPU:24 before, /device:TPU:0 now
where the time goes in v4:
time: 58.2 us; the launch traced here: 57.9 us
  waiting for transfers between devices  16.9 us (29%)
  Pallas kernels  15.4 us (26%)
  blocking collectives  13.7 us (24%)
  starting transfers between devices  10.4 us (18%)
  between operations  1.37 us (2%)
    all_to_all x1, blocking collectives, per_device(): home = lax.all_to_all(done[-1], ('hl', 'rad'), 0, 0, tiled=True)  13.7 us
    all_to_all x1, waiting for transfers between devices, per_device(): message = lax.all_to_all(send, ('hl', 'rad'), 0, 0, tiled=True)  11.6 us
    pallas_call x3, Pallas kernels, per_device(): pl.pallas_call(functools.partial(advance, dims, n), out_shape=outs, in_sp...  10.2 us
    all_to_all x1, starting transfers between devices, per_device(): message = lax.all_to_all(send, ('hl', 'rad'), 0, 0, tiled=True)  6.33 us
    ppermute x3, waiting for transfers between devices, swap(): return [lax.ppermute(parts[0], 'g', [(0, 1), (1, 0)])]  5.38 us
    ppermute x3, starting transfers between devices, swap(): return [lax.ppermute(parts[0], 'g', [(0, 1), (1, 0)])]  4.11 us
    pallas_call x1, Pallas kernels, per_device(): pl.pallas_call(functools.partial(pack, (slab, nvib, nang, share, blocks))...  2.63 us
    pallas_call x1, Pallas kernels, per_device(): pl.pallas_call(functools.partial(unpack, (slab, nvib, nang, -(-chan // LA...  1.65 us
  transfers between devices with their start and end apart: 4, of which 4 were waited for; matrix products, arithmetic and copies ran while one was open for 0% of the time, Pallas kernels for 18%

profile of v4, /device:TPU:0, one launch (start us, length us, event | category | flops | bytes accessed | tf_op | source)
XLA Modules:
  0.0 57.9 jit_solution(10329541361676416986)
XLA Ops:
  1.3 0.0 copy-start.1
  1.3 2.6 %pack.1 = bf16[16,152,128]{2,1,0:T(8,128)(2,1)} custom-call(f32[256,768]{1,0:T(8,128)} %bitcast.12, f32[256,1536]{1,0:T(8,128)} %bitcast.11, bf16[1,768]{1,0:T(2,128)(2,1)} %coup_ref.1, s32[1,1]{1,0:T(1,128)} %bitcast.8.hel_ref, f32[1,16]{1,0:T(1,128)} %bitcast.13, f32[1,16]{1,0:T(1,128)} %bitcast.14), custom_call_target="tpu_custom_call" | custom-call | tf_op jit(solution)/shard_map/pack/pallas_call | solution.py:347
  3.9 6.3 %all-to-all-start = ((bf16[16,152,128]{2,1,0:T(8,128)(2,1)}), bf16[16,152,128]{2,1,0:T(8,128)(2,1)S(1)}, u32[]{:S(2)}, u32[]{:S(2)}) async-start(bf16[16,152,128]{2,1,0:T(8,128)(2,1)} %pack.1), calls=%async_computation | async-start | bytes 1245184 | tf_op jit(solution)/shard_map/all_to_all | solution.py:372
  10.3 11.6 %all-to-all-done.refs_0_ = bf16[16,152,128]{2,1,0:T(8,128)(2,1)S(1)} async-done(((bf16[16,152,128]{2,1,0:T(8,128)(2,1)}), bf16[16,152,128]{2,1,0:T(8,128)(2,1)S(1)}, u32[]{:S(2)}, u32[]{:S(2)}) %all-to-all-start) | async-done | bytes 622624 | tf_op jit(solution)/shard_map/all_to_all | solution.py:372
  21.9 2.7 %collective-permute-start = (bf16[4,104,128]{2,1,0:T(8,128)(2,1)S(1)}, bf16[4,104,128]{2,1,0:T(8,128)(2,1)S(1)}, u32[]{:S(2)}, u32[]{:S(2)}) collective-permute-start(bf16[4,104,128]{2,1,0:T(8,128)(2,1)S(1)} %constant_dynamic-slice_fusion), channel_id=1, source_target_pairs={{0,16},{16,0},{1,17},{17,1},{2,18},{18,2},{3,19},{19,3},{4,20},{20... | collective-permute-start | bytes 319496 | tf_op jit(solution)/shard_map/ppermute | solution.py:380
  24.6 0.0 copy-done.1
  24.6 4.1 %advance1.1 = (f32[4,64,768]{2,1,0:T(8,128)S(1)}, bf16[4,64,768]{2,1,0:T(8,128)(2,1)S(1)}, bf16[4,64,768]{2,1,0:T(8,128)(2,1)S(1)}, bf16[768,1536]{1,0:T(8,128)(...) custom-call(bf16[16,152,128]{2,1,0:T(8,128)(2,1)S(1)} %all-to-all-do, ...), custom_call_target="tpu_custom_call" | custom-call | flops 1207959552 | bytes 8388608 | tf_op jit(solution)/shard_map/advance1/pallas_call | solution.py:420
  28.7 0.6 %collective-permute-done.refs_0_ = bf16[4,104,128]{2,1,0:T(8,128)(2,1)S(1)} collective-permute-done((bf16[4,104,128]{2,1,0:T(8,128)(2,1)S(1)}, bf16[4,104,128]{2,1,0:T(8,128)(2,1)S(1)}, u32[]{:S(2)}, u32[]{:S(2)}) %collective-permute-start) | collective-permute-done | bytes 106528 | tf_op jit(solution)/shard_map/ppermute | solution.py:380
  29.3 0.1 edges1.1
  29.4 1.1 %collective-permute-start.1 = (bf16[64,768]{1,0:T(8,128)(2,1)S(1)}, bf16[64,768]{1,0:T(8,128)(2,1)S(1)}, u32[]{:S(2)}, u32[]{:S(2)}) collective-permute-start(bf16[64,768]{1,0:T(8,128)(2,1)S(1)} %get-tuple-element.27), channel_id=1, source_target_pairs={{0,16},{16,0},{1,17},{17,1},{2,18},{18,2},{3,19},{19,3},{4,20},{20... | collective-permute-start | bytes 294920 | tf_op jit(solution)/shard_map/ppermute | solution.py:380
  30.5 3.0 %advance2.1 = (f32[4,64,768]{2,1,0:T(8,128)S(1)}, bf16[4,64,768]{2,1,0:T(8,128)(2,1)S(1)}) custom-call(bf16[4,64,768]{2,1,0:T(8,128)(2,1)S(1)} %get-tuple-element.28.refs_0_, f32[4,64,768]{2,1,0:T(8,128)S(1)} %get-tuple-element.29.refs_1_.refs_2_, bf16[4,64,768]{2,1,0:T(8,128)(2,1)S(1)} %get-tuple-element.30.refs_2_, ...), custom_call_target="tpu_custom_call" | custom-call | flops 1207959552 | bytes 8388608 | tf_op jit(solution)/shard_map/advance2/pallas_call | solution.py:420
  33.5 2.2 %collective-permute-done.1.refs_0_ = bf16[64,768]{1,0:T(8,128)(2,1)S(1)} collective-permute-done((bf16[64,768]{1,0:T(8,128)(2,1)S(1)}, bf16[64,768]{1,0:T(8,128)(2,1)S(1)}, u32[]{:S(2)}, u32[]{:S(2)}) %collective-permute-start.1) | collective-permute-done | bytes 98336 | tf_op jit(solution)/shard_map/ppermute | solution.py:380
  35.7 0.1 edges2.1
  35.8 0.4 collective-permute-start.2
  36.2 0.0 copy-start
  36.2 0.0 copy-start.2
  36.2 0.0 copy-start.3
  36.2 3.0 %advance3.1 = (f32[4,64,768]{2,1,0:T(8,128)S(1)}, bf16[4,64,768]{2,1,0:T(8,128)(2,1)S(1)}) custom-call(bf16[4,64,768]{2,1,0:T(8,128)(2,1)S(1)} %get-tuple-element.38.refs_0_, f32[4,64,768]{2,1,0:T(8,128)S(1)} %get-tuple-element.39.refs_1_, f32[4,64,768]{2,1,0:T(8,128)S(1)} %get-tuple-element.29.refs_1_.refs_2_, ...), custom_call_target="tpu_custom_call" | custom-call | flops 1207959552 | bytes 8388608 | tf_op jit(solution)/shard_map/advance3/pallas_call | solution.py:420
  39.3 2.6 %collective-permute-done.2.refs_0_ = bf16[64,768]{1,0:T(8,128)(2,1)S(1)} collective-permute-done((bf16[64,768]{1,0:T(8,128)(2,1)S(1)}, bf16[64,768]{1,0:T(8,128)(2,1)S(1)}, u32[]{:S(2)}, u32[]{:S(2)}) %collective-permute-start.2) | collective-permute-done | bytes 98336 | tf_op jit(solution)/shard_map/ppermute | solution.py:380
  41.9 0.0 copy-done
  41.9 0.0 copy-done.2
  41.9 0.0 copy-done.3
  41.9 0.7 %edges3.1 = bf16[16,104,128]{2,1,0:T(8,128)(2,1)S(1)} custom-call(bf16[64,768]{1,0:T(8,128)(2,1)S(1)} %collective-permute-done.2.refs_0_, f32[4,64,768]{2,1,0:T(8,128)S(1)} %get-tuple-element.40.refs_1_, bf16[4,64,768]{2,1,0:T(8,128)(2,1)S(1)} %get-tuple-element.41.refs_2_, f32[2,64,128]{2,1,0:T(8,128)S(1)} %get-tuple-element.25.refs_3_.refs_6_, ...), custom_call_target="tpu_custom_call" | custom-call | tf_op jit(solution)/shard_map/edges3/pallas_call | solution.py:448
  42.6 13.7 %all_to_all.10.msg_ref = bf16[16,104,128]{2,1,0:T(8,128)(2,1)S(1)} all-to-all(bf16[16,104,128]{2,1,0:T(8,128)(2,1)S(1)} %edges3.1), channel_id=1, replica_groups=mesh['g'=2,'hl'=4,'rad'=4] {'hl','rad'}, dimensions={0} | all-to-all | bytes 851968 | tf_op jit(solution)/shard_map/all_to_all | solution.py:464
  56.3 1.7 %unpack.1 = (f32[256,768]{1,0:T(8,128)}, f32[1,256]{1,0:T(1,128)}) custom-call(bf16[16,104,128]{2,1,0:T(8,128)(2,1)S(1)} %all_to_all.10.msg_ref), custom_call_target="tpu_custom_call" | custom-call | tf_op jit(solution)/shard_map/unpack/pallas_call | solution.py:466
  (2 shorter events, 0.1 us)
Async XLA Ops:
  1.3 23.3 %copy-start.1 = (bf16[64,64]{1,0:T(8,128)(2,1)S(1)}, bf16[64,64]{1,0:T(8,128)(2,1)}, u32[]{:S(2)}) copy-start(bf16[64,64]{1,0:T(8,128)(2,1)} %refs_4_.3) | copy-start | bytes 24580
  3.9 17.9 %all-to-all-start = ((bf16[16,152,128]{2,1,0:T(8,128)(2,1)}), bf16[16,152,128]{2,1,0:T(8,128)(2,1)S(1)}, u32[]{:S(2)}, u32[]{:S(2)}) async-start(bf16[16,152,128]{2,1,0:T(8,128)(2,1)} %pack.1), calls=%async_computation | async-start | bytes 1245184 | tf_op jit(solution)/shard_map/all_to_all | solution.py:372
  21.9 7.4 %collective-permute-start = (bf16[4,104,128]{2,1,0:T(8,128)(2,1)S(1)}, bf16[4,104,128]{2,1,0:T(8,128)(2,1)S(1)}, u32[]{:S(2)}, u32[]{:S(2)}) collective-permute-start(bf16[4,104,128]{2,1,0:T(8,128)(2,1)S(1)} %constant_dynamic-slice_fusion), channel_id=1, source_target_pairs={{0,16},{16,0},{1,17},{17,1},{2,18},{18,2},{3,19},{19,3},{4,20},{20... | collective-permute-start | bytes 319496 | tf_op jit(solution)/shard_map/ppermute | solution.py:380
  29.4 6.3 %collective-permute-start.1 = (bf16[64,768]{1,0:T(8,128)(2,1)S(1)}, bf16[64,768]{1,0:T(8,128)(2,1)S(1)}, u32[]{:S(2)}, u32[]{:S(2)}) collective-permute-start(bf16[64,768]{1,0:T(8,128)(2,1)S(1)} %get-tuple-element.27), channel_id=1, source_target_pairs={{0,16},{16,0},{1,17},{17,1},{2,18},{18,2},{3,19},{19,3},{4,20},{20... | collective-permute-start | bytes 294920 | tf_op jit(solution)/shard_map/ppermute | solution.py:380
  35.8 6.0 %collective-permute-start.2 = (bf16[64,768]{1,0:T(8,128)(2,1)S(1)}, bf16[64,768]{1,0:T(8,128)(2,1)S(1)}, u32[]{:S(2)}, u32[]{:S(2)}) collective-permute-start(bf16[64,768]{1,0:T(8,128)(2,1)S(1)} %get-tuple-element.37), channel_id=1, source_target_pairs={{0,16},{16,0},{1,17},{17,1},{2,18},{18,2},{3,19},{19,3},{4,20},{20... | collective-permute-start | bytes 294920 | tf_op jit(solution)/shard_map/ppermute | solution.py:380
  36.2 5.7 %copy-start = (bf16[1024,768]{1,0:T(8,128)(2,1)S(1)}, bf16[1024,768]{1,0:T(8,128)(2,1)}, u32[]{:S(2)}) copy-start(bf16[1024,768]{1,0:T(8,128)(2,1)} %refs_8_.1) | copy-start | bytes 4718596
  36.2 5.7 %copy-start.2 = (s32[1024]{0:T(1024)S(1)}, s32[1024]{0:T(1024)}, u32[]{:S(2)}) copy-start(s32[1024]{0:T(1024)} %param.19) | copy-start | bytes 12292
  36.2 5.7 %copy-start.3 = (s32[1024]{0:T(1024)S(1)}, s32[1024]{0:T(1024)}, u32[]{:S(2)}) copy-start(s32[1024]{0:T(1024)} %param.20) | copy-start | bytes 12292

commit v5 on v4

v5 whole, which is shorter than its diff:
```python
import functools

import jax
import jax.numpy as jnp
from jax import lax
from jax.experimental import pallas as pl
from jax.experimental.pallas import tpu as pltpu
from jax.sharding import Mesh
from jax.sharding import PartitionSpec as P

ITERS = 3
LANES = 128
STEP = 256
WIDE = 384
SMALL = 8
NT = (((1,), (1,)), ((), ()))
F32 = jnp.float32
BF16 = jnp.bfloat16
VMEM = pl.BlockSpec(memory_space=pltpu.VMEM)
HBM = pl.BlockSpec(memory_space=pltpu.HBM)
PARAMS = pltpu.CompilerParams(vmem_limit_bytes=24 * 1024 * 1024)


def in_hbm(array):
    return pltpu.with_memory_space_constraint(array, pltpu.HBM)


def moved_rows(rows, major):
    minor = rows // major
    at = lax.broadcasted_iota(jnp.int32, (1, rows), 1)
    dest = lax.rem(at, minor) * major + at // minor
    return (lax.broadcasted_iota(jnp.int32, (rows, rows), 0) == dest).astype(BF16)


def pack(
    dims, psi_ref, pot_ref, coup_ref, hel_ref, rf_ref, dp_ref, out_ref,
    wide, ready, coup, rf, dp, in_sems, out_sems, sems,
):
    slab, nvib, nang, share, blocks = dims
    near = lax.axis_size("hl")
    here = lax.axis_index("hl")
    is_last = lax.axis_index("g") * near + here == blocks - 1
    tall = WIDE // LANES * slab
    chunks = (nang + share) // WIDE
    height = (nang + share) // LANES * slab

    def load(i):
        if i * WIDE < share:
            first = pl.multiple_of(here * share + i * WIDE, LANES)
            source = pot_ref.at[:, pl.ds(first, WIDE)]
        else:
            source = psi_ref.at[:, pl.ds(i * WIDE - share, WIDE)]
        return pltpu.make_async_copy(source, wide.at[i], in_sems.at[i])

    def save(i):
        size = tall + (SMALL if i == chunks - 1 else 0)
        lines = pl.ds(i * tall, size)
        return pltpu.make_async_copy(
            ready.at[:, lines, :], out_ref.at[:, lines, :], out_sems.at[i]
        )

    small = [
        pltpu.make_async_copy(source, target, sems.at[i])
        for i, (source, target) in enumerate(
            [(coup_ref, coup), (rf_ref, rf), (dp_ref, dp)]
        )
    ]
    for i in range(chunks):
        load(i).start()
    for copy in small:
        copy.start()
    pick = moved_rows(slab * nvib, nvib)

    for copy in small:
        copy.wait()
    ce = jnp.where(is_last, 0.0, coup[...].astype(F32))
    lines = [ce[:, i * LANES : (i + 1) * LANES] for i in range(nang // LANES)]
    parts = []
    for value in (rf[...], dp[...]):
        high = value.astype(BF16).astype(F32)
        parts += [high, value - high]
    spread = (
        lax.rem(lax.broadcasted_iota(jnp.int32, (slab, LANES), 1), slab)
        == lax.broadcasted_iota(jnp.int32, (slab, LANES), 0)
    ).astype(BF16)
    filler = [jnp.zeros((SMALL - len(parts), slab), F32)]
    repeated = jnp.dot(
        jnp.concatenate(parts + filler, axis=0).astype(BF16), spread, preferred_element_type=F32
    )
    owner = lax.broadcasted_iota(jnp.int32, (SMALL, LANES), 1) // slab
    mine = owner == lax.broadcasted_iota(jnp.int32, (SMALL, LANES), 0)
    line = jnp.sum(jnp.where(mine, repeated, 0.0), axis=0, keepdims=True)
    lane = lax.broadcasted_iota(jnp.int32, (1, LANES), 1)
    lines.append(jnp.where(lane == LANES - 1, hel_ref[...].astype(F32), line))
    if len(lines) < SMALL:
        lines.append(jnp.zeros((SMALL - len(lines), LANES), F32))
    tile = jnp.concatenate(lines, axis=0).astype(BF16)
    for v in range(nvib):
        ready[v, height:, :] = tile

    for i in range(chunks):
        load(i).wait()
        moved = jnp.dot(pick, wide[i].astype(BF16), preferred_element_type=F32)
        moved = moved.astype(BF16).reshape(nvib, slab, WIDE)
        for t in range(WIDE // LANES):
            row = i * tall + t * slab
            ready[:, row : row + slab, :] = moved[:, :, t * LANES : (t + 1) * LANES]
        save(i).start()
    for i in range(chunks):
        save(i).wait()


def unpack(dims, msg_ref, out_ref, amp_ref, wide, sems):
    slab, nvib, nang, pieces = dims
    rows = slab * nvib
    tall = STEP // LANES * slab
    steps = nang // STEP

    def save(step):
        cols = pl.ds(step * STEP, STEP)
        return pltpu.make_async_copy(wide.at[:, cols], out_ref.at[:, cols], sems.at[step])

    pick = moved_rows(rows, slab)
    for step in range(steps):
        parts = [
            msg_ref[:, row : row + slab, :].reshape(rows, LANES)
            for row in range(step * tall, (step + 1) * tall, slab)
        ]
        wide[:, step * STEP : (step + 1) * STEP] = jnp.dot(
            pick, jnp.concatenate(parts, axis=1), preferred_element_type=F32
        )
        save(step).start()
    base = nang // LANES * slab
    lines = jnp.sum(msg_ref[:, base : base + SMALL, :].astype(F32), axis=0)
    lines = [lines[i : i + 1] + lines[pieces + i : pieces + i + 1] for i in range(pieces)]
    amp_ref[...] = jnp.concatenate(lines, axis=1)[:, : amp_ref.shape[1]]
    for step in range(steps):
        save(step).wait()


def rows_in(ref, first, count, slab, nang, base):
    return jnp.concatenate(
        [
            jnp.concatenate(
                [ref[m, base + i * slab : base + (i + 1) * slab, :] for i in range(nang // LANES)],
                axis=1,
            )
            for m in [first + i for i in range(count)]
        ],
        axis=0,
    )


def small_in(ref, m, base, nang):
    page = ref[m, base : base + SMALL, :].astype(F32)
    lines = [page[i : i + 1, :] for i in range(nang // LANES)]
    value = page[len(lines) : len(lines) + 1, LANES - 1 :]
    return jnp.concatenate(lines, axis=1), jnp.broadcast_to(-2.0 * value * value, (1, LANES))


def link(mirror, side, near, far):
    if mirror:
        return jnp.where(lax.axis_index("g") == 0, near, far)
    return far if side == 0 else near


def place(mirror, own, i):
    if mirror:
        return jnp.where(lax.axis_index("g") == 0, own - 1 - i, i)
    return i


def unfold(dims, msg_ref, src, pot, radii, khat, coup):
    own, nslab, slab, nang, nquad, mirror = dims
    share = nquad // own
    top = share // LANES * slab
    base = top + nang // LANES * slab
    lane = lax.broadcasted_iota(jnp.int32, (slab, LANES), 1)
    row = lax.broadcasted_iota(jnp.int32, (slab, LANES), 0)
    for k in range(own):
        for m in range(nslab):
            for t in range(share // LANES):
                cols = pl.ds(k * share + t * LANES, LANES)
                tile = msg_ref[k * nslab + m, t * slab : (t + 1) * slab, :]
                pot[m * slab : (m + 1) * slab, cols] = tile.astype(F32)
    for i in range(own):
        first = place(mirror, own, i) * nslab
        src[i] = rows_in(msg_ref, first, nslab, slab, nang, top)
        coup[i], khat[i] = small_in(msg_ref, first, base, nang)
    for m in range(nslab):
        page = msg_ref[m, base : base + SMALL, :].astype(F32)
        line = page[nang // LANES : nang // LANES + 1, :]
        for i in range(2):
            hit = (lane == row + 2 * i * slab) | (lane == row + (2 * i + 1) * slab)
            value = jnp.sum(jnp.where(hit, line, 0.0), axis=1, keepdims=True)
            radii[i, m * slab : (m + 1) * slab, :] = jnp.broadcast_to(value, (slab, LANES))


def wider(tile, size):
    return jnp.concatenate([tile] * (size // LANES), axis=1)


def advance(dims, sides, n, *refs):
    own, nslab, slab, nang, nquad, mirror = dims
    nrad = nslab * slab
    refs = list(refs)
    take = lambda count: [refs.pop(0) for _ in range(count)]
    edge_of = [0, own - 1]
    if n == 1:
        msg_ref, basis_hbm, kin_ref = take(3)
        new_ref, src, basis, pot, radii, khat, coup, chain = take(8)
        rows, scaled, sems = take(3)
        for qi in range(nquad // STEP):
            cols = pl.ds(qi * STEP, STEP)
            pltpu.make_async_copy(basis_hbm.at[:, cols], basis.at[:, cols], sems.at[qi]).start()
        unfold(dims, msg_ref, src, pot, radii, khat, coup)
        rows[...] = src[...]
        for i in range(own - 1):
            chain[i] = link(mirror, 0, coup[i + 1], coup[i])
    else:
        raw = take(sides)
        basis, kin_ref, pot, radii, khat, coup, chain = take(7)
        scale = wider(radii[1] if n == 2 else 2.0 * radii[1], nang)
        base = nang // LANES * slab
        if n == 2:
            part, first_b = take(2)
            full, block, new_ref, part_h, halo_b, halo_c, halo_k = take(7)
            rows, scaled, joint = take(3)
        else:
            part, first_b, first_f, halo_part, halo1_b, halo1_c, halo1_k, level1_b = take(8)
            new_ref, part_h, part_hh, halo_c = take(4)
            full, halo_b, halo_k, rows, scaled, joint = take(6)
        for i in range(own):
            value = part[i]
            full[i] = value
            rows[i] = value.astype(BF16)
        for s in range(sides):
            halo_b[s] = rows_in(raw[s], 0, nslab, slab, nang, 0)
            halo_c[s], halo_k[s] = small_in(raw[s], 0, base, nang)
            at = edge_of[s]
            if n == 2:
                joint[s, 0] = link(mirror, s, coup[at], halo_c[s])
                seen = halo_b[s]
                rows[own + s] = seen
            else:
                joint[s, 0] = link(mirror, s, coup[at], halo1_c[s])
                joint[s, 1] = link(mirror, s, halo1_c[s], halo_c[s])
                level = halo_part[s] + wider(radii[1], nang) * (
                    joint[s, 1] * halo_b[s].astype(F32)
                )
                seen = level.astype(BF16)
                rows[own + s] = seen
                rows[own + sides + s] = halo_b[s]
            value = full[at] + scale * (joint[s, 0] * seen.astype(F32))
            full[at] = value
            rows[at] = value.astype(BF16)
        if n == 2:
            block[...] = rows[:own]
    count = own + sides * (n - 1)

    @pl.loop(0, nquad // STEP)
    def _(qi):
        cols = pl.ds(pl.multiple_of(qi * STEP, STEP), STEP)
        if n == 1:
            pltpu.make_async_copy(basis_hbm.at[:, cols], basis.at[:, cols], sems.at[qi]).wait()
        grid = jnp.dot(
            rows[...].reshape(count * nrad, nang), basis[:, cols], preferred_element_type=F32
        )
        prod = grid.reshape(count, nrad, STEP) * pot[:, cols][None]
        scaled[:, cols] = prod.astype(BF16).reshape(count * nrad, STEP)

    factor = wider(radii[0], STEP)
    damp = wider(radii[1], STEP)

    @pl.loop(0, nang // STEP)
    def _(ji):
        cols = pl.ds(pl.multiple_of(ji * STEP, STEP), STEP)
        ang = lax.dot_general(
            scaled[...], basis[cols, :], NT, preferred_element_type=F32
        ).reshape(count, nrad, STEP)

        def local(i, hat, value):
            kin = jnp.dot(kin_ref[...], rows[i, :, cols], preferred_element_type=F32)
            return ang[i] + kin + wider(hat, STEP) * factor * value

        for i in range(own):
            value = rows[i, :, cols].astype(F32) if n == 1 else full[i, :, cols]
            total = local(i, khat[i], value)
            if i + 1 < own:
                total += chain[i, :, cols] * rows[i + 1, :, cols].astype(F32)
            if i > 0:
                total += chain[i - 1, :, cols] * rows[i - 1, :, cols].astype(F32)
            if n == 1:
                new_ref[i, :, cols] = damp * total
            else:
                before = first_b if n == 2 else first_f
                new_ref[i, :, cols] = damp * (
                    2.0 * total - damp * before[i, :, cols].astype(F32)
                )
        for s in range(sides if n > 1 else 0):
            at = edge_of[s]
            i = own + s
            hat = halo_k[s] if n == 2 else halo1_k[s]
            total = local(i, hat, rows[i, :, cols].astype(F32))
            edge_b = first_b if n == 2 else level1_b
            total += joint[s, 0, :, cols] * edge_b[at, :, cols].astype(F32)
            if n == 2:
                part_h[s, :, cols] = damp * total
                continue
            before = halo1_b[s, :, cols].astype(F32)
            part_h[s, :, cols] = damp * (2.0 * total - damp * before)
            i = own + sides + s
            total = local(i, halo_k[s], rows[i, :, cols].astype(F32))
            total += joint[s, 1, :, cols] * before
            part_hh[s, :, cols] = damp * total


def close(dims, sides, nchan, *refs):
    own, nslab, slab, nang, nquad, mirror = dims
    nrad = nslab * slab
    raw, refs = refs[:sides], refs[sides:]
    part, part_h, part_hh, halo1_c, halo2_c, coup, radii = refs[:7]
    rad_ref, vib_ref, proj_ref, out_ref, final = refs[7:]
    base = nang // LANES * slab
    damp = wider(radii[1], nang)
    for i in range(own):
        final[i] = part[i].astype(BF16)
    for s in range(sides):
        at = 0 if s == 0 else own - 1
        far = rows_in(raw[s], 0, nslab, slab, nang, 0).astype(F32)
        far_c, _ = small_in(raw[s], 0, base, nang)
        value = part_hh[s] + damp * (link(mirror, s, halo2_c[s], far_c) * far)
        value = value.astype(BF16).astype(F32)
        value = part_h[s] + 2.0 * damp * (link(mirror, s, halo1_c[s], halo2_c[s]) * value)
        value = value.astype(BF16).astype(F32)
        term = 2.0 * damp * (link(mirror, s, coup[at], halo1_c[s]) * value)
        fixed = (part[at] if s == 0 or own > 1 else fixed) + term
        final[at] = fixed.astype(BF16)

    chan = nchan // nslab
    pieces = -(-chan // LANES)
    vib = lax.axis_index("hl") * nslab + lax.axis_index("rad")
    rows_at = lax.broadcasted_iota(jnp.int32, (nrad, chan), 0)
    for m in range(nslab):
        cols = slice(m * chan, (m + 1) * chan)
        table = lax.dot_general(
            final[...].reshape(own * nrad, nang),
            proj_ref[cols, :],
            NT,
            preferred_element_type=F32,
        ).reshape(own, nrad, chan)
        hit = (rows_at == rad_ref[:, cols]) & (vib_ref[:, cols] == vib)
        for i in range(own):
            amp = jnp.sum(jnp.where(hit, table[i], 0.0), axis=0, keepdims=True)
            if pieces * LANES > chan:
                amp = jnp.concatenate([amp, jnp.zeros((1, pieces * LANES - chan), F32)], axis=1)
            high = amp.astype(BF16).astype(F32)
            tile = [
                half[:, p * LANES : (p + 1) * LANES]
                for half in (high, amp - high)
                for p in range(pieces)
            ]
            if len(tile) < SMALL:
                tile.append(jnp.zeros((SMALL - len(tile), LANES), F32))
            to = place(mirror, own, i) * nslab + m
            out_ref[to, base : base + SMALL, :] = jnp.concatenate(tile, axis=0).astype(BF16)
            for t in range(nang // LANES):
                out_ref[to, t * slab : (t + 1) * slab, :] = final[
                    i, m * slab : (m + 1) * slab, t * LANES : (t + 1) * LANES
                ]


def per_device(
    psi_start,
    potential,
    basis,
    kinetic,
    radial_factor,
    damping,
    coupling,
    helicity,
    chan_rad,
    chan_vib,
    projector,
):
    _, slab, nvib, nang = psi_start.shape
    nquad = basis.shape[1]
    nchan = projector.shape[0]
    groups = lax.axis_size("g")
    own = lax.axis_size("hl")
    nslab = lax.axis_size("rad")
    blocks = groups * own
    group = lax.axis_index("g")
    nrad = nslab * slab
    share = nquad // own
    chunks = (nang + share) // WIDE
    height = (nang + share) // LANES * slab + SMALL
    shape = jax.ShapeDtypeStruct

    send = pl.pallas_call(
        functools.partial(pack, (slab, nvib, nang, share, blocks)),
        out_shape=shape((nvib, height, LANES), BF16),
        in_specs=[HBM] * 3 + [VMEM] + [HBM] * 2,
        out_specs=HBM,
        scratch_shapes=[
            pltpu.VMEM((chunks, slab * nvib, WIDE), F32),
            pltpu.VMEM((nvib, height, LANES), BF16),
            pltpu.VMEM((1, nang), BF16),
            pltpu.VMEM((1, slab), F32),
            pltpu.VMEM((1, slab), F32),
            pltpu.SemaphoreType.DMA((chunks,)),
            pltpu.SemaphoreType.DMA((chunks,)),
            pltpu.SemaphoreType.DMA((3,)),
        ],
        compiler_params=PARAMS,
        name="pack",
    )(
        in_hbm(psi_start.reshape(slab * nvib, nang)),
        in_hbm(potential.reshape(slab * nvib, nquad)),
        in_hbm(coupling),
        helicity[None],
        in_hbm(radial_factor[None]),
        in_hbm(damping[None]),
    )
    message = lax.all_to_all(send, ("hl", "rad"), 0, 0, tiled=True)

    mirror = groups == 2 and own >= ITERS
    sides = 1 if mirror else 2
    rows = message[:, share // LANES * slab :]
    halos = []
    for j in range(ITERS):
        if mirror:
            first = jnp.where(group == 0, own - 1 - j, j) * nslab
            part = lax.dynamic_slice_in_dim(rows, first, nslab, 0)
            halos.append([lax.ppermute(part, "g", [(0, 1), (1, 0)])])
            continue
        away, at = j // own + 1, j % own
        upper = rows[at * nslab : (at + 1) * nslab]
        lower = rows[(own - 1 - at) * nslab : (own - at) * nslab]
        up = [(i, i + away) for i in range(groups - away)]
        halos.append(
            [
                lax.ppermute(lower, "g", up),
                lax.ppermute(upper, "g", [(i, j) for j, i in up]),
            ]
        )

    full_type = shape((own, nrad, nang), F32)
    block_type = shape((own, nrad, nang), BF16)
    side_type = shape((sides, nrad, nang), F32)
    halo_type = shape((sides, nrad, nang), BF16)
    coup_type = shape((sides, 1, nang), F32)
    hat_type = shape((sides, 1, LANES), F32)
    dims = (own, nslab, slab, nang, nquad, mirror)

    def run(n, operands, specs, outs, scratch):
        count = own + sides * (n - 1)
        return pl.pallas_call(
            functools.partial(advance, dims, sides, n),
            out_shape=outs,
            in_specs=specs,
            out_specs=[VMEM] * len(outs),
            scratch_shapes=scratch[:-1]
            + [
                pltpu.VMEM((count, nrad, nang), BF16),
                pltpu.VMEM((count * nrad, nquad), BF16),
                scratch[-1],
            ],
            compiler_params=PARAMS,
            cost_estimate=pl.CostEstimate(
                flops=4 * count * nrad * nang * nquad,
                bytes_accessed=8 * 1024 * 1024,
                transcendentals=0,
            ),
            name=f"advance{n}",
        )(*operands)

    new, first_b, basis, pot, radii, khat, coup, chain = run(
        1,
        [message, in_hbm(basis), kinetic],
        [VMEM, HBM, VMEM],
        [
            full_type,
            block_type,
            shape(basis.shape, BF16),
            shape((nrad, nquad), F32),
            shape((2, nrad, LANES), F32),
            shape((own, 1, LANES), F32),
            shape((own, 1, nang), F32),
            shape((max(own - 1, 1), 1, nang), F32),
        ],
        [pltpu.SemaphoreType.DMA((nquad // STEP,))],
    )
    common = [basis, kinetic, pot, radii, khat, coup, chain]
    joint = pltpu.VMEM((sides, 2, 1, nang), F32)
    operands = halos[0] + common + [new, first_b]
    first_f, level1_b, new, halo_part, halo1_b, halo1_c, halo1_k = run(
        2,
        operands,
        [VMEM] * len(operands),
        [full_type, block_type, full_type, side_type, halo_type, coup_type, hat_type],
        [joint],
    )
    operands = (
        halos[1]
        + common
        + [new, first_b, first_f, halo_part, halo1_b, halo1_c, halo1_k, level1_b]
    )
    new, halo_part, far_part, halo2_c = run(
        3,
        operands,
        [VMEM] * len(operands),
        [full_type, side_type, side_type, coup_type],
        [
            pltpu.VMEM((own, nrad, nang), F32),
            pltpu.VMEM((sides, nrad, nang), BF16),
            pltpu.VMEM((sides, 1, LANES), F32),
            joint,
        ],
    )
    operands = halos[2] + [new, halo_part, far_part, halo1_c, halo2_c, coup, radii]
    operands += [chan_rad[None], chan_vib[None], projector]
    back = pl.pallas_call(
        functools.partial(close, dims, sides, nchan),
        out_shape=shape((own * nslab, nang // LANES * slab + SMALL, LANES), BF16),
        in_specs=[VMEM] * len(operands),
        out_specs=VMEM,
        scratch_shapes=[pltpu.VMEM((own, nrad, nang), BF16)],
        compiler_params=PARAMS,
        name="close",
    )(*operands)

    home = lax.all_to_all(back, ("hl", "rad"), 0, 0, tiled=True)
    chan = nchan // nslab
    psi_final, amplitude = pl.pallas_call(
        functools.partial(unpack, (slab, nvib, nang, -(-chan // LANES))),
        out_shape=[shape((slab * nvib, nang), F32), shape((1, chan), F32)],
        in_specs=[VMEM],
        out_specs=[HBM, VMEM],
        scratch_shapes=[
            pltpu.VMEM((slab * nvib, nang), F32),
            pltpu.SemaphoreType.DMA((nang // STEP,)),
        ],
        compiler_params=PARAMS,
        name="unpack",
    )(home)
    return (psi_final.reshape(1, slab, nvib, nang), amplitude)


def solution(mesh):
    nhel, nrad = mesh.shape["hel"], mesh.shape["rad"]

    def run(*args):
        nvib = args[0].shape[2]
        groups = nhel * nrad // nvib
        fine = Mesh(mesh.devices.reshape(groups, nhel // groups, nrad), ("g", "hl", "rad"))
        hel = ("g", "hl")
        placed = (
            P(hel, "rad", None, None),
            P("rad", None, None),
            P(),
            P(),
            P("rad"),
            P("rad"),
            P(hel, None),
            P(hel),
            P(),
            P(),
            P(),
        )
        return jax.shard_map(
            per_device,
            mesh=fine,
            in_specs=placed,
            out_specs=(P(hel, "rad", None, None), P(hel, "rad")),
            check_vma=False,
        )(*args)

    return run
```

time: 58.2 us -> 56.7 us (0.974)
  waiting for transfers between devices: 16.9 us -> 14.4 us
  blocking collectives: 13.7 us -> 12.1 us
  starting transfers between devices: 10.4 us -> 11.9 us
  Pallas kernels: 15.4 us -> 16.5 us
    ppermute x3, waiting for transfers between devices: 5.38 us -> 2.8 us  [per_device(): halos.append([lax.ppermute(part, 'g', [(0, 1), (1, 0)])])]
    all_to_all x1, blocking collectives: 13.7 us -> 12.1 us  [per_device(): home = lax.all_to_all(back, ('hl', 'rad'), 0, 0, tiled=True)]
    ppermute x3, starting transfers between devices: 4.11 us -> 5.59 us  [per_device(): halos.append([lax.ppermute(part, 'g', [(0, 1), (1, 0)])])]
    pallas_call x6 -> x4, Pallas kernels: 11.1 us -> 12.3 us  [the longest x3 11.5 us: run(): pl.pallas_call(functools.partial(advance, dims, sides, n), out_shape=outs...]
  transfers between devices with their start and end apart: 4 -> 4, of which waited for: 4 -> 2; matrix products, arithmetic and copies ran while one was open for 0% -> 0% of each run, Pallas kernels for 18% -> 20%
where the time goes in v5:
time: 56.7 us; the launch traced here: 56.4 us
  Pallas kernels  16.5 us (29%)
  waiting for transfers between devices  14.4 us (25%)
  blocking collectives  12.1 us (21%)
  starting transfers between devices  11.9 us (21%)
  between operations  1.42 us (3%)
    all_to_all x1, blocking collectives, per_device(): home = lax.all_to_all(back, ('hl', 'rad'), 0, 0, tiled=True)  12.1 us
    all_to_all x1, waiting for transfers between devices, per_device(): message = lax.all_to_all(send, ('hl', 'rad'), 0, 0, tiled=True)  11.6 us
    pallas_call x3, Pallas kernels, run(): pl.pallas_call(functools.partial(advance, dims, sides, n), out_shape=outs...  11.5 us
    all_to_all x1, starting transfers between devices, per_device(): message = lax.all_to_all(send, ('hl', 'rad'), 0, 0, tiled=True)  6.33 us
    ppermute x3, starting transfers between devices, per_device(): halos.append([lax.ppermute(part, 'g', [(0, 1), (1, 0)])])  5.59 us
    ppermute x3, waiting for transfers between devices, per_device(): halos.append([lax.ppermute(part, 'g', [(0, 1), (1, 0)])])  2.8 us
    pallas_call x1, Pallas kernels, per_device(): pl.pallas_call(functools.partial(pack, (slab, nvib, nang, share, blocks))...  2.63 us
    pallas_call x1, Pallas kernels, per_device(): pl.pallas_call(functools.partial(unpack, (slab, nvib, nang, -(-chan // LA...  1.65 us
  transfers between devices with their start and end apart: 4, of which 2 were waited for; matrix products, arithmetic and copies ran while one was open for 0% of the time, Pallas kernels for 20%

profile of v5, /device:TPU:0, one launch (start us, length us, event | category | flops | bytes accessed | tf_op | source)
XLA Modules:
  0.0 56.4 jit_solution(15085889817798312485)
XLA Ops:
  1.3 0.0 copy-start.3
  1.3 2.6 %pack.1 = bf16[16,152,128]{2,1,0:T(8,128)(2,1)} custom-call(f32[256,768]{1,0:T(8,128)} %bitcast.12, f32[256,1536]{1,0:T(8,128)} %bitcast.11, bf16[1,768]{1,0:T(2,128)(2,1)} %coup_ref.1, s32[1,1]{1,0:T(1,128)} %bitcast.8.hel_ref, f32[1,16]{1,0:T(1,128)} %bitcast.13, f32[1,16]{1,0:T(1,128)} %bitcast.14), custom_call_target="tpu_custom_call" | custom-call | tf_op jit(solution)/shard_map/pack/pallas_call | solution.py:400
  3.9 6.3 %all-to-all-start = ((bf16[16,152,128]{2,1,0:T(8,128)(2,1)}), bf16[16,152,128]{2,1,0:T(8,128)(2,1)S(1)}, u32[]{:S(2)}, u32[]{:S(2)}) async-start(bf16[16,152,128]{2,1,0:T(8,128)(2,1)} %pack.1), calls=%async_computation | async-start | bytes 1245184 | tf_op jit(solution)/shard_map/all_to_all | solution.py:425
  10.3 11.6 %all-to-all-done.refs_0_ = bf16[16,152,128]{2,1,0:T(8,128)(2,1)S(1)} async-done(((bf16[16,152,128]{2,1,0:T(8,128)(2,1)}), bf16[16,152,128]{2,1,0:T(8,128)(2,1)S(1)}, u32[]{:S(2)}, u32[]{:S(2)}) %all-to-all-start) | async-done | bytes 622624 | tf_op jit(solution)/shard_map/all_to_all | solution.py:425
  21.9 2.7 %collective-permute-start.2 = (bf16[4,104,128]{2,1,0:T(8,128)(2,1)S(1)}, bf16[4,104,128]{2,1,0:T(8,128)(2,1)S(1)}, u32[]{:S(2)}, u32[]{:S(2)}) collective-permute-start(bf16[4,104,128]{2,1,0:T(8,128)(2,1)S(1)} %get-tuple-element.44), channel_id=1, source_target_pairs={{0,16},{16,0},{1,17},{17,1},{2,18},{18,2},{3,19},{19,3},{4,20},{20... | collective-permute-start | bytes 319496 | tf_op jit(solution)/shard_map/ppermute | solution.py:435
  24.6 0.3 collective-permute-start.1
  24.9 2.6 %collective-permute-start = (bf16[4,104,128]{2,1,0:T(8,128)(2,1)S(1)}, bf16[4,104,128]{2,1,0:T(8,128)(2,1)S(1)}, u32[]{:S(2)}, u32[]{:S(2)}) collective-permute-start(bf16[4,104,128]{2,1,0:T(8,128)(2,1)S(1)} %get-tuple-element.46), channel_id=1, source_target_pairs={{0,16},{16,0},{1,17},{17,1},{2,18},{18,2},{3,19},{19,3},{4,20},{20... | collective-permute-start | bytes 319496 | tf_op jit(solution)/shard_map/ppermute | solution.py:435
  27.5 0.0 copy-done.3
  27.5 4.1 %advance1.1 = (f32[4,64,768]{2,1,0:T(8,128)S(1)}, bf16[4,64,768]{2,1,0:T(8,128)(2,1)S(1)}, bf16[768,1536]{1,0:T(8,128)(2,1)S(1)}, f32[64,1536]{1,0:T(8,128)S(1)}...) custom-call(bf16[16,152,128]{2,1,0:T(8,128)(2,1)S(1)} %all-to-all-do, ...), custom_call_target="tpu_custom_call" | custom-call | flops 1207959552 | bytes 8388608 | tf_op jit(solution)/shard_map/advance1/pallas_call | solution.py:458
  31.6 2.8 %collective-permute-done.2.refs_0_ = bf16[4,104,128]{2,1,0:T(8,128)(2,1)S(1)} collective-permute-done((bf16[4,104,128]{2,1,0:T(8,128)(2,1)S(1)}, bf16[4,104,128]{2,1,0:T(8,128)(2,1)S(1)}, u32[]{:S(2)}, u32[]{:S(2)}) %collective-permute-start.2) | collective-permute-done | bytes 106528 | tf_op jit(solution)/shard_map/ppermute | solution.py:435
  34.4 3.5 %advance2.1 = (f32[4,64,768]{2,1,0:T(8,128)S(1)}, bf16[4,64,768]{2,1,0:T(8,128)(2,1)S(1)}, f32[4,64,768]{2,1,0:T(8,128)S(1)}, f32[1,64,768]{2,1,0:T(8,128)S(1)},...) custom-call(bf16[4,104,128]{2,1,0:T(8,128)(2,1)S(1)} %collective-permute-done.2.refs_0_, ...), custom_call_target="tpu_custom_call" | custom-call | flops 1509949440 | bytes 8388608 | tf_op jit(solution)/shard_map/advance2/pallas_call | solution.py:458
  37.9 0.0 collective-permute-done.1.refs_0_
  37.9 0.0 copy-start
  37.9 0.0 copy-start.1
  38.0 0.0 copy-start.2
  38.0 3.9 %advance3.1 = (f32[4,64,768]{2,1,0:T(8,128)S(1)}, f32[1,64,768]{2,1,0:T(8,128)S(1)}, f32[1,64,768]{2,1,0:T(8,128)S(1)}, f32[1,1,768]{2,1,0:T(1,128)S(1)}) custom-call(bf16[4,104,128]{2,1,0:T(8,128)(2,1)S(1)} %collective-permute-done.1.refs_0_, bf16[768,1536]{1,0:T(8,128)(2,1)S(1)} %get-tuple-element.23.refs_1_, bf16[64,64]{1,0:T(8,128)(2,1)S(1)} %copy-done.3, ...), custom_call_target="tpu_custom_call" | custom-call | flops 1811939328 | bytes 8388608 | tf_op jit(solution)/shard_map/advance3/pallas_call | solution.py:458
  41.9 0.0 collective-permute-done.refs_0_
  41.9 0.0 copy-done
  41.9 0.0 copy-done.1
  41.9 0.0 copy-done.2
  42.0 0.7 %close.1 = bf16[16,104,128]{2,1,0:T(8,128)(2,1)S(1)} custom-call(bf16[4,104,128]{2,1,0:T(8,128)(2,1)S(1)} %collective-permute-done.refs_0_, f32[4,64,768]{2,1,0:T(8,128)S(1)} %get-tuple-element.38.refs_1_, f32[1,64,768]{2,1,0:T(8,128)S(1)} %get-tuple-element.39.refs_2_, f32[1,64,768]{2,1,0:T(8,128)S(1)} %get-tuple-element.40.refs_3_, ...), custom_call_target="tpu_custom_call" | custom-call | tf_op jit(solution)/shard_map/close/pallas_call | solution.py:523
  42.7 12.1 %all_to_all.10.msg_ref = bf16[16,104,128]{2,1,0:T(8,128)(2,1)S(1)} all-to-all(bf16[16,104,128]{2,1,0:T(8,128)(2,1)S(1)} %close.1), channel_id=1, replica_groups=mesh['g'=2,'hl'=4,'rad'=4] {'hl','rad'}, dimensions={0} | all-to-all | bytes 851968 | tf_op jit(solution)/shard_map/all_to_all | solution.py:533
  54.8 1.7 %unpack.1 = (f32[256,768]{1,0:T(8,128)}, f32[1,256]{1,0:T(1,128)}) custom-call(bf16[16,104,128]{2,1,0:T(8,128)(2,1)S(1)} %all_to_all.10.msg_ref), custom_call_target="tpu_custom_call" | custom-call | tf_op jit(solution)/shard_map/unpack/pallas_call | solution.py:535
  (2 shorter events, 0.1 us)
Async XLA Ops:
  1.3 26.2 %copy-start.3 = (bf16[64,64]{1,0:T(8,128)(2,1)S(1)}, bf16[64,64]{1,0:T(8,128)(2,1)}, u32[]{:S(2)}) copy-start(bf16[64,64]{1,0:T(8,128)(2,1)} %refs_2_.5) | copy-start | bytes 24580
  3.9 17.9 %all-to-all-start = ((bf16[16,152,128]{2,1,0:T(8,128)(2,1)}), bf16[16,152,128]{2,1,0:T(8,128)(2,1)S(1)}, u32[]{:S(2)}, u32[]{:S(2)}) async-start(bf16[16,152,128]{2,1,0:T(8,128)(2,1)} %pack.1), calls=%async_computation | async-start | bytes 1245184 | tf_op jit(solution)/shard_map/all_to_all | solution.py:425
  21.9 12.5 %collective-permute-start.2 = (bf16[4,104,128]{2,1,0:T(8,128)(2,1)S(1)}, bf16[4,104,128]{2,1,0:T(8,128)(2,1)S(1)}, u32[]{:S(2)}, u32[]{:S(2)}) collective-permute-start(bf16[4,104,128]{2,1,0:T(8,128)(2,1)S(1)} %get-tuple-element.44), channel_id=1, source_target_pairs={{0,16},{16,0},{1,17},{17,1},{2,18},{18,2},{3,19},{19,3},{4,20},{20... | collective-permute-start | bytes 319496 | tf_op jit(solution)/shard_map/ppermute | solution.py:435
  24.6 13.4 %collective-permute-start.1 = (bf16[4,104,128]{2,1,0:T(8,128)(2,1)S(1)}, bf16[4,104,128]{2,1,0:T(8,128)(2,1)S(1)}, u32[]{:S(2)}, u32[]{:S(2)}) collective-permute-start(bf16[4,104,128]{2,1,0:T(8,128)(2,1)S(1)} %get-tuple-element.45), channel_id=1, source_target_pairs={{0,16},{16,0},{1,17},{17,1},{2,18},{18,2},{3,19},{19,3},{4,20},{20... | collective-permute-start | bytes 319496 | tf_op jit(solution)/shard_map/ppermute | solution.py:435
  24.9 17.0 %collective-permute-start = (bf16[4,104,128]{2,1,0:T(8,128)(2,1)S(1)}, bf16[4,104,128]{2,1,0:T(8,128)(2,1)S(1)}, u32[]{:S(2)}, u32[]{:S(2)}) collective-permute-start(bf16[4,104,128]{2,1,0:T(8,128)(2,1)S(1)} %get-tuple-element.46), channel_id=1, source_target_pairs={{0,16},{16,0},{1,17},{17,1},{2,18},{18,2},{3,19},{19,3},{4,20},{20... | collective-permute-start | bytes 319496 | tf_op jit(solution)/shard_map/ppermute | solution.py:435
  37.9 4.0 %copy-start = (bf16[1024,768]{1,0:T(8,128)(2,1)S(1)}, bf16[1024,768]{1,0:T(8,128)(2,1)}, u32[]{:S(2)}) copy-start(bf16[1024,768]{1,0:T(8,128)(2,1)} %refs_10_.1) | copy-start | bytes 4718596
  37.9 4.0 %copy-start.1 = (s32[1024]{0:T(1024)S(1)}, s32[1024]{0:T(1024)}, u32[]{:S(2)}) copy-start(s32[1024]{0:T(1024)} %param.19) | copy-start | bytes 12292
  38.0 4.0 %copy-start.2 = (s32[1024]{0:T(1024)S(1)}, s32[1024]{0:T(1024)}, u32[]{:S(2)}) copy-start(s32[1024]{0:T(1024)} %param.20) | copy-start | bytes 12292

commit v6 on v5

--- a/solution.py
+++ b/solution.py
@@ -168,6 +168,12 @@
     if mirror:
         return jnp.where(lax.axis_index("g") == 0, own - 1 - i, i)
     return i
+
+
+def edge_block(mirror, own, side, j):
+    if mirror:
+        return place(mirror, own, j)
+    return own - 1 - j % own if side == 0 else j % own
 
 
 def unfold(dims, msg_ref, src, pot, radii, khat, coup):
@@ -204,11 +210,14 @@
     own, nslab, slab, nang, nquad, mirror = dims
     nrad = nslab * slab
     refs = list(refs)
+    share = nquad // own
+    top = share // LANES * slab
     take = lambda count: [refs.pop(0) for _ in range(count)]
     edge_of = [0, own - 1]
     if n == 1:
         msg_ref, basis_hbm, kin_ref = take(3)
         new_ref, src, basis, pot, radii, khat, coup, chain = take(8)
+        sends = take(sides)
         rows, scaled, sems = take(3)
         for qi in range(nquad // STEP):
             cols = pl.ds(qi * STEP, STEP)
@@ -223,8 +232,9 @@
         scale = wider(radii[1] if n == 2 else 2.0 * radii[1], nang)
         base = nang // LANES * slab
         if n == 2:
-            part, first_b = take(2)
+            part, first_b, msg_ref = take(3)
             full, block, new_ref, part_h, halo_b, halo_c, halo_k = take(7)
+            sends = take(sides)
             rows, scaled, joint = take(3)
         else:
             part, first_b, first_f, halo_part, halo1_b, halo1_c, halo1_k, level1_b = take(8)
@@ -257,6 +267,11 @@
         if n == 2:
             block[...] = rows[:own]
     count = own + sides * (n - 1)
+    if n < ITERS:
+        for s in range(sides):
+            first = edge_block(mirror, own, s, n) * nslab
+            for m in range(nslab):
+                sends[s][m] = msg_ref[first + m, top:, :]
 
     @pl.loop(0, nquad // STEP)
     def _(qi):
@@ -426,24 +441,24 @@
 
     mirror = groups == 2 and own >= ITERS
     sides = 1 if mirror else 2
+    send_type = shape((nslab, height - share // LANES * slab, LANES), BF16)
+
+    def cross(parts, j):
+        if mirror:
+            return [lax.ppermute(parts[0], "g", [(0, 1), (1, 0)])]
+        away = j // own + 1
+        up = [(i, i + away) for i in range(groups - away)]
+        return [
+            lax.ppermute(parts[0], "g", up),
+            lax.ppermute(parts[1], "g", [(i, j) for j, i in up]),
+        ]
+
     rows = message[:, share // LANES * slab :]
-    halos = []
-    for j in range(ITERS):
-        if mirror:
-            first = jnp.where(group == 0, own - 1 - j, j) * nslab
-            part = lax.dynamic_slice_in_dim(rows, first, nslab, 0)
-            halos.append([lax.ppermute(part, "g", [(0, 1), (1, 0)])])
-            continue
-        away, at = j // own + 1, j % own
-        upper = rows[at * nslab : (at + 1) * nslab]
-        lower = rows[(own - 1 - at) * nslab : (own - at) * nslab]
-        up = [(i, i + away) for i in range(groups - away)]
-        halos.append(
-            [
-                lax.ppermute(lower, "g", up),
-                lax.ppermute(upper, "g", [(i, j) for j, i in up]),
-            ]
-        )
+    sent = [
+        lax.dynamic_slice_in_dim(rows, edge_block(mirror, own, s, 0) * nslab, nslab, 0)
+        for s in range(sides)
+    ]
+    halo = cross(sent, 0)
 
     full_type = shape((own, nrad, nang), F32)
     block_type = shape((own, nrad, nang), BF16)
@@ -475,7 +490,7 @@
             name=f"advance{n}",
         )(*operands)
 
-    new, first_b, basis, pot, radii, khat, coup, chain = run(
+    new, first_b, basis, pot, radii, khat, coup, chain, *sent = run(
         1,
         [message, in_hbm(basis), kinetic],
         [VMEM, HBM, VMEM],
@@ -488,24 +503,28 @@
             shape((own, 1, LANES), F32),
             shape((own, 1, nang), F32),
             shape((max(own - 1, 1), 1, nang), F32),
-        ],
+        ]
+        + [send_type] * sides,
         [pltpu.SemaphoreType.DMA((nquad // STEP,))],
     )
     common = [basis, kinetic, pot, radii, khat, coup, chain]
     joint = pltpu.VMEM((sides, 2, 1, nang), F32)
-    operands = halos[0] + common + [new, first_b]
-    first_f, level1_b, new, halo_part, halo1_b, halo1_c, halo1_k = run(
+    operands = halo + common + [new, first_b, message]
+    halo = cross(sent, 1)
+    first_f, level1_b, new, halo_part, halo1_b, halo1_c, halo1_k, *sent = run(
         2,
         operands,
         [VMEM] * len(operands),
-        [full_type, block_type, full_type, side_type, halo_type, coup_type, hat_type],
+        [full_type, block_type, full_type, side_type, halo_type, coup_type, hat_type]
+        + [send_type] * sides,
         [joint],
     )
     operands = (
-        halos[1]
+        halo
         + common
         + [new, first_b, first_f, halo_part, halo1_b, halo1_c, halo1_k, level1_b]
     )
+    halo = cross(sent, 2)
     new, halo_part, far_part, halo2_c = run(
         3,
         operands,
@@ -518,7 +537,7 @@
             joint,
         ],
     )
-    operands = halos[2] + [new, halo_part, far_part, halo1_c, halo2_c, coup, radii]
+    operands = halo + [new, halo_part, far_part, halo1_c, halo2_c, coup, radii]
     operands += [chan_rad[None], chan_vib[None], projector]
     back = pl.pallas_call(
         functools.partial(close, dims, sides, nchan),

time: 56.7 us -> 57.7 us (1.018)
  waiting for transfers between devices: 14.4 us -> 15.3 us
    ppermute x3, waiting for transfers between devices: 2.8 us -> 3.79 us  [cross(): return [lax.ppermute(parts[0], 'g', [(0, 1), (1, 0)])]]
  transfers between devices with their start and end apart: 4 -> 4, of which waited for: 2 -> 3; matrix products, arithmetic and copies ran while one was open for 0% -> 0% of each run, Pallas kernels for 20% -> 20%
where the time goes in v6:
time: 57.7 us; the launch traced here: 57.4 us
  Pallas kernels  16.6 us (29%)
  waiting for transfers between devices  15.3 us (27%)
  blocking collectives  12.1 us (21%)
  starting transfers between devices  11.9 us (21%)
  between operations  1.39 us (2%)
    all_to_all x1, blocking collectives, per_device(): home = lax.all_to_all(back, ('hl', 'rad'), 0, 0, tiled=True)  12.1 us
    pallas_call x3, Pallas kernels, run(): pl.pallas_call(functools.partial(advance, dims, sides, n), out_shape=outs...  11.6 us
    all_to_all x1, waiting for transfers between devices, per_device(): message = lax.all_to_all(send, ('hl', 'rad'), 0, 0, tiled=True)  11.6 us
    all_to_all x1, starting transfers between devices, per_device(): message = lax.all_to_all(send, ('hl', 'rad'), 0, 0, tiled=True)  6.33 us
    ppermute x3, starting transfers between devices, cross(): return [lax.ppermute(parts[0], 'g', [(0, 1), (1, 0)])]  5.57 us
    ppermute x3, waiting for transfers between devices, cross(): return [lax.ppermute(parts[0], 'g', [(0, 1), (1, 0)])]  3.79 us
    pallas_call x1, Pallas kernels, per_device(): pl.pallas_call(functools.partial(pack, (slab, nvib, nang, share, blocks))...  2.63 us
    pallas_call x1, Pallas kernels, per_device(): pl.pallas_call(functools.partial(unpack, (slab, nvib, nang, -(-chan // LA...  1.65 us
  transfers between devices with their start and end apart: 4, of which 3 were waited for; matrix products, arithmetic and copies ran while one was open for 0% of the time, Pallas kernels for 20%

profile of v6, /device:TPU:0, one launch (start us, length us, event | category | flops | bytes accessed | tf_op | source)
XLA Modules:
  0.0 57.4 jit_solution(9033599807695056720)
XLA Ops:
  1.3 0.0 copy-start.3
  1.3 2.6 %pack.1 = bf16[16,152,128]{2,1,0:T(8,128)(2,1)} custom-call(f32[256,768]{1,0:T(8,128)} %bitcast.12, f32[256,1536]{1,0:T(8,128)} %bitcast.11, bf16[1,768]{1,0:T(2,128)(2,1)} %coup_ref.1, s32[1,1]{1,0:T(1,128)} %bitcast.8.hel_ref, f32[1,16]{1,0:T(1,128)} %bitcast.13, f32[1,16]{1,0:T(1,128)} %bitcast.14), custom_call_target="tpu_custom_call" | custom-call | tf_op jit(solution)/shard_map/pack/pallas_call | solution.py:415
  3.9 6.3 %all-to-all-start = ((bf16[16,152,128]{2,1,0:T(8,128)(2,1)}), bf16[16,152,128]{2,1,0:T(8,128)(2,1)S(1)}, u32[]{:S(2)}, u32[]{:S(2)}) async-start(bf16[16,152,128]{2,1,0:T(8,128)(2,1)} %pack.1), calls=%async_computation | async-start | bytes 1245184 | tf_op jit(solution)/shard_map/all_to_all | solution.py:440
  10.3 11.6 %all-to-all-done.refs_0_.refs_10_ = bf16[16,152,128]{2,1,0:T(8,128)(2,1)S(1)} async-done(((bf16[16,152,128]{2,1,0:T(8,128)(2,1)}), bf16[16,152,128]{2,1,0:T(8,128)(2,1)S(1)}, u32[]{:S(2)}, u32[]{:S(2)}) %all-to-all-start) | async-done | bytes 622624 | tf_op jit(solution)/shard_map/all_to_all | solution.py:440
  21.9 2.7 %collective-permute-start = (bf16[4,104,128]{2,1,0:T(8,128)(2,1)S(1)}, bf16[4,104,128]{2,1,0:T(8,128)(2,1)S(1)}, u32[]{:S(2)}, u32[]{:S(2)}) collective-permute-start(bf16[4,104,128]{2,1,0:T(8,128)(2,1)S(1)} %constant_dynamic-slice_fusion), channel_id=1, source_target_pairs={{0,16},{16,0},{1,17},{17,1},{2,18},{18,2},{3,19},{19,3},{4,20},{20... | collective-permute-start | bytes 319496 | tf_op jit(solution)/shard_map/ppermute | solution.py:448
  24.6 0.0 copy-done.3
  24.6 4.1 %advance1.1 = (f32[4,64,768]{2,1,0:T(8,128)S(1)}, bf16[4,64,768]{2,1,0:T(8,128)(2,1)S(1)}, bf16[768,1536]{1,0:T(8,128)(2,1)S(1)}, f32[64,1536]{1,0:T(8,128)S(1)}...) custom-call(bf16[16,152,128]{2,1,0:T(8,128)(2,1)S(1)} %all-to-all-do, ...), custom_call_target="tpu_custom_call" | custom-call | flops 1207959552 | bytes 8388608 | tf_op jit(solution)/shard_map/advance1/pallas_call | solution.py:473
  28.7 0.4 collective-permute-start.2
  29.1 0.2 collective-permute-done.refs_0_
  29.3 3.5 %advance2.1 = (f32[4,64,768]{2,1,0:T(8,128)S(1)}, bf16[4,64,768]{2,1,0:T(8,128)(2,1)S(1)}, f32[4,64,768]{2,1,0:T(8,128)S(1)}, f32[1,64,768]{2,1,0:T(8,128)S(1)},...) custom-call(bf16[4,104,128]{2,1,0:T(8,128)(2,1)S(1)} %collective-per, ...), custom_call_target="tpu_custom_call" | custom-call | flops 1509949440 | bytes 8388608 | tf_op jit(solution)/shard_map/advance2/pallas_call | solution.py:473
  32.8 2.5 %collective-permute-start.1 = (bf16[4,104,128]{2,1,0:T(8,128)(2,1)S(1)}, bf16[4,104,128]{2,1,0:T(8,128)(2,1)S(1)}, u32[]{:S(2)}, u32[]{:S(2)}) collective-permute-start(bf16[4,104,128]{2,1,0:T(8,128)(2,1)S(1)} %get-tuple-element.33), channel_id=1, source_target_pairs={{0,16},{16,0},{1,17},{17,1},{2,18},{18,2},{3,19},{19,3},{4,20},{20... | collective-permute-start | bytes 319496 | tf_op jit(solution)/shard_map/ppermute | solution.py:448
  35.3 3.6 %collective-permute-done.2.refs_0_ = bf16[4,104,128]{2,1,0:T(8,128)(2,1)S(1)} collective-permute-done((bf16[4,104,128]{2,1,0:T(8,128)(2,1)S(1)}, bf16[4,104,128]{2,1,0:T(8,128)(2,1)S(1)}, u32[]{:S(2)}, u32[]{:S(2)}) %collective-permute-start.2) | collective-permute-done | bytes 106528 | tf_op jit(solution)/shard_map/ppermute | solution.py:448
  38.9 0.0 copy-start
  38.9 0.0 copy-start.1
  38.9 0.0 copy-start.2
  38.9 4.0 %advance3.1 = (f32[4,64,768]{2,1,0:T(8,128)S(1)}, f32[1,64,768]{2,1,0:T(8,128)S(1)}, f32[1,64,768]{2,1,0:T(8,128)S(1)}, f32[1,1,768]{2,1,0:T(1,128)S(1)}) custom-call(bf16[4,104,128]{2,1,0:T(8,128)(2,1)S(1)} %collective-permute-done.2.refs_0_, bf16[768,1536]{1,0:T(8,128)(2,1)S(1)} %get-tuple-element.25.refs_1_, bf16[64,64]{1,0:T(8,128)(2,1)S(1)} %copy-done.3, ...), custom_call_target="tpu_custom_call" | custom-call | flops 1811939328 | bytes 8388608 | tf_op jit(solution)/shard_map/advance3/pallas_call | solution.py:473
  42.9 0.0 collective-permute-done.1.refs_0_
  42.9 0.0 copy-done
  42.9 0.0 copy-done.1
  42.9 0.0 copy-done.2
  42.9 0.7 %close.1 = bf16[16,104,128]{2,1,0:T(8,128)(2,1)S(1)} custom-call(bf16[4,104,128]{2,1,0:T(8,128)(2,1)S(1)} %collective-permute-done.1.refs_0_, f32[4,64,768]{2,1,0:T(8,128)S(1)} %get-tuple-element.42.refs_1_, f32[1,64,768]{2,1,0:T(8,128)S(1)} %get-tuple-element.43.refs_2_, f32[1,64,768]{2,1,0:T(8,128)S(1)} %get-tuple-element.44.refs_3_, ...), custom_call_target="tpu_custom_call" | custom-call | tf_op jit(solution)/shard_map/close/pallas_call | solution.py:542
  43.7 12.1 %all_to_all.10.msg_ref = bf16[16,104,128]{2,1,0:T(8,128)(2,1)S(1)} all-to-all(bf16[16,104,128]{2,1,0:T(8,128)(2,1)S(1)} %close.1), channel_id=1, replica_groups=mesh['g'=2,'hl'=4,'rad'=4] {'hl','rad'}, dimensions={0} | all-to-all | bytes 851968 | tf_op jit(solution)/shard_map/all_to_all | solution.py:552
  55.7 1.7 %unpack.1 = (f32[256,768]{1,0:T(8,128)}, f32[1,256]{1,0:T(1,128)}) custom-call(bf16[16,104,128]{2,1,0:T(8,128)(2,1)S(1)} %all_to_all.10.msg_ref), custom_call_target="tpu_custom_call" | custom-call | tf_op jit(solution)/shard_map/unpack/pallas_call | solution.py:554
  (2 shorter events, 0.1 us)
Async XLA Ops:
  1.3 23.3 %copy-start.3 = (bf16[64,64]{1,0:T(8,128)(2,1)S(1)}, bf16[64,64]{1,0:T(8,128)(2,1)}, u32[]{:S(2)}) copy-start(bf16[64,64]{1,0:T(8,128)(2,1)} %refs_2_.5) | copy-start | bytes 24580
  3.9 17.9 %all-to-all-start = ((bf16[16,152,128]{2,1,0:T(8,128)(2,1)}), bf16[16,152,128]{2,1,0:T(8,128)(2,1)S(1)}, u32[]{:S(2)}, u32[]{:S(2)}) async-start(bf16[16,152,128]{2,1,0:T(8,128)(2,1)} %pack.1), calls=%async_computation | async-start | bytes 1245184 | tf_op jit(solution)/shard_map/all_to_all | solution.py:440
  21.9 7.4 %collective-permute-start = (bf16[4,104,128]{2,1,0:T(8,128)(2,1)S(1)}, bf16[4,104,128]{2,1,0:T(8,128)(2,1)S(1)}, u32[]{:S(2)}, u32[]{:S(2)}) collective-permute-start(bf16[4,104,128]{2,1,0:T(8,128)(2,1)S(1)} %constant_dynamic-slice_fusion), channel_id=1, source_target_pairs={{0,16},{16,0},{1,17},{17,1},{2,18},{18,2},{3,19},{19,3},{4,20},{20... | collective-permute-start | bytes 319496 | tf_op jit(solution)/shard_map/ppermute | solution.py:448
  28.7 10.2 %collective-permute-start.2 = (bf16[4,104,128]{2,1,0:T(8,128)(2,1)S(1)}, bf16[4,104,128]{2,1,0:T(8,128)(2,1)S(1)}, u32[]{:S(2)}, u32[]{:S(2)}) collective-permute-start(bf16[4,104,128]{2,1,0:T(8,128)(2,1)S(1)} %get-tuple-element.34), channel_id=1, source_target_pairs={{0,16},{16,0},{1,17},{17,1},{2,18},{18,2},{3,19},{19,3},{4,20},{20... | collective-permute-start | bytes 319496 | tf_op jit(solution)/shard_map/ppermute | solution.py:448
  32.8 10.1 %collective-permute-start.1 = (bf16[4,104,128]{2,1,0:T(8,128)(2,1)S(1)}, bf16[4,104,128]{2,1,0:T(8,128)(2,1)S(1)}, u32[]{:S(2)}, u32[]{:S(2)}) collective-permute-start(bf16[4,104,128]{2,1,0:T(8,128)(2,1)S(1)} %get-tuple-element.33), channel_id=1, source_target_pairs={{0,16},{16,0},{1,17},{17,1},{2,18},{18,2},{3,19},{19,3},{4,20},{20... | collective-permute-start | bytes 319496 | tf_op jit(solution)/shard_map/ppermute | solution.py:448
  38.9 4.0 %copy-start = (bf16[1024,768]{1,0:T(8,128)(2,1)S(1)}, bf16[1024,768]{1,0:T(8,128)(2,1)}, u32[]{:S(2)}) copy-start(bf16[1024,768]{1,0:T(8,128)(2,1)} %refs_10_.1) | copy-start | bytes 4718596
  38.9 4.0 %copy-start.1 = (s32[1024]{0:T(1024)S(1)}, s32[1024]{0:T(1024)}, u32[]{:S(2)}) copy-start(s32[1024]{0:T(1024)} %param.19) | copy-start | bytes 12292
  38.9 4.0 %copy-start.2 = (s32[1024]{0:T(1024)S(1)}, s32[1024]{0:T(1024)}, u32[]{:S(2)}) copy-start(s32[1024]{0:T(1024)} %param.20) | copy-start | bytes 12292

commit v7 on v5

--- a/solution.py
+++ b/solution.py
@@ -11,7 +11,8 @@
 ITERS = 3
 LANES = 128
 STEP = 256
-WIDE = 384
+WIDE = 128
+AHEAD = 3
 SMALL = 8
 NT = (((1,), (1,)), ((), ()))
 F32 = jnp.float32
@@ -65,7 +66,7 @@
             [(coup_ref, coup), (rf_ref, rf), (dp_ref, dp)]
         )
     ]
-    for i in range(chunks):
+    for i in range(min(AHEAD, chunks)):
         load(i).start()
     for copy in small:
         copy.start()
@@ -100,6 +101,8 @@
 
     for i in range(chunks):
         load(i).wait()
+        if i + AHEAD < chunks:
+            load(i + AHEAD).start()
         moved = jnp.dot(pick, wide[i].astype(BF16), preferred_element_type=F32)
         moved = moved.astype(BF16).reshape(nvib, slab, WIDE)
         for t in range(WIDE // LANES):
@@ -200,6 +203,45 @@
     return jnp.concatenate([tile] * (size // LANES), axis=1)
 
 
+def inner(dims, *refs):
+    own, nslab, slab, nang, nquad, mirror = dims
+    nrad = nslab * slab
+    basis, kin_ref, pot, radii, khat, coup, chain, part, first_b, new_ref, rows, scaled = refs
+    count = own - 1
+    for i in range(count):
+        rows[i] = part[i + 1].astype(BF16)
+
+    @pl.loop(0, nquad // STEP)
+    def _(qi):
+        cols = pl.ds(pl.multiple_of(qi * STEP, STEP), STEP)
+        grid = jnp.dot(
+            rows[...].reshape(count * nrad, nang), basis[:, cols], preferred_element_type=F32
+        )
+        prod = grid.reshape(count, nrad, STEP) * pot[:, cols][None]
+        scaled[:, cols] = prod.astype(BF16).reshape(count * nrad, STEP)
+
+    factor = wider(radii[0], STEP)
+    damp = wider(radii[1], STEP)
+
+    @pl.loop(0, nang // STEP)
+    def _(ji):
+        cols = pl.ds(pl.multiple_of(ji * STEP, STEP), STEP)
+        ang = lax.dot_general(
+            scaled[...], basis[cols, :], NT, preferred_element_type=F32
+        ).reshape(count, nrad, STEP)
+        for i in range(count):
+            total = ang[i] + jnp.dot(
+                kin_ref[...], rows[i, :, cols], preferred_element_type=F32
+            )
+            total += wider(khat[i + 1], STEP) * factor * part[i + 1, :, cols]
+            if i + 1 < count:
+                total += chain[i + 1, :, cols] * rows[i + 1, :, cols].astype(F32)
+            if i > 0:
+                total += chain[i, :, cols] * rows[i - 1, :, cols].astype(F32)
+            before = first_b[i + 1, :, cols].astype(F32)
+            new_ref[i, :, cols] = damp * (2.0 * total - damp * before)
+
+
 def advance(dims, sides, n, *refs):
     own, nslab, slab, nang, nquad, mirror = dims
     nrad = nslab * slab
@@ -224,16 +266,20 @@
         base = nang // LANES * slab
         if n == 2:
             part, first_b = take(2)
+            inner_ref = take(1)[0] if mirror else None
             full, block, new_ref, part_h, halo_b, halo_c, halo_k = take(7)
             rows, scaled, joint = take(3)
         else:
             part, first_b, first_f, halo_part, halo1_b, halo1_c, halo1_k, level1_b = take(8)
             new_ref, part_h, part_hh, halo_c = take(4)
             full, halo_b, halo_k, rows, scaled, joint = take(6)
+        split = mirror and n == 2
+        level = block if split else rows
+        shift = 1 if split else own
         for i in range(own):
             value = part[i]
             full[i] = value
-            rows[i] = value.astype(BF16)
+            level[i] = value.astype(BF16)
         for s in range(sides):
             halo_b[s] = rows_in(raw[s], 0, nslab, slab, nang, 0)
             halo_c[s], halo_k[s] = small_in(raw[s], 0, base, nang)
@@ -241,22 +287,26 @@
             if n == 2:
                 joint[s, 0] = link(mirror, s, coup[at], halo_c[s])
                 seen = halo_b[s]
-                rows[own + s] = seen
+                rows[shift + s] = seen
             else:
                 joint[s, 0] = link(mirror, s, coup[at], halo1_c[s])
                 joint[s, 1] = link(mirror, s, halo1_c[s], halo_c[s])
-                level = halo_part[s] + wider(radii[1], nang) * (
+                value = halo_part[s] + wider(radii[1], nang) * (
                     joint[s, 1] * halo_b[s].astype(F32)
                 )
-                seen = level.astype(BF16)
+                seen = value.astype(BF16)
                 rows[own + s] = seen
                 rows[own + sides + s] = halo_b[s]
             value = full[at] + scale * (joint[s, 0] * seen.astype(F32))
             full[at] = value
-            rows[at] = value.astype(BF16)
-        if n == 2:
+            level[at] = value.astype(BF16)
+        if split:
+            rows[0] = block[0]
+        elif n == 2:
             block[...] = rows[:own]
-    count = own + sides * (n - 1)
+    if n == 1:
+        split, level, shift = False, rows, own
+    count = shift + sides * (n - 1)
 
     @pl.loop(0, nquad // STEP)
     def _(qi):
@@ -284,12 +334,18 @@
             return ang[i] + kin + wider(hat, STEP) * factor * value
 
         for i in range(own):
+            if split and i > 0:
+                value = inner_ref[i - 1, :, cols]
+                if i == 1:
+                    value += 2.0 * damp * (chain[0, :, cols] * level[0, :, cols].astype(F32))
+                new_ref[i, :, cols] = value
+                continue
             value = rows[i, :, cols].astype(F32) if n == 1 else full[i, :, cols]
             total = local(i, khat[i], value)
             if i + 1 < own:
-                total += chain[i, :, cols] * rows[i + 1, :, cols].astype(F32)
+                total += chain[i, :, cols] * level[i + 1, :, cols].astype(F32)
             if i > 0:
-                total += chain[i - 1, :, cols] * rows[i - 1, :, cols].astype(F32)
+                total += chain[i - 1, :, cols] * level[i - 1, :, cols].astype(F32)
             if n == 1:
                 new_ref[i, :, cols] = damp * total
             else:
@@ -299,7 +355,7 @@
                 )
         for s in range(sides if n > 1 else 0):
             at = edge_of[s]
-            i = own + s
+            i = shift + s
             hat = halo_k[s] if n == 2 else halo1_k[s]
             total = local(i, hat, rows[i, :, cols].astype(F32))
             edge_b = first_b if n == 2 else level1_b
@@ -454,7 +510,7 @@
     dims = (own, nslab, slab, nang, nquad, mirror)
 
     def run(n, operands, specs, outs, scratch):
-        count = own + sides * (n - 1)
+        count = (1 if mirror and n == 2 else own) + sides * (n - 1)
         return pl.pallas_call(
             functools.partial(advance, dims, sides, n),
             out_shape=outs,
@@ -494,6 +550,26 @@
     common = [basis, kinetic, pot, radii, khat, coup, chain]
     joint = pltpu.VMEM((sides, 2, 1, nang), F32)
     operands = halos[0] + common + [new, first_b]
+    if mirror:
+        operands.append(
+            pl.pallas_call(
+                functools.partial(inner, dims),
+                out_shape=shape((own - 1, nrad, nang), F32),
+                in_specs=[VMEM] * 9,
+                out_specs=VMEM,
+                scratch_shapes=[
+                    pltpu.VMEM((own - 1, nrad, nang), BF16),
+                    pltpu.VMEM(((own - 1) * nrad, nquad), BF16),
+                ],
+                compiler_params=PARAMS,
+                cost_estimate=pl.CostEstimate(
+                    flops=4 * own * nrad * nang * nquad,
+                    bytes_accessed=8 * 1024 * 1024,
+                    transcendentals=0,
+                ),
+                name="inner",
+            )(*common, new, first_b)
+        )
     first_f, level1_b, new, halo_part, halo1_b, halo1_c, halo1_k = run(
         2,
         operands,

time: 56.7 us -> 57.9 us (1.021)
  Pallas kernels: 16.5 us -> 20.4 us
  waiting for transfers between devices: 14.4 us -> 11.6 us
    pallas_call x0 -> x1, Pallas kernels: none -> 2.91 us  [per_device(): pl.pallas_call(functools.partial(inner, dims), out_shape=shape((own - 1,...]
    ppermute x3, waiting for transfers between devices: 2.8 us -> 0.01 us  [per_device(): halos.append([lax.ppermute(part, 'g', [(0, 1), (1, 0)])])]
    pallas_call x1, Pallas kernels: 2.63 us -> 4.35 us  [per_device(): pl.pallas_call(functools.partial(pack, (slab, nvib, nang, share, blocks))...]
    pallas_call x3, Pallas kernels: 11.5 us -> 10.8 us  [run(): pl.pallas_call(functools.partial(advance, dims, sides, n), out_shape=outs...]
  transfers between devices with their start and end apart: 4 -> 4, of which waited for: 2 -> 1; matrix products, arithmetic and copies ran while one was open for 0% -> 0% of each run, Pallas kernels for 20% -> 24%
where the time goes in v7:
time: 57.9 us; the launch traced here: 57.5 us
  Pallas kernels  20.4 us (35%)
  blocking collectives  12.1 us (21%)
  starting transfers between devices  11.9 us (21%)
  waiting for transfers between devices  11.6 us (20%)
  between operations  1.44 us (2%)
    all_to_all x1, blocking collectives, per_device(): home = lax.all_to_all(back, ('hl', 'rad'), 0, 0, tiled=True)  12.1 us
    all_to_all x1, waiting for transfers between devices, per_device(): message = lax.all_to_all(send, ('hl', 'rad'), 0, 0, tiled=True)  11.6 us
    pallas_call x3, Pallas kernels, run(): pl.pallas_call(functools.partial(advance, dims, sides, n), out_shape=outs...  10.8 us
    all_to_all x1, starting transfers between devices, per_device(): message = lax.all_to_all(send, ('hl', 'rad'), 0, 0, tiled=True)  6.33 us
    ppermute x3, starting transfers between devices, per_device(): halos.append([lax.ppermute(part, 'g', [(0, 1), (1, 0)])])  5.58 us
    pallas_call x1, Pallas kernels, per_device(): pl.pallas_call(functools.partial(pack, (slab, nvib, nang, share, blocks))...  4.35 us
    pallas_call x1, Pallas kernels, per_device(): pl.pallas_call(functools.partial(inner, dims), out_shape=shape((own - 1,...  2.91 us
    pallas_call x1, Pallas kernels, per_device(): pl.pallas_call(functools.partial(unpack, (slab, nvib, nang, -(-chan // LA...  1.65 us
  transfers between devices with their start and end apart: 4, of which 1 were waited for; matrix products, arithmetic and copies ran while one was open for 0% of the time, Pallas kernels for 24%

profile of v7, /device:TPU:0, one launch (start us, length us, event | category | flops | bytes accessed | tf_op | source)
XLA Modules:
  0.0 57.5 jit_solution(595590213661838679)
XLA Ops:
  1.3 0.0 copy-start.1
  1.3 4.4 %pack.1 = bf16[16,152,128]{2,1,0:T(8,128)(2,1)} custom-call(f32[256,768]{1,0:T(8,128)} %bitcast.12, f32[256,1536]{1,0:T(8,128)} %bitcast.11, bf16[1,768]{1,0:T(2,128)(2,1)} %coup_ref.1, s32[1,1]{1,0:T(1,128)} %bitcast.8.hel_ref, f32[1,16]{1,0:T(1,128)} %bitcast.13, f32[1,16]{1,0:T(1,128)} %bitcast.14), custom_call_target="tpu_custom_call" | custom-call | tf_op jit(solution)/shard_map/pack/pallas_call | solution.py:456
  5.6 6.3 %all-to-all-start = ((bf16[16,152,128]{2,1,0:T(8,128)(2,1)}), bf16[16,152,128]{2,1,0:T(8,128)(2,1)S(1)}, u32[]{:S(2)}, u32[]{:S(2)}) async-start(bf16[16,152,128]{2,1,0:T(8,128)(2,1)} %pack.1), calls=%async_computation | async-start | bytes 1245184 | tf_op jit(solution)/shard_map/all_to_all | solution.py:481
  12.0 11.6 %all-to-all-done.refs_0_ = bf16[16,152,128]{2,1,0:T(8,128)(2,1)S(1)} async-done(((bf16[16,152,128]{2,1,0:T(8,128)(2,1)}), bf16[16,152,128]{2,1,0:T(8,128)(2,1)S(1)}, u32[]{:S(2)}, u32[]{:S(2)}) %all-to-all-start) | async-done | bytes 622624 | tf_op jit(solution)/shard_map/all_to_all | solution.py:481
  23.6 2.7 %collective-permute-start.2 = (bf16[4,104,128]{2,1,0:T(8,128)(2,1)S(1)}, bf16[4,104,128]{2,1,0:T(8,128)(2,1)S(1)}, u32[]{:S(2)}, u32[]{:S(2)}) collective-permute-start(bf16[4,104,128]{2,1,0:T(8,128)(2,1)S(1)} %get-tuple-element.44), channel_id=1, source_target_pairs={{0,16},{16,0},{1,17},{17,1},{2,18},{18,2},{3,19},{19,3},{4,20},{20... | collective-permute-start | bytes 319496 | tf_op jit(solution)/shard_map/ppermute | solution.py:491
  26.3 0.3 collective-permute-start.1
  26.6 2.6 %collective-permute-start = (bf16[4,104,128]{2,1,0:T(8,128)(2,1)S(1)}, bf16[4,104,128]{2,1,0:T(8,128)(2,1)S(1)}, u32[]{:S(2)}, u32[]{:S(2)}) collective-permute-start(bf16[4,104,128]{2,1,0:T(8,128)(2,1)S(1)} %get-tuple-element.46), channel_id=1, source_target_pairs={{0,16},{16,0},{1,17},{17,1},{2,18},{18,2},{3,19},{19,3},{4,20},{20... | collective-permute-start | bytes 319496 | tf_op jit(solution)/shard_map/ppermute | solution.py:491
  29.2 0.0 copy-done.1
  29.2 4.1 %advance1.1 = (f32[4,64,768]{2,1,0:T(8,128)S(1)}, bf16[4,64,768]{2,1,0:T(8,128)(2,1)S(1)}, bf16[768,1536]{1,0:T(8,128)(2,1)S(1)}, f32[64,1536]{1,0:T(8,128)S(1)}...) custom-call(bf16[16,152,128]{2,1,0:T(8,128)(2,1)S(1)} %all-to-all-do, ...), custom_call_target="tpu_custom_call" | custom-call | flops 1207959552 | bytes 8388608 | tf_op jit(solution)/shard_map/advance1/pallas_call | solution.py:514
  33.3 2.9 %inner.1.refs_10_ = f32[3,64,768]{2,1,0:T(8,128)S(1)} custom-call(bf16[768,1536]{1,0:T(8,128)(2,1)S(1)} %get-tuple-element.23.refs_0_.refs_1_, bf16[64,64]{1,0:T(8,128)(2,1)S(1)} %copy-done.1, f32[64,1536]{1,0:T(8,128)S(1)} %get-tuple-element.24.refs_2_.refs_3_, f32[2,64,128]{2,1,0:T(8,128)S(1)} %get-tuple-element.25.refs_3_.refs_4_.refs_7_, ...), custom_call_target="tpu_custom_call" | custom-call | flops 1207959552 | bytes 8388608 | tf_op jit(solution)/shard_map/inner/pallas_call | solution.py:555
  36.3 0.0 collective-permute-done.2.refs_0_
  36.3 2.7 %advance2.1 = (f32[4,64,768]{2,1,0:T(8,128)S(1)}, bf16[4,64,768]{2,1,0:T(8,128)(2,1)S(1)}, f32[4,64,768]{2,1,0:T(8,128)S(1)}, f32[1,64,768]{2,1,0:T(8,128)S(1)},...) custom-call(bf16[4,104,128]{2,1,0:T(8,128)(2,1)S(1)} %collective-permute-done.2.refs_0_, ...), custom_call_target="tpu_custom_call" | custom-call | flops 603979776 | bytes 8388608 | tf_op jit(solution)/shard_map/advance2/pallas_call | solution.py:514
  39.0 0.0 collective-permute-done.1.refs_0_
  39.0 0.0 copy-start
  39.0 0.0 copy-start.2
  39.1 0.0 copy-start.3
  39.1 3.9 %advance3.1 = (f32[4,64,768]{2,1,0:T(8,128)S(1)}, f32[1,64,768]{2,1,0:T(8,128)S(1)}, f32[1,64,768]{2,1,0:T(8,128)S(1)}, f32[1,1,768]{2,1,0:T(1,128)S(1)}) custom-call(bf16[4,104,128]{2,1,0:T(8,128)(2,1)S(1)} %collective-permute-done.1.refs_0_, bf16[768,1536]{1,0:T(8,128)(2,1)S(1)} %get-tuple-element.23.refs_0_.refs_1_, bf16[64,64]{1,0:T(8,128)(2,1)S(1)} %copy-done.1, ...), custom_call_target="tpu_custom_call" | custom-call | flops 1811939328 | bytes 8388608 | tf_op jit(solution)/shard_map/advance3/pallas_call | solution.py:514
  43.0 0.0 collective-permute-done.refs_0_
  43.0 0.0 copy-done
  43.0 0.0 copy-done.2
  43.0 0.0 copy-done.3
  43.1 0.7 %close.1 = bf16[16,104,128]{2,1,0:T(8,128)(2,1)S(1)} custom-call(bf16[4,104,128]{2,1,0:T(8,128)(2,1)S(1)} %collective-permute-done.refs_0_, f32[4,64,768]{2,1,0:T(8,128)S(1)} %get-tuple-element.38.refs_1_, f32[1,64,768]{2,1,0:T(8,128)S(1)} %get-tuple-element.39.refs_2_, f32[1,64,768]{2,1,0:T(8,128)S(1)} %get-tuple-element.40.refs_3_, ...), custom_call_target="tpu_custom_call" | custom-call | tf_op jit(solution)/shard_map/close/pallas_call | solution.py:599
  43.8 12.1 %all_to_all.10.msg_ref = bf16[16,104,128]{2,1,0:T(8,128)(2,1)S(1)} all-to-all(bf16[16,104,128]{2,1,0:T(8,128)(2,1)S(1)} %close.1), channel_id=1, replica_groups=mesh['g'=2,'hl'=4,'rad'=4] {'hl','rad'}, dimensions={0} | all-to-all | bytes 851968 | tf_op jit(solution)/shard_map/all_to_all | solution.py:609
  55.8 1.7 %unpack.1 = (f32[256,768]{1,0:T(8,128)}, f32[1,256]{1,0:T(1,128)}) custom-call(bf16[16,104,128]{2,1,0:T(8,128)(2,1)S(1)} %all_to_all.10.msg_ref), custom_call_target="tpu_custom_call" | custom-call | tf_op jit(solution)/shard_map/unpack/pallas_call | solution.py:611
  (2 shorter events, 0.1 us)
Async XLA Ops:
  1.3 27.9 %copy-start.1 = (bf16[64,64]{1,0:T(8,128)(2,1)S(1)}, bf16[64,64]{1,0:T(8,128)(2,1)}, u32[]{:S(2)}) copy-start(bf16[64,64]{1,0:T(8,128)(2,1)} %refs_2_.5) | copy-start | bytes 24580
  5.6 17.9 %all-to-all-start = ((bf16[16,152,128]{2,1,0:T(8,128)(2,1)}), bf16[16,152,128]{2,1,0:T(8,128)(2,1)S(1)}, u32[]{:S(2)}, u32[]{:S(2)}) async-start(bf16[16,152,128]{2,1,0:T(8,128)(2,1)} %pack.1), calls=%async_computation | async-start | bytes 1245184 | tf_op jit(solution)/shard_map/all_to_all | solution.py:481
  23.6 12.6 %collective-permute-start.2 = (bf16[4,104,128]{2,1,0:T(8,128)(2,1)S(1)}, bf16[4,104,128]{2,1,0:T(8,128)(2,1)S(1)}, u32[]{:S(2)}, u32[]{:S(2)}) collective-permute-start(bf16[4,104,128]{2,1,0:T(8,128)(2,1)S(1)} %get-tuple-element.44), channel_id=1, source_target_pairs={{0,16},{16,0},{1,17},{17,1},{2,18},{18,2},{3,19},{19,3},{4,20},{20... | collective-permute-start | bytes 319496 | tf_op jit(solution)/shard_map/ppermute | solution.py:491
  26.3 12.7 %collective-permute-start.1 = (bf16[4,104,128]{2,1,0:T(8,128)(2,1)S(1)}, bf16[4,104,128]{2,1,0:T(8,128)(2,1)S(1)}, u32[]{:S(2)}, u32[]{:S(2)}) collective-permute-start(bf16[4,104,128]{2,1,0:T(8,128)(2,1)S(1)} %get-tuple-element.45), channel_id=1, source_target_pairs={{0,16},{16,0},{1,17},{17,1},{2,18},{18,2},{3,19},{19,3},{4,20},{20... | collective-permute-start | bytes 319496 | tf_op jit(solution)/shard_map/ppermute | solution.py:491
  26.6 16.4 %collective-permute-start = (bf16[4,104,128]{2,1,0:T(8,128)(2,1)S(1)}, bf16[4,104,128]{2,1,0:T(8,128)(2,1)S(1)}, u32[]{:S(2)}, u32[]{:S(2)}) collective-permute-start(bf16[4,104,128]{2,1,0:T(8,128)(2,1)S(1)} %get-tuple-element.46), channel_id=1, source_target_pairs={{0,16},{16,0},{1,17},{17,1},{2,18},{18,2},{3,19},{19,3},{4,20},{20... | collective-permute-start | bytes 319496 | tf_op jit(solution)/shard_map/ppermute | solution.py:491
  39.0 4.0 %copy-start = (bf16[1024,768]{1,0:T(8,128)(2,1)S(1)}, bf16[1024,768]{1,0:T(8,128)(2,1)}, u32[]{:S(2)}) copy-start(bf16[1024,768]{1,0:T(8,128)(2,1)} %refs_10_.1) | copy-start | bytes 4718596
  39.0 4.0 %copy-start.2 = (s32[1024]{0:T(1024)S(1)}, s32[1024]{0:T(1024)}, u32[]{:S(2)}) copy-start(s32[1024]{0:T(1024)} %param.19) | copy-start | bytes 12292
  39.1 4.0 %copy-start.3 = (s32[1024]{0:T(1024)S(1)}, s32[1024]{0:T(1024)}, u32[]{:S(2)}) copy-start(s32[1024]{0:T(1024)} %param.20) | copy-start | bytes 12292

commit v8 on v7

--- a/solution.py
+++ b/solution.py
@@ -11,8 +11,7 @@
 ITERS = 3
 LANES = 128
 STEP = 256
-WIDE = 128
-AHEAD = 3
+WIDE = 384
 SMALL = 8
 NT = (((1,), (1,)), ((), ()))
 F32 = jnp.float32
@@ -66,7 +65,7 @@
             [(coup_ref, coup), (rf_ref, rf), (dp_ref, dp)]
         )
     ]
-    for i in range(min(AHEAD, chunks)):
+    for i in range(chunks):
         load(i).start()
     for copy in small:
         copy.start()
@@ -101,8 +100,6 @@
 
     for i in range(chunks):
         load(i).wait()
-        if i + AHEAD < chunks:
-            load(i + AHEAD).start()
         moved = jnp.dot(pick, wide[i].astype(BF16), preferred_element_type=F32)
         moved = moved.astype(BF16).reshape(nvib, slab, WIDE)
         for t in range(WIDE // LANES):
@@ -249,12 +246,9 @@
     take = lambda count: [refs.pop(0) for _ in range(count)]
     edge_of = [0, own - 1]
     if n == 1:
-        msg_ref, basis_hbm, kin_ref = take(3)
-        new_ref, src, basis, pot, radii, khat, coup, chain = take(8)
-        rows, scaled, sems = take(3)
-        for qi in range(nquad // STEP):
-            cols = pl.ds(qi * STEP, STEP)
-            pltpu.make_async_copy(basis_hbm.at[:, cols], basis.at[:, cols], sems.at[qi]).start()
+        msg_ref, basis, kin_ref = take(3)
+        new_ref, src, pot, radii, khat, coup, chain = take(7)
+        rows, scaled = take(2)
         unfold(dims, msg_ref, src, pot, radii, khat, coup)
         rows[...] = src[...]
         for i in range(own - 1):
@@ -311,8 +305,6 @@
     @pl.loop(0, nquad // STEP)
     def _(qi):
         cols = pl.ds(pl.multiple_of(qi * STEP, STEP), STEP)
-        if n == 1:
-            pltpu.make_async_copy(basis_hbm.at[:, cols], basis.at[:, cols], sems.at[qi]).wait()
         grid = jnp.dot(
             rows[...].reshape(count * nrad, nang), basis[:, cols], preferred_element_type=F32
         )
@@ -520,8 +512,8 @@
             + [
                 pltpu.VMEM((count, nrad, nang), BF16),
                 pltpu.VMEM((count * nrad, nquad), BF16),
-                scratch[-1],
-            ],
+            ]
+            + scratch[-1:],
             compiler_params=PARAMS,
             cost_estimate=pl.CostEstimate(
                 flops=4 * count * nrad * nang * nquad,
@@ -531,21 +523,20 @@
             name=f"advance{n}",
         )(*operands)
 
-    new, first_b, basis, pot, radii, khat, coup, chain = run(
+    new, first_b, pot, radii, khat, coup, chain = run(
         1,
-        [message, in_hbm(basis), kinetic],
-        [VMEM, HBM, VMEM],
+        [message, basis, kinetic],
+        [VMEM] * 3,
         [
             full_type,
             block_type,
-            shape(basis.shape, BF16),
             shape((nrad, nquad), F32),
             shape((2, nrad, LANES), F32),
             shape((own, 1, LANES), F32),
             shape((own, 1, nang), F32),
             shape((max(own - 1, 1), 1, nang), F32),
         ],
-        [pltpu.SemaphoreType.DMA((nquad // STEP,))],
+        [],
     )
     common = [basis, kinetic, pot, radii, khat, coup, chain]
     joint = pltpu.VMEM((sides, 2, 1, nang), F32)

time: 57.9 us -> 56.1 us (0.969)
  Pallas kernels: 20.4 us -> 17.7 us
  waiting for transfers between devices: 11.6 us -> 12.4 us
    pallas_call x1, Pallas kernels: 4.35 us -> 2.63 us  [per_device(): pl.pallas_call(functools.partial(pack, (slab, nvib, nang, share, blocks))...]
    pallas_call x3, Pallas kernels: 10.8 us -> 9.8 us  [run(): pl.pallas_call(functools.partial(advance, dims, sides, n), out_shape=outs...]
    ppermute x3, waiting for transfers between devices: 0.01 us -> 0.85 us  [per_device(): halos.append([lax.ppermute(part, 'g', [(0, 1), (1, 0)])])]
  transfers between devices with their start and end apart: 4 -> 4, of which waited for: 1 -> 2; matrix products, arithmetic and copies ran while one was open for 0% -> 0% of each run, Pallas kernels for 24% -> 23%
where the time goes in v8:
time: 56.1 us; the launch traced here: 55.8 us
  Pallas kernels  17.7 us (32%)
  waiting for transfers between devices  12.4 us (22%)
  blocking collectives  12.1 us (22%)
  starting transfers between devices  12 us (21%)
  between operations  1.44 us (3%)
    all_to_all x1, blocking collectives, per_device(): home = lax.all_to_all(back, ('hl', 'rad'), 0, 0, tiled=True)  12.1 us
    all_to_all x1, waiting for transfers between devices, per_device(): message = lax.all_to_all(send, ('hl', 'rad'), 0, 0, tiled=True)  11.6 us
    pallas_call x3, Pallas kernels, run(): pl.pallas_call(functools.partial(advance, dims, sides, n), out_shape=outs...  9.8 us
    all_to_all x1, starting transfers between devices, per_device(): message = lax.all_to_all(send, ('hl', 'rad'), 0, 0, tiled=True)  6.45 us
    ppermute x3, starting transfers between devices, per_device(): halos.append([lax.ppermute(part, 'g', [(0, 1), (1, 0)])])  5.58 us
    pallas_call x1, Pallas kernels, per_device(): pl.pallas_call(functools.partial(inner, dims), out_shape=shape((own - 1,...  2.91 us
    pallas_call x1, Pallas kernels, per_device(): pl.pallas_call(functools.partial(pack, (slab, nvib, nang, share, blocks))...  2.63 us
    pallas_call x1, Pallas kernels, per_device(): pl.pallas_call(functools.partial(unpack, (slab, nvib, nang, -(-chan // LA...  1.65 us
  transfers between devices with their start and end apart: 4, of which 2 were waited for; matrix products, arithmetic and copies ran while one was open for 0% of the time, Pallas kernels for 23%

profile of v8, /device:TPU:0, one launch (start us, length us, event | category | flops | bytes accessed | tf_op | source)
XLA Modules:
  0.0 55.8 jit_solution(15139285427849061699)
XLA Ops:
  1.3 2.6 %pack.1 = bf16[16,152,128]{2,1,0:T(8,128)(2,1)} custom-call(f32[256,768]{1,0:T(8,128)} %bitcast.12, f32[256,1536]{1,0:T(8,128)} %bitcast.11, bf16[1,768]{1,0:T(2,128)(2,1)} %coup_ref.1, s32[1,1]{1,0:T(1,128)} %bitcast.8.hel_ref, f32[1,16]{1,0:T(1,128)} %bitcast.13, f32[1,16]{1,0:T(1,128)} %bitcast.14), custom_call_target="tpu_custom_call" | custom-call | tf_op jit(solution)/shard_map/pack/pallas_call | solution.py:448
  3.9 0.0 copy-start
  3.9 0.0 copy-start.2
  3.9 6.5 %all-to-all-start = ((bf16[16,152,128]{2,1,0:T(8,128)(2,1)}), bf16[16,152,128]{2,1,0:T(8,128)(2,1)S(1)}, u32[]{:S(2)}, u32[]{:S(2)}) async-start(bf16[16,152,128]{2,1,0:T(8,128)(2,1)} %pack.1), calls=%async_computation | async-start | bytes 1245184 | tf_op jit(solution)/shard_map/all_to_all | solution.py:473
  10.4 11.6 %all-to-all-done.refs_0_ = bf16[16,152,128]{2,1,0:T(8,128)(2,1)S(1)} async-done(((bf16[16,152,128]{2,1,0:T(8,128)(2,1)}), bf16[16,152,128]{2,1,0:T(8,128)(2,1)S(1)}, u32[]{:S(2)}, u32[]{:S(2)}) %all-to-all-start) | async-done | bytes 622624 | tf_op jit(solution)/shard_map/all_to_all | solution.py:473
  22.1 2.7 %collective-permute-start.2 = (bf16[4,104,128]{2,1,0:T(8,128)(2,1)S(1)}, bf16[4,104,128]{2,1,0:T(8,128)(2,1)S(1)}, u32[]{:S(2)}, u32[]{:S(2)}) collective-permute-start(bf16[4,104,128]{2,1,0:T(8,128)(2,1)S(1)} %get-tuple-element.42), channel_id=1, source_target_pairs={{0,16},{16,0},{1,17},{17,1},{2,18},{18,2},{3,19},{19,3},{4,20},{20... | collective-permute-start | bytes 319496 | tf_op jit(solution)/shard_map/ppermute | solution.py:483
  24.7 0.3 collective-permute-start.1
  25.0 2.6 %collective-permute-start = (bf16[4,104,128]{2,1,0:T(8,128)(2,1)S(1)}, bf16[4,104,128]{2,1,0:T(8,128)(2,1)S(1)}, u32[]{:S(2)}, u32[]{:S(2)}) collective-permute-start(bf16[4,104,128]{2,1,0:T(8,128)(2,1)S(1)} %get-tuple-element.44), channel_id=1, source_target_pairs={{0,16},{16,0},{1,17},{17,1},{2,18},{18,2},{3,19},{19,3},{4,20},{20... | collective-permute-start | bytes 319496 | tf_op jit(solution)/shard_map/ppermute | solution.py:483
  27.6 0.0 copy-done
  27.6 0.0 copy-done.2
  27.6 3.1 %advance1.1 = (f32[4,64,768]{2,1,0:T(8,128)S(1)}, bf16[4,64,768]{2,1,0:T(8,128)(2,1)S(1)}, f32[64,1536]{1,0:T(8,128)S(1)}, f32[2,64,128]{2,1,0:T(8,128)S(1)}, f3...) custom-call(bf16[16,152,128]{2,1,0:T(8,128)(2,1)S(1)} %all-to-all-done.refs_0_, ...), custom_call_target="tpu_custom_call" | custom-call | flops 1207959552 | bytes 8388608 | tf_op jit(solution)/shard_map/advance1/pallas_call | solution.py:506
  30.8 2.9 %inner.1.refs_10_ = f32[3,64,768]{2,1,0:T(8,128)S(1)} custom-call(bf16[768,1536]{1,0:T(8,128)(2,1)S(1)} %copy-done, bf16[64,64]{1,0:T(8,128)(2,1)S(1)} %copy-done.2, f32[64,1536]{1,0:T(8,128)S(1)} %get-tuple-element.22.refs_2_.refs_3_, f32[2,64,128]{2,1,0:T(8,128)S(1)} %get-tuple-element.23.refs_3_.refs_4_.refs_7_, ...), custom_call_target="tpu_custom_call" | custom-call | flops 1207959552 | bytes 8388608 | tf_op jit(solution)/shard_map/inner/pallas_call | solution.py:546
  33.7 0.8 %collective-permute-done.2.refs_0_ = bf16[4,104,128]{2,1,0:T(8,128)(2,1)S(1)} collective-permute-done((bf16[4,104,128]{2,1,0:T(8,128)(2,1)S(1)}, bf16[4,104,128]{2,1,0:T(8,128)(2,1)S(1)}, u32[]{:S(2)}, u32[]{:S(2)}) %collective-permute-start.2) | collective-permute-done | bytes 106528 | tf_op jit(solution)/shard_map/ppermute | solution.py:483
  34.6 2.7 %advance2.1 = (f32[4,64,768]{2,1,0:T(8,128)S(1)}, bf16[4,64,768]{2,1,0:T(8,128)(2,1)S(1)}, f32[4,64,768]{2,1,0:T(8,128)S(1)}, f32[1,64,768]{2,1,0:T(8,128)S(1)},...) custom-call(bf16[4,104,128]{2,1,0:T(8,128)(2,1)S(1)} %collective-permute-done.2.refs_0_, ...), custom_call_target="tpu_custom_call" | custom-call | flops 603979776 | bytes 8388608 | tf_op jit(solution)/shard_map/advance2/pallas_call | solution.py:506
  37.3 0.0 collective-permute-done.1.refs_0_
  37.3 0.0 copy-start.1
  37.3 0.0 copy-start.3
  37.3 0.0 copy-start.4
  37.3 3.9 %advance3.1 = (f32[4,64,768]{2,1,0:T(8,128)S(1)}, f32[1,64,768]{2,1,0:T(8,128)S(1)}, f32[1,64,768]{2,1,0:T(8,128)S(1)}, f32[1,1,768]{2,1,0:T(1,128)S(1)}) custom-call(bf16[4,104,128]{2,1,0:T(8,128)(2,1)S(1)} %collective-permute-done.1.refs_0_, bf16[768,1536]{1,0:T(8,128)(2,1)S(1)} %copy-done, bf16[64,64]{1,0:T(8,128)(2,1)S(1)} %copy-done.2, ...), custom_call_target="tpu_custom_call" | custom-call | flops 1811939328 | bytes 8388608 | tf_op jit(solution)/shard_map/advance3/pallas_call | solution.py:506
  41.3 0.0 collective-permute-done.refs_0_
  41.3 0.0 copy-done.1
  41.3 0.0 copy-done.3
  41.3 0.0 copy-done.4
  41.3 0.7 %close.1 = bf16[16,104,128]{2,1,0:T(8,128)(2,1)S(1)} custom-call(bf16[4,104,128]{2,1,0:T(8,128)(2,1)S(1)} %collective-permute-done.refs_0_, f32[4,64,768]{2,1,0:T(8,128)S(1)} %get-tuple-element.36.refs_1_, f32[1,64,768]{2,1,0:T(8,128)S(1)} %get-tuple-element.37.refs_2_, f32[1,64,768]{2,1,0:T(8,128)S(1)} %get-tuple-element.38.refs_3_, ...), custom_call_target="tpu_custom_call" | custom-call | tf_op jit(solution)/shard_map/close/pallas_call | solution.py:590
  42.0 12.1 %all_to_all.10.msg_ref = bf16[16,104,128]{2,1,0:T(8,128)(2,1)S(1)} all-to-all(bf16[16,104,128]{2,1,0:T(8,128)(2,1)S(1)} %close.1), channel_id=1, replica_groups=mesh['g'=2,'hl'=4,'rad'=4] {'hl','rad'}, dimensions={0} | all-to-all | bytes 851968 | tf_op jit(solution)/shard_map/all_to_all | solution.py:600
  54.1 1.7 %unpack.1 = (f32[256,768]{1,0:T(8,128)}, f32[1,256]{1,0:T(1,128)}) custom-call(bf16[16,104,128]{2,1,0:T(8,128)(2,1)S(1)} %all_to_all.10.msg_ref), custom_call_target="tpu_custom_call" | custom-call | tf_op jit(solution)/shard_map/unpack/pallas_call | solution.py:602
  (2 shorter events, 0.1 us)
Async XLA Ops:
  3.9 23.7 %copy-start = (bf16[768,1536]{1,0:T(8,128)(2,1)S(1)}, bf16[768,1536]{1,0:T(8,128)(2,1)}, u32[]{:S(2)}) copy-start(bf16[768,1536]{1,0:T(8,128)(2,1)} %refs_1_.7) | copy-start | bytes 7077892
  3.9 23.7 %copy-start.2 = (bf16[64,64]{1,0:T(8,128)(2,1)S(1)}, bf16[64,64]{1,0:T(8,128)(2,1)}, u32[]{:S(2)}) copy-start(bf16[64,64]{1,0:T(8,128)(2,1)} %refs_2_.5) | copy-start | bytes 24580
  3.9 18.0 %all-to-all-start = ((bf16[16,152,128]{2,1,0:T(8,128)(2,1)}), bf16[16,152,128]{2,1,0:T(8,128)(2,1)S(1)}, u32[]{:S(2)}, u32[]{:S(2)}) async-start(bf16[16,152,128]{2,1,0:T(8,128)(2,1)} %pack.1), calls=%async_computation | async-start | bytes 1245184 | tf_op jit(solution)/shard_map/all_to_all | solution.py:473
  22.1 12.5 %collective-permute-start.2 = (bf16[4,104,128]{2,1,0:T(8,128)(2,1)S(1)}, bf16[4,104,128]{2,1,0:T(8,128)(2,1)S(1)}, u32[]{:S(2)}, u32[]{:S(2)}) collective-permute-start(bf16[4,104,128]{2,1,0:T(8,128)(2,1)S(1)} %get-tuple-element.42), channel_id=1, source_target_pairs={{0,16},{16,0},{1,17},{17,1},{2,18},{18,2},{3,19},{19,3},{4,20},{20... | collective-permute-start | bytes 319496 | tf_op jit(solution)/shard_map/ppermute | solution.py:483
  24.7 12.6 %collective-permute-start.1 = (bf16[4,104,128]{2,1,0:T(8,128)(2,1)S(1)}, bf16[4,104,128]{2,1,0:T(8,128)(2,1)S(1)}, u32[]{:S(2)}, u32[]{:S(2)}) collective-permute-start(bf16[4,104,128]{2,1,0:T(8,128)(2,1)S(1)} %get-tuple-element.43), channel_id=1, source_target_pairs={{0,16},{16,0},{1,17},{17,1},{2,18},{18,2},{3,19},{19,3},{4,20},{20... | collective-permute-start | bytes 319496 | tf_op jit(solution)/shard_map/ppermute | solution.py:483
  25.0 16.2 %collective-permute-start = (bf16[4,104,128]{2,1,0:T(8,128)(2,1)S(1)}, bf16[4,104,128]{2,1,0:T(8,128)(2,1)S(1)}, u32[]{:S(2)}, u32[]{:S(2)}) collective-permute-start(bf16[4,104,128]{2,1,0:T(8,128)(2,1)S(1)} %get-tuple-element.44), channel_id=1, source_target_pairs={{0,16},{16,0},{1,17},{17,1},{2,18},{18,2},{3,19},{19,3},{4,20},{20... | collective-permute-start | bytes 319496 | tf_op jit(solution)/shard_map/ppermute | solution.py:483
  37.3 4.0 %copy-start.1 = (bf16[1024,768]{1,0:T(8,128)(2,1)S(1)}, bf16[1024,768]{1,0:T(8,128)(2,1)}, u32[]{:S(2)}) copy-start(bf16[1024,768]{1,0:T(8,128)(2,1)} %refs_10_.1) | copy-start | bytes 4718596
  37.3 4.0 %copy-start.3 = (s32[1024]{0:T(1024)S(1)}, s32[1024]{0:T(1024)}, u32[]{:S(2)}) copy-start(s32[1024]{0:T(1024)} %param.19) | copy-start | bytes 12292
  37.3 4.0 %copy-start.4 = (s32[1024]{0:T(1024)S(1)}, s32[1024]{0:T(1024)}, u32[]{:S(2)}) copy-start(s32[1024]{0:T(1024)} %param.20) | copy-start | bytes 12292

commit v9 on v8

--- a/solution.py
+++ b/solution.py
@@ -203,7 +203,12 @@
 def inner(dims, *refs):
     own, nslab, slab, nang, nquad, mirror = dims
     nrad = nslab * slab
-    basis, kin_ref, pot, radii, khat, coup, chain, part, first_b, new_ref, rows, scaled = refs
+    basis, kin_ref, pot, radii, khat, coup, chain, part, first_b, msg_ref = refs[:10]
+    new_ref, send_ref, rows, scaled = refs[10:]
+    top = nquad // own // LANES * slab
+    first = place(mirror, own, ITERS - 1) * nslab
+    for m in range(nslab):
+        send_ref[m] = msg_ref[first + m, top:, :]
     count = own - 1
     for i in range(count):
         rows[i] = part[i + 1].astype(BF16)
@@ -447,7 +452,7 @@
 
     send = pl.pallas_call(
         functools.partial(pack, (slab, nvib, nang, share, blocks)),
-        out_shape=shape((nvib, height, LANES), BF16),
+        out_shape=pltpu.HBM((nvib, height, LANES), BF16),
         in_specs=[HBM] * 3 + [VMEM] + [HBM] * 2,
         out_specs=HBM,
         scratch_shapes=[
@@ -476,11 +481,12 @@
     sides = 1 if mirror else 2
     rows = message[:, share // LANES * slab :]
     halos = []
-    for j in range(ITERS):
+    swapped = [(0, 1), (1, 0)]
+    for j in range(ITERS - 1 if mirror else ITERS):
         if mirror:
             first = jnp.where(group == 0, own - 1 - j, j) * nslab
             part = lax.dynamic_slice_in_dim(rows, first, nslab, 0)
-            halos.append([lax.ppermute(part, "g", [(0, 1), (1, 0)])])
+            halos.append([lax.ppermute(part, "g", swapped)])
             continue
         away, at = j // own + 1, j % own
         upper = rows[at * nslab : (at + 1) * nslab]
@@ -542,25 +548,28 @@
     joint = pltpu.VMEM((sides, 2, 1, nang), F32)
     operands = halos[0] + common + [new, first_b]
     if mirror:
-        operands.append(
-            pl.pallas_call(
-                functools.partial(inner, dims),
-                out_shape=shape((own - 1, nrad, nang), F32),
-                in_specs=[VMEM] * 9,
-                out_specs=VMEM,
-                scratch_shapes=[
-                    pltpu.VMEM((own - 1, nrad, nang), BF16),
-                    pltpu.VMEM(((own - 1) * nrad, nquad), BF16),
-                ],
-                compiler_params=PARAMS,
-                cost_estimate=pl.CostEstimate(
-                    flops=4 * own * nrad * nang * nquad,
-                    bytes_accessed=8 * 1024 * 1024,
-                    transcendentals=0,
-                ),
-                name="inner",
-            )(*common, new, first_b)
-        )
+        ready, part = pl.pallas_call(
+            functools.partial(inner, dims),
+            out_shape=[
+                shape((own - 1, nrad, nang), F32),
+                shape((nslab, height - share // LANES * slab, LANES), BF16),
+            ],
+            in_specs=[VMEM] * 10,
+            out_specs=[VMEM] * 2,
+            scratch_shapes=[
+                pltpu.VMEM((own - 1, nrad, nang), BF16),
+                pltpu.VMEM(((own - 1) * nrad, nquad), BF16),
+            ],
+            compiler_params=PARAMS,
+            cost_estimate=pl.CostEstimate(
+                flops=4 * own * nrad * nang * nquad,
+                bytes_accessed=8 * 1024 * 1024,
+                transcendentals=0,
+            ),
+            name="inner",
+        )(*common, new, first_b, message)
+        operands.append(ready)
+        halos.append([lax.ppermute(part, "g", swapped)])
     first_f, level1_b, new, halo_part, halo1_b, halo1_c, halo1_k = run(
         2,
         operands,

time: 56.1 us -> 55.3 us (0.986)
  waiting for transfers between devices: 12.4 us -> 11.6 us
    ppermute x3, waiting for transfers between devices: 0.85 us -> 0.01 us  [per_device(): halos.append([lax.ppermute(part, 'g', swapped)])]
  transfers between devices with their start and end apart: 4 -> 4, of which waited for: 2 -> 1; matrix products, arithmetic and copies ran while one was open for 0% -> 0% of each run, Pallas kernels for 23% -> 23%
where the time goes in v9:
time: 55.3 us; the launch traced here: 55 us
  Pallas kernels  17.7 us (32%)
  starting transfers between devices  12.1 us (22%)
  blocking collectives  12.1 us (22%)
  waiting for transfers between devices  11.6 us (21%)
  between operations  1.43 us (3%)
    all_to_all x1, blocking collectives, per_device(): home = lax.all_to_all(back, ('hl', 'rad'), 0, 0, tiled=True)  12.1 us
    all_to_all x1, waiting for transfers between devices, per_device(): message = lax.all_to_all(send, ('hl', 'rad'), 0, 0, tiled=True)  11.6 us
    pallas_call x3, Pallas kernels, run(): pl.pallas_call(functools.partial(advance, dims, sides, n), out_shape=outs...  9.79 us
    all_to_all x1, starting transfers between devices, per_device(): message = lax.all_to_all(send, ('hl', 'rad'), 0, 0, tiled=True)  6.45 us
    ppermute x3, starting transfers between devices, per_device(): halos.append([lax.ppermute(part, 'g', swapped)])  5.64 us
    pallas_call x1, Pallas kernels, per_device(): pl.pallas_call(functools.partial(inner, dims), out_shape=[shape((own - 1,...  2.92 us
    pallas_call x1, Pallas kernels, per_device(): pl.pallas_call(functools.partial(pack, (slab, nvib, nang, share, blocks))...  2.63 us
    pallas_call x1, Pallas kernels, per_device(): pl.pallas_call(functools.partial(unpack, (slab, nvib, nang, -(-chan // LA...  1.65 us
  transfers between devices with their start and end apart: 4, of which 1 were waited for; matrix products, arithmetic and copies ran while one was open for 0% of the time, Pallas kernels for 23%

profile of v9, /device:TPU:0, one launch (start us, length us, event | category | flops | bytes accessed | tf_op | source)
XLA Modules:
  0.0 55.0 jit_solution(4996922902654438520)
XLA Ops:
  1.3 2.6 %pack.1 = bf16[16,152,128]{2,1,0:T(8,128)(2,1)} custom-call(f32[256,768]{1,0:T(8,128)} %bitcast.12, f32[256,1536]{1,0:T(8,128)} %bitcast.11, bf16[1,768]{1,0:T(2,128)(2,1)} %coup_ref.1, s32[1,1]{1,0:T(1,128)} %bitcast.8.hel_ref, f32[1,16]{1,0:T(1,128)} %bitcast.13, f32[1,16]{1,0:T(1,128)} %bitcast.14), custom_call_target="tpu_custom_call" | custom-call | tf_op jit(solution)/shard_map/pack/pallas_call | solution.py:453
  3.9 0.0 copy-start
  3.9 0.0 copy-start.2
  3.9 6.5 %all-to-all-start = ((bf16[16,152,128]{2,1,0:T(8,128)(2,1)}), bf16[16,152,128]{2,1,0:T(8,128)(2,1)S(1)}, u32[]{:S(2)}, u32[]{:S(2)}) async-start(bf16[16,152,128]{2,1,0:T(8,128)(2,1)} %pack.1), calls=%async_computation | async-start | bytes 1245184 | tf_op jit(solution)/shard_map/all_to_all | solution.py:478
  10.4 11.6 %all-to-all-done.refs_0_.refs_9_ = bf16[16,152,128]{2,1,0:T(8,128)(2,1)S(1)} async-done(((bf16[16,152,128]{2,1,0:T(8,128)(2,1)}), bf16[16,152,128]{2,1,0:T(8,128)(2,1)S(1)}, u32[]{:S(2)}, u32[]{:S(2)}) %all-to-all-start) | async-done | bytes 622624 | tf_op jit(solution)/shard_map/all_to_all | solution.py:478
  22.0 2.7 %collective-permute-start.2 = (bf16[4,104,128]{2,1,0:T(8,128)(2,1)S(1)}, bf16[4,104,128]{2,1,0:T(8,128)(2,1)S(1)}, u32[]{:S(2)}, u32[]{:S(2)}) collective-permute-start(bf16[4,104,128]{2,1,0:T(8,128)(2,1)S(1)} %get-tuple-element.46), channel_id=1, source_target_pairs={{0,16},{16,0},{1,17},{17,1},{2,18},{18,2},{3,19},{19,3},{4,20},{20... | collective-permute-start | bytes 319496 | tf_op jit(solution)/shard_map/ppermute | solution.py:489
  24.7 0.3 collective-permute-start.1
  25.0 0.0 copy-done
  25.0 0.0 copy-done.2
  25.0 3.1 %advance1.1 = (f32[4,64,768]{2,1,0:T(8,128)S(1)}, bf16[4,64,768]{2,1,0:T(8,128)(2,1)S(1)}, f32[64,1536]{1,0:T(8,128)S(1)}, f32[2,64,128]{2,1,0:T(8,128)S(1)}, f3...) custom-call(bf16[16,152,128]{2,1,0:T(8,128)(2,1)S(1)} %all-to-all-done.refs_0_.refs_9_, ...), custom_call_target="tpu_custom_call" | custom-call | flops 1207959552 | bytes 8388608 | tf_op jit(solution)/shard_map/advance1/pallas_call | solution.py:512
  28.2 2.9 %inner.1 = (f32[3,64,768]{2,1,0:T(8,128)S(1)}, bf16[4,104,128]{2,1,0:T(8,128)(2,1)S(1)}) custom-call(bf16[768,1536]{1,0:T(8,128)(2,1)S(1)} %copy-done, bf16[64,64]{1,0:T(8,128)(2,1)S(1)} %copy-done.2, f32[64,1536]{1,0:T(8,128)S(1)} %get-tuple-element.24.refs_2_.refs_3_, f32[2,64,128]{2,1,0:T(8,128)S(1)} %get-tuple-element.25.refs_3_.refs_4_.refs_7_, ...), custom_call_target="tpu_custom_call" | custom-call | flops 1207959552 | bytes 8388608 | tf_op jit(solution)/shard_map/inner/pallas_call | solution.py:551
  31.1 2.7 %collective-permute-start = (bf16[4,104,128]{2,1,0:T(8,128)(2,1)S(1)}, bf16[4,104,128]{2,1,0:T(8,128)(2,1)S(1)}, u32[]{:S(2)}, u32[]{:S(2)}) collective-permute-start(bf16[4,104,128]{2,1,0:T(8,128)(2,1)S(1)} %get-tuple-element.31), channel_id=1, source_target_pairs={{0,16},{16,0},{1,17},{17,1},{2,18},{18,2},{3,19},{19,3},{4,20},{20... | collective-permute-start | bytes 319496 | tf_op jit(solution)/shard_map/ppermute | solution.py:572
  33.8 0.0 collective-permute-done.2.refs_0_
  33.8 2.7 %advance2.1 = (f32[4,64,768]{2,1,0:T(8,128)S(1)}, bf16[4,64,768]{2,1,0:T(8,128)(2,1)S(1)}, f32[4,64,768]{2,1,0:T(8,128)S(1)}, f32[1,64,768]{2,1,0:T(8,128)S(1)},...) custom-call(bf16[4,104,128]{2,1,0:T(8,128)(2,1)S(1)} %collective-permute-done.2.refs_0_, ...), custom_call_target="tpu_custom_call" | custom-call | flops 603979776 | bytes 8388608 | tf_op jit(solution)/shard_map/advance2/pallas_call | solution.py:512
  36.5 0.0 collective-permute-done.1.refs_0_
  36.5 0.0 copy-start.1
  36.5 0.0 copy-start.3
  36.5 0.0 copy-start.4
  36.6 3.9 %advance3.1 = (f32[4,64,768]{2,1,0:T(8,128)S(1)}, f32[1,64,768]{2,1,0:T(8,128)S(1)}, f32[1,64,768]{2,1,0:T(8,128)S(1)}, f32[1,1,768]{2,1,0:T(1,128)S(1)}) custom-call(bf16[4,104,128]{2,1,0:T(8,128)(2,1)S(1)} %collective-permute-done.1.refs_0_, bf16[768,1536]{1,0:T(8,128)(2,1)S(1)} %copy-done, bf16[64,64]{1,0:T(8,128)(2,1)S(1)} %copy-done.2, ...), custom_call_target="tpu_custom_call" | custom-call | flops 1811939328 | bytes 8388608 | tf_op jit(solution)/shard_map/advance3/pallas_call | solution.py:512
  40.5 0.0 collective-permute-done.refs_0_
  40.5 0.0 copy-done.1
  40.5 0.0 copy-done.3
  40.5 0.0 copy-done.4
  40.5 0.7 %close.1 = bf16[16,104,128]{2,1,0:T(8,128)(2,1)S(1)} custom-call(bf16[4,104,128]{2,1,0:T(8,128)(2,1)S(1)} %collective-permute-done.refs_0_, f32[4,64,768]{2,1,0:T(8,128)S(1)} %get-tuple-element.40.refs_1_, f32[1,64,768]{2,1,0:T(8,128)S(1)} %get-tuple-element.41.refs_2_, f32[1,64,768]{2,1,0:T(8,128)S(1)} %get-tuple-element.42.refs_3_, ...), custom_call_target="tpu_custom_call" | custom-call | tf_op jit(solution)/shard_map/close/pallas_call | solution.py:599
  41.3 12.1 %all_to_all.10.msg_ref = bf16[16,104,128]{2,1,0:T(8,128)(2,1)S(1)} all-to-all(bf16[16,104,128]{2,1,0:T(8,128)(2,1)S(1)} %close.1), channel_id=1, replica_groups=mesh['g'=2,'hl'=4,'rad'=4] {'hl','rad'}, dimensions={0} | all-to-all | bytes 851968 | tf_op jit(solution)/shard_map/all_to_all | solution.py:609
  53.3 1.7 %unpack.1 = (f32[256,768]{1,0:T(8,128)}, f32[1,256]{1,0:T(1,128)}) custom-call(bf16[16,104,128]{2,1,0:T(8,128)(2,1)S(1)} %all_to_all.10.msg_ref), custom_call_target="tpu_custom_call" | custom-call | tf_op jit(solution)/shard_map/unpack/pallas_call | solution.py:611
  (2 shorter events, 0.1 us)
Async XLA Ops:
  3.9 21.1 %copy-start = (bf16[768,1536]{1,0:T(8,128)(2,1)S(1)}, bf16[768,1536]{1,0:T(8,128)(2,1)}, u32[]{:S(2)}) copy-start(bf16[768,1536]{1,0:T(8,128)(2,1)} %refs_1_.7) | copy-start | bytes 7077892
  3.9 21.1 %copy-start.2 = (bf16[64,64]{1,0:T(8,128)(2,1)S(1)}, bf16[64,64]{1,0:T(8,128)(2,1)}, u32[]{:S(2)}) copy-start(bf16[64,64]{1,0:T(8,128)(2,1)} %refs_2_.5) | copy-start | bytes 24580
  3.9 18.0 %all-to-all-start = ((bf16[16,152,128]{2,1,0:T(8,128)(2,1)}), bf16[16,152,128]{2,1,0:T(8,128)(2,1)S(1)}, u32[]{:S(2)}, u32[]{:S(2)}) async-start(bf16[16,152,128]{2,1,0:T(8,128)(2,1)} %pack.1), calls=%async_computation | async-start | bytes 1245184 | tf_op jit(solution)/shard_map/all_to_all | solution.py:478
  22.0 11.7 %collective-permute-start.2 = (bf16[4,104,128]{2,1,0:T(8,128)(2,1)S(1)}, bf16[4,104,128]{2,1,0:T(8,128)(2,1)S(1)}, u32[]{:S(2)}, u32[]{:S(2)}) collective-permute-start(bf16[4,104,128]{2,1,0:T(8,128)(2,1)S(1)} %get-tuple-element.46), channel_id=1, source_target_pairs={{0,16},{16,0},{1,17},{17,1},{2,18},{18,2},{3,19},{19,3},{4,20},{20... | collective-permute-start | bytes 319496 | tf_op jit(solution)/shard_map/ppermute | solution.py:489
  24.7 11.8 %collective-permute-start.1 = (bf16[4,104,128]{2,1,0:T(8,128)(2,1)S(1)}, bf16[4,104,128]{2,1,0:T(8,128)(2,1)S(1)}, u32[]{:S(2)}, u32[]{:S(2)}) collective-permute-start(bf16[4,104,128]{2,1,0:T(8,128)(2,1)S(1)} %get-tuple-element.47), channel_id=1, source_target_pairs={{0,16},{16,0},{1,17},{17,1},{2,18},{18,2},{3,19},{19,3},{4,20},{20... | collective-permute-start | bytes 319496 | tf_op jit(solution)/shard_map/ppermute | solution.py:489
  31.1 9.4 %collective-permute-start = (bf16[4,104,128]{2,1,0:T(8,128)(2,1)S(1)}, bf16[4,104,128]{2,1,0:T(8,128)(2,1)S(1)}, u32[]{:S(2)}, u32[]{:S(2)}) collective-permute-start(bf16[4,104,128]{2,1,0:T(8,128)(2,1)S(1)} %get-tuple-element.31), channel_id=1, source_target_pairs={{0,16},{16,0},{1,17},{17,1},{2,18},{18,2},{3,19},{19,3},{4,20},{20... | collective-permute-start | bytes 319496 | tf_op jit(solution)/shard_map/ppermute | solution.py:572
  36.5 4.0 %copy-start.1 = (bf16[1024,768]{1,0:T(8,128)(2,1)S(1)}, bf16[1024,768]{1,0:T(8,128)(2,1)}, u32[]{:S(2)}) copy-start(bf16[1024,768]{1,0:T(8,128)(2,1)} %refs_10_.1) | copy-start | bytes 4718596
  36.5 4.0 %copy-start.3 = (s32[1024]{0:T(1024)S(1)}, s32[1024]{0:T(1024)}, u32[]{:S(2)}) copy-start(s32[1024]{0:T(1024)} %param.19) | copy-start | bytes 12292
  36.5 4.0 %copy-start.4 = (s32[1024]{0:T(1024)S(1)}, s32[1024]{0:T(1024)}, u32[]{:S(2)}) copy-start(s32[1024]{0:T(1024)} %param.20) | copy-start | bytes 12292

commit v10 on v9

--- a/solution.py
+++ b/solution.py
@@ -12,6 +12,8 @@
 LANES = 128
 STEP = 256
 WIDE = 384
+QSTEP = 512
+JSTEP = 384
 SMALL = 8
 NT = (((1,), (1,)), ((), ()))
 F32 = jnp.float32
@@ -213,29 +215,29 @@
     for i in range(count):
         rows[i] = part[i + 1].astype(BF16)
 
-    @pl.loop(0, nquad // STEP)
+    @pl.loop(0, nquad // QSTEP)
     def _(qi):
-        cols = pl.ds(pl.multiple_of(qi * STEP, STEP), STEP)
+        cols = pl.ds(pl.multiple_of(qi * QSTEP, QSTEP), QSTEP)
         grid = jnp.dot(
             rows[...].reshape(count * nrad, nang), basis[:, cols], preferred_element_type=F32
         )
-        prod = grid.reshape(count, nrad, STEP) * pot[:, cols][None]
-        scaled[:, cols] = prod.astype(BF16).reshape(count * nrad, STEP)
-
-    factor = wider(radii[0], STEP)
-    damp = wider(radii[1], STEP)
-
-    @pl.loop(0, nang // STEP)
+        prod = grid.reshape(count, nrad, QSTEP) * pot[:, cols][None]
+        scaled[:, cols] = prod.astype(BF16).reshape(count * nrad, QSTEP)
+
+    factor = wider(radii[0], JSTEP)
+    damp = wider(radii[1], JSTEP)
+
+    @pl.loop(0, nang // JSTEP)
     def _(ji):
-        cols = pl.ds(pl.multiple_of(ji * STEP, STEP), STEP)
+        cols = pl.ds(pl.multiple_of(ji * JSTEP, JSTEP), JSTEP)
         ang = lax.dot_general(
             scaled[...], basis[cols, :], NT, preferred_element_type=F32
-        ).reshape(count, nrad, STEP)
+        ).reshape(count, nrad, JSTEP)
         for i in range(count):
             total = ang[i] + jnp.dot(
                 kin_ref[...], rows[i, :, cols], preferred_element_type=F32
             )
-            total += wider(khat[i + 1], STEP) * factor * part[i + 1, :, cols]
+            total += wider(khat[i + 1], JSTEP) * factor * part[i + 1, :, cols]
             if i + 1 < count:
                 total += chain[i + 1, :, cols] * rows[i + 1, :, cols].astype(F32)
             if i > 0:
@@ -307,28 +309,28 @@
         split, level, shift = False, rows, own
     count = shift + sides * (n - 1)
 
-    @pl.loop(0, nquad // STEP)
+    @pl.loop(0, nquad // QSTEP)
     def _(qi):
-        cols = pl.ds(pl.multiple_of(qi * STEP, STEP), STEP)
+        cols = pl.ds(pl.multiple_of(qi * QSTEP, QSTEP), QSTEP)
         grid = jnp.dot(
             rows[...].reshape(count * nrad, nang), basis[:, cols], preferred_element_type=F32
         )
-        prod = grid.reshape(count, nrad, STEP) * pot[:, cols][None]
-        scaled[:, cols] = prod.astype(BF16).reshape(count * nrad, STEP)
-
-    factor = wider(radii[0], STEP)
-    damp = wider(radii[1], STEP)
-
-    @pl.loop(0, nang // STEP)
+        prod = grid.reshape(count, nrad, QSTEP) * pot[:, cols][None]
+        scaled[:, cols] = prod.astype(BF16).reshape(count * nrad, QSTEP)
+
+    factor = wider(radii[0], JSTEP)
+    damp = wider(radii[1], JSTEP)
+
+    @pl.loop(0, nang // JSTEP)
     def _(ji):
-        cols = pl.ds(pl.multiple_of(ji * STEP, STEP), STEP)
+        cols = pl.ds(pl.multiple_of(ji * JSTEP, JSTEP), JSTEP)
         ang = lax.dot_general(
             scaled[...], basis[cols, :], NT, preferred_element_type=F32
-        ).reshape(count, nrad, STEP)
+        ).reshape(count, nrad, JSTEP)
 
         def local(i, hat, value):
             kin = jnp.dot(kin_ref[...], rows[i, :, cols], preferred_element_type=F32)
-            return ang[i] + kin + wider(hat, STEP) * factor * value
+            return ang[i] + kin + wider(hat, JSTEP) * factor * value
 
         for i in range(own):
             if split and i > 0:

time: 55.3 us -> 55.2 us (level)
  Pallas kernels: 17.7 us -> 15.4 us
  waiting for transfers between devices: 11.6 us -> 13.8 us
    ppermute x3, waiting for transfers between devices: 0.01 us -> 2.27 us  [per_device(): halos.append([lax.ppermute(part, 'g', swapped)])]
    pallas_call x3, Pallas kernels: 9.79 us -> 8.17 us  [run(): pl.pallas_call(functools.partial(advance, dims, sides, n), out_shape=outs...]
    pallas_call x1, Pallas kernels: 2.92 us -> 2.24 us  [per_device(): pl.pallas_call(functools.partial(inner, dims), out_shape=[shape((own - 1,...]
  transfers between devices with their start and end apart: 4 -> 4, of which waited for: 1 -> 3; matrix products, arithmetic and copies ran while one was open for 0% -> 0% of each run, Pallas kernels for 23% -> 19%
where the time goes in v10:
time: 55.2 us; the launch traced here: 54.9 us
  Pallas kernels  15.4 us (28%)
  waiting for transfers between devices  13.8 us (25%)
  starting transfers between devices  12.1 us (22%)
  blocking collectives  12.1 us (22%)
  between operations  1.4 us (3%)
    all_to_all x1, blocking collectives, per_device(): home = lax.all_to_all(back, ('hl', 'rad'), 0, 0, tiled=True)  12.1 us
    all_to_all x1, waiting for transfers between devices, per_device(): message = lax.all_to_all(send, ('hl', 'rad'), 0, 0, tiled=True)  11.6 us
    pallas_call x3, Pallas kernels, run(): pl.pallas_call(functools.partial(advance, dims, sides, n), out_shape=outs...  8.17 us
    all_to_all x1, starting transfers between devices, per_device(): message = lax.all_to_all(send, ('hl', 'rad'), 0, 0, tiled=True)  6.45 us
    ppermute x3, starting transfers between devices, per_device(): halos.append([lax.ppermute(part, 'g', swapped)])  5.65 us
    pallas_call x1, Pallas kernels, per_device(): pl.pallas_call(functools.partial(pack, (slab, nvib, nang, share, blocks))...  2.63 us
    ppermute x3, waiting for transfers between devices, per_device(): halos.append([lax.ppermute(part, 'g', swapped)])  2.27 us
    pallas_call x1, Pallas kernels, per_device(): pl.pallas_call(functools.partial(inner, dims), out_shape=[shape((own - 1,...  2.24 us
  transfers between devices with their start and end apart: 4, of which 3 were waited for; matrix products, arithmetic and copies ran while one was open for 0% of the time, Pallas kernels for 19%

profile of v10, /device:TPU:0, one launch (start us, length us, event | category | flops | bytes accessed | tf_op | source)
XLA Modules:
  0.0 54.9 jit_solution(2585338874838895364)
XLA Ops:
  1.3 2.6 %pack.1 = bf16[16,152,128]{2,1,0:T(8,128)(2,1)} custom-call(f32[256,768]{1,0:T(8,128)} %bitcast.12, f32[256,1536]{1,0:T(8,128)} %bitcast.11, bf16[1,768]{1,0:T(2,128)(2,1)} %coup_ref.1, s32[1,1]{1,0:T(1,128)} %bitcast.8.hel_ref, f32[1,16]{1,0:T(1,128)} %bitcast.13, f32[1,16]{1,0:T(1,128)} %bitcast.14), custom_call_target="tpu_custom_call" | custom-call | tf_op jit(solution)/shard_map/pack/pallas_call | solution.py:455
  3.9 0.0 copy-start
  3.9 0.0 copy-start.2
  3.9 6.5 %all-to-all-start = ((bf16[16,152,128]{2,1,0:T(8,128)(2,1)}), bf16[16,152,128]{2,1,0:T(8,128)(2,1)S(1)}, u32[]{:S(2)}, u32[]{:S(2)}) async-start(bf16[16,152,128]{2,1,0:T(8,128)(2,1)} %pack.1), calls=%async_computation | async-start | bytes 1245184 | tf_op jit(solution)/shard_map/all_to_all | solution.py:480
  10.4 11.6 %all-to-all-done.refs_0_.refs_9_ = bf16[16,152,128]{2,1,0:T(8,128)(2,1)S(1)} async-done(((bf16[16,152,128]{2,1,0:T(8,128)(2,1)}), bf16[16,152,128]{2,1,0:T(8,128)(2,1)S(1)}, u32[]{:S(2)}, u32[]{:S(2)}) %all-to-all-start) | async-done | bytes 622624 | tf_op jit(solution)/shard_map/all_to_all | solution.py:480
  22.0 2.7 %collective-permute-start.2 = (bf16[4,104,128]{2,1,0:T(8,128)(2,1)S(1)}, bf16[4,104,128]{2,1,0:T(8,128)(2,1)S(1)}, u32[]{:S(2)}, u32[]{:S(2)}) collective-permute-start(bf16[4,104,128]{2,1,0:T(8,128)(2,1)S(1)} %get-tuple-element.46), channel_id=1, source_target_pairs={{0,16},{16,0},{1,17},{17,1},{2,18},{18,2},{3,19},{19,3},{4,20},{20... | collective-permute-start | bytes 319496 | tf_op jit(solution)/shard_map/ppermute | solution.py:491
  24.7 0.3 collective-permute-start.1
  25.0 0.0 copy-done
  25.0 0.0 copy-done.2
  25.0 2.6 %advance1.1 = (f32[4,64,768]{2,1,0:T(8,128)S(1)}, bf16[4,64,768]{2,1,0:T(8,128)(2,1)S(1)}, f32[64,1536]{1,0:T(8,128)S(1)}, f32[2,64,128]{2,1,0:T(8,128)S(1)}, f3...) custom-call(bf16[16,152,128]{2,1,0:T(8,128)(2,1)S(1)} %all-to-all-done.refs_0_.refs_9_, ...), custom_call_target="tpu_custom_call" | custom-call | flops 1207959552 | bytes 8388608 | tf_op jit(solution)/shard_map/advance1/pallas_call | solution.py:514
  27.6 2.2 %inner.1 = (f32[3,64,768]{2,1,0:T(8,128)S(1)}, bf16[4,104,128]{2,1,0:T(8,128)(2,1)S(1)}) custom-call(bf16[768,1536]{1,0:T(8,128)(2,1)S(1)} %copy-done, bf16[64,64]{1,0:T(8,128)(2,1)S(1)} %copy-done.2, f32[64,1536]{1,0:T(8,128)S(1)} %get-tuple-element.24.refs_2_.refs_3_, f32[2,64,128]{2,1,0:T(8,128)S(1)} %get-tuple-element.25.refs_3_.refs_4_.refs_7_, ...), custom_call_target="tpu_custom_call" | custom-call | flops 1207959552 | bytes 8388608 | tf_op jit(solution)/shard_map/inner/pallas_call | solution.py:553
  29.9 2.7 %collective-permute-start = (bf16[4,104,128]{2,1,0:T(8,128)(2,1)S(1)}, bf16[4,104,128]{2,1,0:T(8,128)(2,1)S(1)}, u32[]{:S(2)}, u32[]{:S(2)}) collective-permute-start(bf16[4,104,128]{2,1,0:T(8,128)(2,1)S(1)} %get-tuple-element.31), channel_id=1, source_target_pairs={{0,16},{16,0},{1,17},{17,1},{2,18},{18,2},{3,19},{19,3},{4,20},{20... | collective-permute-start | bytes 319496 | tf_op jit(solution)/shard_map/ppermute | solution.py:574
  32.5 0.9 %collective-permute-done.2.refs_0_ = bf16[4,104,128]{2,1,0:T(8,128)(2,1)S(1)} collective-permute-done((bf16[4,104,128]{2,1,0:T(8,128)(2,1)S(1)}, bf16[4,104,128]{2,1,0:T(8,128)(2,1)S(1)}, u32[]{:S(2)}, u32[]{:S(2)}) %collective-permute-start.2) | collective-permute-done | bytes 106528 | tf_op jit(solution)/shard_map/ppermute | solution.py:491
  33.4 2.0 %advance2.1 = (f32[4,64,768]{2,1,0:T(8,128)S(1)}, bf16[4,64,768]{2,1,0:T(8,128)(2,1)S(1)}, f32[4,64,768]{2,1,0:T(8,128)S(1)}, f32[1,64,768]{2,1,0:T(8,128)S(1)},...) custom-call(bf16[4,104,128]{2,1,0:T(8,128)(2,1)S(1)} %collective-permute-done.2.refs_0_, ...), custom_call_target="tpu_custom_call" | custom-call | flops 603979776 | bytes 8388608 | tf_op jit(solution)/shard_map/advance2/pallas_call | solution.py:514
  35.5 1.4 %collective-permute-done.1.refs_0_ = bf16[4,104,128]{2,1,0:T(8,128)(2,1)S(1)} collective-permute-done((bf16[4,104,128]{2,1,0:T(8,128)(2,1)S(1)}, bf16[4,104,128]{2,1,0:T(8,128)(2,1)S(1)}, u32[]{:S(2)}, u32[]{:S(2)}) %collective-permute-start.1) | collective-permute-done | bytes 106528 | tf_op jit(solution)/shard_map/ppermute | solution.py:491
  36.8 0.0 copy-start.1
  36.8 0.0 copy-start.3
  36.8 0.0 copy-start.4
  36.8 3.6 %advance3.1 = (f32[4,64,768]{2,1,0:T(8,128)S(1)}, f32[1,64,768]{2,1,0:T(8,128)S(1)}, f32[1,64,768]{2,1,0:T(8,128)S(1)}, f32[1,1,768]{2,1,0:T(1,128)S(1)}) custom-call(bf16[4,104,128]{2,1,0:T(8,128)(2,1)S(1)} %collective-permute-done.1.refs_0_, bf16[768,1536]{1,0:T(8,128)(2,1)S(1)} %copy-done, bf16[64,64]{1,0:T(8,128)(2,1)S(1)} %copy-done.2, ...), custom_call_target="tpu_custom_call" | custom-call | flops 1811939328 | bytes 8388608 | tf_op jit(solution)/shard_map/advance3/pallas_call | solution.py:514
  40.4 0.0 collective-permute-done.refs_0_
  40.4 0.0 copy-done.1
  40.4 0.0 copy-done.3
  40.4 0.0 copy-done.4
  40.5 0.7 %close.1 = bf16[16,104,128]{2,1,0:T(8,128)(2,1)S(1)} custom-call(bf16[4,104,128]{2,1,0:T(8,128)(2,1)S(1)} %collective-permute-done.refs_0_, f32[4,64,768]{2,1,0:T(8,128)S(1)} %get-tuple-element.40.refs_1_, f32[1,64,768]{2,1,0:T(8,128)S(1)} %get-tuple-element.41.refs_2_, f32[1,64,768]{2,1,0:T(8,128)S(1)} %get-tuple-element.42.refs_3_, ...), custom_call_target="tpu_custom_call" | custom-call | tf_op jit(solution)/shard_map/close/pallas_call | solution.py:601
  41.2 12.1 %all_to_all.10.msg_ref = bf16[16,104,128]{2,1,0:T(8,128)(2,1)S(1)} all-to-all(bf16[16,104,128]{2,1,0:T(8,128)(2,1)S(1)} %close.1), channel_id=1, replica_groups=mesh['g'=2,'hl'=4,'rad'=4] {'hl','rad'}, dimensions={0} | all-to-all | bytes 851968 | tf_op jit(solution)/shard_map/all_to_all | solution.py:611
  53.3 1.7 %unpack.1 = (f32[256,768]{1,0:T(8,128)}, f32[1,256]{1,0:T(1,128)}) custom-call(bf16[16,104,128]{2,1,0:T(8,128)(2,1)S(1)} %all_to_all.10.msg_ref), custom_call_target="tpu_custom_call" | custom-call | tf_op jit(solution)/shard_map/unpack/pallas_call | solution.py:613
  (2 shorter events, 0.1 us)
Async XLA Ops:
  3.9 21.1 %copy-start = (bf16[768,1536]{1,0:T(8,128)(2,1)S(1)}, bf16[768,1536]{1,0:T(8,128)(2,1)}, u32[]{:S(2)}) copy-start(bf16[768,1536]{1,0:T(8,128)(2,1)} %refs_1_.7) | copy-start | bytes 7077892
  3.9 21.1 %copy-start.2 = (bf16[64,64]{1,0:T(8,128)(2,1)S(1)}, bf16[64,64]{1,0:T(8,128)(2,1)}, u32[]{:S(2)}) copy-start(bf16[64,64]{1,0:T(8,128)(2,1)} %refs_2_.5) | copy-start | bytes 24580
  3.9 18.0 %all-to-all-start = ((bf16[16,152,128]{2,1,0:T(8,128)(2,1)}), bf16[16,152,128]{2,1,0:T(8,128)(2,1)S(1)}, u32[]{:S(2)}, u32[]{:S(2)}) async-start(bf16[16,152,128]{2,1,0:T(8,128)(2,1)} %pack.1), calls=%async_computation | async-start | bytes 1245184 | tf_op jit(solution)/shard_map/all_to_all | solution.py:480
  22.0 11.4 %collective-permute-start.2 = (bf16[4,104,128]{2,1,0:T(8,128)(2,1)S(1)}, bf16[4,104,128]{2,1,0:T(8,128)(2,1)S(1)}, u32[]{:S(2)}, u32[]{:S(2)}) collective-permute-start(bf16[4,104,128]{2,1,0:T(8,128)(2,1)S(1)} %get-tuple-element.46), channel_id=1, source_target_pairs={{0,16},{16,0},{1,17},{17,1},{2,18},{18,2},{3,19},{19,3},{4,20},{20... | collective-permute-start | bytes 319496 | tf_op jit(solution)/shard_map/ppermute | solution.py:491
  24.7 12.1 %collective-permute-start.1 = (bf16[4,104,128]{2,1,0:T(8,128)(2,1)S(1)}, bf16[4,104,128]{2,1,0:T(8,128)(2,1)S(1)}, u32[]{:S(2)}, u32[]{:S(2)}) collective-permute-start(bf16[4,104,128]{2,1,0:T(8,128)(2,1)S(1)} %get-tuple-element.47), channel_id=1, source_target_pairs={{0,16},{16,0},{1,17},{17,1},{2,18},{18,2},{3,19},{19,3},{4,20},{20... | collective-permute-start | bytes 319496 | tf_op jit(solution)/shard_map/ppermute | solution.py:491
  29.9 10.6 %collective-permute-start = (bf16[4,104,128]{2,1,0:T(8,128)(2,1)S(1)}, bf16[4,104,128]{2,1,0:T(8,128)(2,1)S(1)}, u32[]{:S(2)}, u32[]{:S(2)}) collective-permute-start(bf16[4,104,128]{2,1,0:T(8,128)(2,1)S(1)} %get-tuple-element.31), channel_id=1, source_target_pairs={{0,16},{16,0},{1,17},{17,1},{2,18},{18,2},{3,19},{19,3},{4,20},{20... | collective-permute-start | bytes 319496 | tf_op jit(solution)/shard_map/ppermute | solution.py:574
  36.8 3.6 %copy-start.1 = (bf16[1024,768]{1,0:T(8,128)(2,1)S(1)}, bf16[1024,768]{1,0:T(8,128)(2,1)}, u32[]{:S(2)}) copy-start(bf16[1024,768]{1,0:T(8,128)(2,1)} %refs_10_.1) | copy-start | bytes 4718596
  36.8 3.6 %copy-start.3 = (s32[1024]{0:T(1024)S(1)}, s32[1024]{0:T(1024)}, u32[]{:S(2)}) copy-start(s32[1024]{0:T(1024)} %param.19) | copy-start | bytes 12292
  36.8 3.6 %copy-start.4 = (s32[1024]{0:T(1024)S(1)}, s32[1024]{0:T(1024)}, u32[]{:S(2)}) copy-start(s32[1024]{0:T(1024)} %param.20) | copy-start | bytes 12292

commit v11 on v10

--- a/solution.py
+++ b/solution.py
@@ -255,6 +255,11 @@
     if n == 1:
         msg_ref, basis, kin_ref = take(3)
         new_ref, src, pot, radii, khat, coup, chain = take(7)
+        if mirror:
+            send_ref = take(1)[0]
+            first = place(mirror, own, 1) * nslab
+            for m in range(nslab):
+                send_ref[m] = msg_ref[first + m, nquad // own // LANES * slab :, :]
         rows, scaled = take(2)
         unfold(dims, msg_ref, src, pot, radii, khat, coup)
         rows[...] = src[...]
@@ -484,7 +489,7 @@
     rows = message[:, share // LANES * slab :]
     halos = []
     swapped = [(0, 1), (1, 0)]
-    for j in range(ITERS - 1 if mirror else ITERS):
+    for j in range(1 if mirror else ITERS):
         if mirror:
             first = jnp.where(group == 0, own - 1 - j, j) * nslab
             part = lax.dynamic_slice_in_dim(rows, first, nslab, 0)
@@ -531,7 +536,7 @@
             name=f"advance{n}",
         )(*operands)
 
-    new, first_b, pot, radii, khat, coup, chain = run(
+    new, first_b, pot, radii, khat, coup, chain, *sent = run(
         1,
         [message, basis, kinetic],
         [VMEM] * 3,
@@ -543,9 +548,12 @@
             shape((own, 1, LANES), F32),
             shape((own, 1, nang), F32),
             shape((max(own - 1, 1), 1, nang), F32),
-        ],
+        ]
+        + [shape((nslab, height - share // LANES * slab, LANES), BF16)] * mirror,
         [],
     )
+    if mirror:
+        halos.append([lax.ppermute(sent[0], "g", swapped)])
     common = [basis, kinetic, pot, radii, khat, coup, chain]
     joint = pltpu.VMEM((sides, 2, 1, nang), F32)
     operands = halos[0] + common + [new, first_b]

time: 55.2 us -> 55.9 us (1.013)
  waiting for transfers between devices: 13.8 us -> 14.5 us
    ppermute x0 -> x1, waiting for transfers between devices: none -> 2.89 us  [per_device(): halos.append([lax.ppermute(sent[0], 'g', swapped)])]
    ppermute x3 -> x2, waiting for transfers between devices: 2.27 us -> 0.01 us  [per_device(): halos.append([lax.ppermute(part, 'g', swapped)])]
    ppermute x3 -> x2, starting transfers between devices: 5.65 us -> 5.3 us  [per_device(): halos.append([lax.ppermute(part, 'g', swapped)])]
  transfers between devices with their start and end apart: 4 -> 4, of which waited for: 3 -> 2; matrix products, arithmetic and copies ran while one was open for 0% -> 0% of each run, Pallas kernels for 19% -> 19%
where the time goes in v11:
time: 55.9 us; the launch traced here: 55.6 us
  Pallas kernels  15.6 us (28%)
  waiting for transfers between devices  14.5 us (26%)
  blocking collectives  12.1 us (22%)
  starting transfers between devices  12 us (21%)
  between operations  1.41 us (3%)
    all_to_all x1, blocking collectives, per_device(): home = lax.all_to_all(back, ('hl', 'rad'), 0, 0, tiled=True)  12.1 us
    all_to_all x1, waiting for transfers between devices, per_device(): message = lax.all_to_all(send, ('hl', 'rad'), 0, 0, tiled=True)  11.6 us
    pallas_call x3, Pallas kernels, run(): pl.pallas_call(functools.partial(advance, dims, sides, n), out_shape=outs...  8.2 us
    all_to_all x1, starting transfers between devices, per_device(): message = lax.all_to_all(send, ('hl', 'rad'), 0, 0, tiled=True)  6.33 us
    ppermute x2, starting transfers between devices, per_device(): halos.append([lax.ppermute(part, 'g', swapped)])  5.3 us
    ppermute x1, waiting for transfers between devices, per_device(): halos.append([lax.ppermute(sent[0], 'g', swapped)])  2.89 us
    pallas_call x1, Pallas kernels, per_device(): pl.pallas_call(functools.partial(pack, (slab, nvib, nang, share, blocks))...  2.78 us
    pallas_call x1, Pallas kernels, per_device(): pl.pallas_call(functools.partial(inner, dims), out_shape=[shape((own - 1,...  2.24 us
  transfers between devices with their start and end apart: 4, of which 2 were waited for; matrix products, arithmetic and copies ran while one was open for 0% of the time, Pallas kernels for 19%

profile of v11, /device:TPU:0, one launch (start us, length us, event | category | flops | bytes accessed | tf_op | source)
XLA Modules:
  0.0 55.6 jit_solution(5774698310502060839)
XLA Ops:
  1.3 0.0 copy-start
  1.3 2.8 %pack.1 = bf16[16,152,128]{2,1,0:T(8,128)(2,1)} custom-call(f32[256,768]{1,0:T(8,128)} %bitcast.12, f32[256,1536]{1,0:T(8,128)} %bitcast.11, bf16[1,768]{1,0:T(2,128)(2,1)} %coup_ref.1, s32[1,1]{1,0:T(1,128)} %bitcast.8.hel_ref, f32[1,16]{1,0:T(1,128)} %bitcast.13, f32[1,16]{1,0:T(1,128)} %bitcast.14), custom_call_target="tpu_custom_call" | custom-call | tf_op jit(solution)/shard_map/pack/pallas_call | solution.py:460
  4.1 0.0 copy-start.2
  4.1 6.3 %all-to-all-start = ((bf16[16,152,128]{2,1,0:T(8,128)(2,1)}), bf16[16,152,128]{2,1,0:T(8,128)(2,1)S(1)}, u32[]{:S(2)}, u32[]{:S(2)}) async-start(bf16[16,152,128]{2,1,0:T(8,128)(2,1)} %pack.1), calls=%async_computation | async-start | bytes 1245184 | tf_op jit(solution)/shard_map/all_to_all | solution.py:485
  10.4 11.6 %all-to-all-done.refs_0_.refs_9_ = bf16[16,152,128]{2,1,0:T(8,128)(2,1)S(1)} async-done(((bf16[16,152,128]{2,1,0:T(8,128)(2,1)}), bf16[16,152,128]{2,1,0:T(8,128)(2,1)S(1)}, u32[]{:S(2)}, u32[]{:S(2)}) %all-to-all-start) | async-done | bytes 622624 | tf_op jit(solution)/shard_map/all_to_all | solution.py:485
  22.1 2.7 %collective-permute-start.2 = (bf16[4,104,128]{2,1,0:T(8,128)(2,1)S(1)}, bf16[4,104,128]{2,1,0:T(8,128)(2,1)S(1)}, u32[]{:S(2)}, u32[]{:S(2)}) collective-permute-start(bf16[4,104,128]{2,1,0:T(8,128)(2,1)S(1)} %constant_dynamic-slice_fusion), channel_id=1, source_target_pairs={{0,16},{16,0},{1,17},{17,1},{2,18},{18,2},{3,19},{19,3},{4,20},{20... | collective-permute-start | bytes 319496 | tf_op jit(solution)/shard_map/ppermute | solution.py:496
  24.7 0.0 copy-done
  24.7 0.0 copy-done.2
  24.7 2.6 %advance1.1 = (f32[4,64,768]{2,1,0:T(8,128)S(1)}, bf16[4,64,768]{2,1,0:T(8,128)(2,1)S(1)}, f32[64,1536]{1,0:T(8,128)S(1)}, f32[2,64,128]{2,1,0:T(8,128)S(1)}, f3...) custom-call(bf16[16,152,128]{2,1,0:T(8,128)(2,1)S(1)} %all-to-all-do, ...), custom_call_target="tpu_custom_call" | custom-call | flops 1207959552 | bytes 8388608 | tf_op jit(solution)/shard_map/advance1/pallas_call | solution.py:519
  27.3 0.4 collective-permute-start.1
  27.7 2.2 %inner.1 = (f32[3,64,768]{2,1,0:T(8,128)S(1)}, bf16[4,104,128]{2,1,0:T(8,128)(2,1)S(1)}) custom-call(bf16[768,1536]{1,0:T(8,128)(2,1)S(1)} %copy-done, bf16[64,64]{1,0:T(8,128)(2,1)S(1)} %copy-done.2, f32[64,1536]{1,0:T(8,128)S(1)} %get-tuple-element.25.refs_2_.refs_3_, f32[2,64,128]{2,1,0:T(8,128)S(1)} %get-tuple-element.26.refs_3_.refs_4_.refs_7_, ...), custom_call_target="tpu_custom_call" | custom-call | flops 1207959552 | bytes 8388608 | tf_op jit(solution)/shard_map/inner/pallas_call | solution.py:561
  30.0 2.6 %collective-permute-start = (bf16[4,104,128]{2,1,0:T(8,128)(2,1)S(1)}, bf16[4,104,128]{2,1,0:T(8,128)(2,1)S(1)}, u32[]{:S(2)}, u32[]{:S(2)}) collective-permute-start(bf16[4,104,128]{2,1,0:T(8,128)(2,1)S(1)} %get-tuple-element.32), channel_id=1, source_target_pairs={{0,16},{16,0},{1,17},{17,1},{2,18},{18,2},{3,19},{19,3},{4,20},{20... | collective-permute-start | bytes 319496 | tf_op jit(solution)/shard_map/ppermute | solution.py:582
  32.6 0.0 collective-permute-done.2.refs_0_
  32.6 2.0 %advance2.1 = (f32[4,64,768]{2,1,0:T(8,128)S(1)}, bf16[4,64,768]{2,1,0:T(8,128)(2,1)S(1)}, f32[4,64,768]{2,1,0:T(8,128)S(1)}, f32[1,64,768]{2,1,0:T(8,128)S(1)},...) custom-call(bf16[4,104,128]{2,1,0:T(8,128)(2,1)S(1)} %collective-permute-done.2.refs_0_, ...), custom_call_target="tpu_custom_call" | custom-call | flops 603979776 | bytes 8388608 | tf_op jit(solution)/shard_map/advance2/pallas_call | solution.py:519
  34.6 2.9 %collective-permute-done.1.refs_0_ = bf16[4,104,128]{2,1,0:T(8,128)(2,1)S(1)} collective-permute-done((bf16[4,104,128]{2,1,0:T(8,128)(2,1)S(1)}, bf16[4,104,128]{2,1,0:T(8,128)(2,1)S(1)}, u32[]{:S(2)}, u32[]{:S(2)}) %collective-permute-start.1) | collective-permute-done | bytes 106528 | tf_op jit(solution)/shard_map/ppermute | solution.py:556
  37.5 0.0 copy-start.1
  37.5 0.0 copy-start.3
  37.5 0.0 copy-start.4
  37.5 3.6 %advance3.1 = (f32[4,64,768]{2,1,0:T(8,128)S(1)}, f32[1,64,768]{2,1,0:T(8,128)S(1)}, f32[1,64,768]{2,1,0:T(8,128)S(1)}, f32[1,1,768]{2,1,0:T(1,128)S(1)}) custom-call(bf16[4,104,128]{2,1,0:T(8,128)(2,1)S(1)} %collective-permute-done.1.refs_0_, bf16[768,1536]{1,0:T(8,128)(2,1)S(1)} %copy-done, bf16[64,64]{1,0:T(8,128)(2,1)S(1)} %copy-done.2, ...), custom_call_target="tpu_custom_call" | custom-call | flops 1811939328 | bytes 8388608 | tf_op jit(solution)/shard_map/advance3/pallas_call | solution.py:519
  41.1 0.0 collective-permute-done.refs_0_
  41.1 0.0 copy-done.1
  41.2 0.0 copy-done.3
  41.2 0.0 copy-done.4
  41.2 0.7 %close.1 = bf16[16,104,128]{2,1,0:T(8,128)(2,1)S(1)} custom-call(bf16[4,104,128]{2,1,0:T(8,128)(2,1)S(1)} %collective-permute-done.refs_0_, f32[4,64,768]{2,1,0:T(8,128)S(1)} %get-tuple-element.42.refs_1_, f32[1,64,768]{2,1,0:T(8,128)S(1)} %get-tuple-element.43.refs_2_, f32[1,64,768]{2,1,0:T(8,128)S(1)} %get-tuple-element.44.refs_3_, ...), custom_call_target="tpu_custom_call" | custom-call | tf_op jit(solution)/shard_map/close/pallas_call | solution.py:609
  41.9 12.1 %all_to_all.10.msg_ref = bf16[16,104,128]{2,1,0:T(8,128)(2,1)S(1)} all-to-all(bf16[16,104,128]{2,1,0:T(8,128)(2,1)S(1)} %close.1), channel_id=1, replica_groups=mesh['g'=2,'hl'=4,'rad'=4] {'hl','rad'}, dimensions={0} | all-to-all | bytes 851968 | tf_op jit(solution)/shard_map/all_to_all | solution.py:619
  54.0 1.7 %unpack.1 = (f32[256,768]{1,0:T(8,128)}, f32[1,256]{1,0:T(1,128)}) custom-call(bf16[16,104,128]{2,1,0:T(8,128)(2,1)S(1)} %all_to_all.10.msg_ref), custom_call_target="tpu_custom_call" | custom-call | tf_op jit(solution)/shard_map/unpack/pallas_call | solution.py:621
  (2 shorter events, 0.1 us)
Async XLA Ops:
  1.3 23.4 %copy-start = (bf16[768,1536]{1,0:T(8,128)(2,1)S(1)}, bf16[768,1536]{1,0:T(8,128)(2,1)}, u32[]{:S(2)}) copy-start(bf16[768,1536]{1,0:T(8,128)(2,1)} %refs_1_.7) | copy-start | bytes 7077892
  4.1 20.6 %copy-start.2 = (bf16[64,64]{1,0:T(8,128)(2,1)S(1)}, bf16[64,64]{1,0:T(8,128)(2,1)}, u32[]{:S(2)}) copy-start(bf16[64,64]{1,0:T(8,128)(2,1)} %refs_2_.5) | copy-start | bytes 24580
  4.1 17.9 %all-to-all-start = ((bf16[16,152,128]{2,1,0:T(8,128)(2,1)}), bf16[16,152,128]{2,1,0:T(8,128)(2,1)S(1)}, u32[]{:S(2)}, u32[]{:S(2)}) async-start(bf16[16,152,128]{2,1,0:T(8,128)(2,1)} %pack.1), calls=%async_computation | async-start | bytes 1245184 | tf_op jit(solution)/shard_map/all_to_all | solution.py:485
  22.1 10.5 %collective-permute-start.2 = (bf16[4,104,128]{2,1,0:T(8,128)(2,1)S(1)}, bf16[4,104,128]{2,1,0:T(8,128)(2,1)S(1)}, u32[]{:S(2)}, u32[]{:S(2)}) collective-permute-start(bf16[4,104,128]{2,1,0:T(8,128)(2,1)S(1)} %constant_dynamic-slice_fusion), channel_id=1, source_target_pairs={{0,16},{16,0},{1,17},{17,1},{2,18},{18,2},{3,19},{19,3},{4,20},{20... | collective-permute-start | bytes 319496 | tf_op jit(solution)/shard_map/ppermute | solution.py:496
  27.3 10.2 %collective-permute-start.1 = (bf16[4,104,128]{2,1,0:T(8,128)(2,1)S(1)}, bf16[4,104,128]{2,1,0:T(8,128)(2,1)S(1)}, u32[]{:S(2)}, u32[]{:S(2)}) collective-permute-start(bf16[4,104,128]{2,1,0:T(8,128)(2,1)S(1)} %get-tuple-element.33), channel_id=1, source_target_pairs={{0,16},{16,0},{1,17},{17,1},{2,18},{18,2},{3,19},{19,3},{4,20},{20... | collective-permute-start | bytes 319496 | tf_op jit(solution)/shard_map/ppermute | solution.py:556
  30.0 11.2 %collective-permute-start = (bf16[4,104,128]{2,1,0:T(8,128)(2,1)S(1)}, bf16[4,104,128]{2,1,0:T(8,128)(2,1)S(1)}, u32[]{:S(2)}, u32[]{:S(2)}) collective-permute-start(bf16[4,104,128]{2,1,0:T(8,128)(2,1)S(1)} %get-tuple-element.32), channel_id=1, source_target_pairs={{0,16},{16,0},{1,17},{17,1},{2,18},{18,2},{3,19},{19,3},{4,20},{20... | collective-permute-start | bytes 319496 | tf_op jit(solution)/shard_map/ppermute | solution.py:582
  37.5 3.6 %copy-start.1 = (bf16[1024,768]{1,0:T(8,128)(2,1)S(1)}, bf16[1024,768]{1,0:T(8,128)(2,1)}, u32[]{:S(2)}) copy-start(bf16[1024,768]{1,0:T(8,128)(2,1)} %refs_10_.1) | copy-start | bytes 4718596
  37.5 3.6 %copy-start.3 = (s32[1024]{0:T(1024)S(1)}, s32[1024]{0:T(1024)}, u32[]{:S(2)}) copy-start(s32[1024]{0:T(1024)} %param.19) | copy-start | bytes 12292
  37.5 3.6 %copy-start.4 = (s32[1024]{0:T(1024)S(1)}, s32[1024]{0:T(1024)}, u32[]{:S(2)}) copy-start(s32[1024]{0:T(1024)} %param.20) | copy-start | bytes 12292
